TPU v7x, 32 devices: a whole 2x2x4 slice. The times are simulated.
32 devices in a mesh: rep: 8 (over z, x), tp: 4 (over y, core).
Axes of the slice: x: 2, y: 2, z: 4, core: 2. Of those that a mesh axis runs over, the one named last changes fastest.
Arguments:
- prompt_queries: bfloat16 [3968, 4096], P('rep', 'tp'), parts along dimension 0, may hold values from -240 to 240
- prompt_entries: bfloat16 [16, 496, 512], P('rep', 'tp'), parts along dimension 0, may hold values from -6 to 6
- history_cache: bfloat16 [16, 1024, 512], P('rep', 'tp'), parts along dimension 0, may hold values from -6 to 6
- decode_queries: bfloat16 [128, 4096], P('rep', 'tp'), parts along dimension 0, may hold values from -240 to 240
- decode_entries: bfloat16 [16, 16, 512], P('rep'), parts along dimension 0, may hold values from -6 to 6
- decode_cache: bfloat16 [16, 16, 768, 512], P('rep', None, 'tp'), parts along dimension 0, may hold values from -6 to 6
- decode_lengths: int32 [128], P('rep'), parts along dimension 0, may hold values from 1 to 768
- prompt_start: int32 [8], P('rep'), parts along dimension 0, may hold values from 512 to 1024
- out_weight: bfloat16 [4096, 4096], P('tp'), may hold values from -0.09375 to 0.09375
- residual: bfloat16 [512, 32768], P('tp', 'rep'), parts along dimension 1, may hold values from -4 to 4
- norm_gain: float32 [4096], replicated, may hold values from 0.5 to 1.5
Outputs:
- new_residual: bfloat16 [512, 32768], P('tp', 'rep'), parts along dimension 1
- normed: bfloat16 [512, 32768], P('tp', 'rep'), parts along dimension 1
There are 8 independent parts, one for each index of `rep`. A program takes and returns all parts, laid end to end along the dimension named above; an argument that names none is the same for every part. Nothing has to cross between parts.
Inputs may be any that keep to these rules, and one draw needn't show every extreme that they name: The rows of history_cache at and past prompt_start are not read. `decode_lengths`: rows of decode_cache at and past a request's length are not read.
All inputs are finite; a program needn't handle non-finite values.
Results may differ from a plain program's by a relative error of at most 0.017.
Values may be sent and summed in bfloat16 or wider, within the bound.
No kernel may reach another device: no remote copies, remote signals or barrier semaphores. Data moves between devices by JAX's collectives and lax.ppermute only.
A program may use at most 64 MiB of HBM per device.

v0:
```python
import jax
import jax.numpy as jnp
import numpy as np
from jax import lax
from jax.experimental import pallas as pl
from jax.experimental.pallas import tpu as pltpu
from jax.sharding import PartitionSpec as P


HEAD_DIM = 128
MASKED = -1e30
EPS = 1e-05
CHUNKS = (64, 64)
COLUMNS = 512

F32 = jnp.float32
BF16 = jnp.bfloat16


def round_up(value, unit):
    return -(-value // unit) * unit


def smem():
    return pl.BlockSpec(memory_space=pltpu.SMEM)


def hbm():
    return pl.BlockSpec(memory_space=pl.ANY)


def in_hbm():
    return pl.BlockSpec(memory_space=pltpu.HBM)


def in_vmem():
    return pl.BlockSpec(memory_space=pltpu.VMEM)


def to_hbm(value):
    return pltpu.with_memory_space_constraint(value, pltpu.HBM)


def params(mib, **kwargs):
    return pltpu.CompilerParams(vmem_limit_bytes=mib << 20, **kwargs)


def pack_history(history, queries, meta, devices, local_heads, group):
    h_rows = history.shape[1]
    rows = queries.shape[0]
    span = 2 * h_rows + rows * local_heads

    def head_of(k):
        return lambda i, m: (0, 0, (m[0] ^ k) * local_heads // group)

    def body(m, *refs):
        q_ref = refs[devices]
        for k in range(devices):
            h_ref, o_ref = refs[k], refs[devices + 1 + k]
            for part in range(2):
                o_ref[part * h_rows : (part + 1) * h_rows, :] = h_ref[part]
            for h in range(local_heads):
                row = 2 * h_rows + h * rows
                o_ref[row : row + rows, :] = q_ref[:, h * HEAD_DIM : (h + 1) * HEAD_DIM]

    return pl.pallas_call(
        body,
        grid_spec=pltpu.PrefetchScalarGridSpec(
            num_scalar_prefetch=1,
            grid=(1,),
            in_specs=[pl.BlockSpec((2, h_rows, HEAD_DIM), head_of(k)) for k in range(devices)]
            + [pl.BlockSpec(queries.shape, lambda i, m: (0, 0))],
            out_specs=[pl.BlockSpec((span, HEAD_DIM), lambda i, m: (0, 0))] * devices,
        ),
        out_shape=[jax.ShapeDtypeStruct((span, HEAD_DIM), BF16)] * devices,
        compiler_params=params(8),
        name="pack_history",
    )(meta, *([to_hbm(history)] * devices), to_hbm(queries))


def stage(prompt, cache, prompt_queries, decode_queries, meta, devices, local_heads, group):
    p_rows = prompt.shape[1]
    p_pad = round_up(p_rows, 16)
    prompt_rows, decode_rows = prompt_queries.shape[0], decode_queries.shape[0]
    parts = 4
    per = cache.shape[1] // parts

    def head_of(k):
        return lambda i, m: (0, 0, (m[0] ^ k) * local_heads // group)

    def body(m, *refs):
        cache_hbm, q_hbm, dq_hbm = refs[devices : devices + 3]
        o_refs = refs[devices + 3 : 2 * devices + 3]
        cache_ref, q_ref, sem = refs[2 * devices + 3 :]
        copies = [
            pltpu.make_async_copy(q_hbm, q_ref.at[0:prompt_rows, :], sem.at[0]),
            pltpu.make_async_copy(dq_hbm, q_ref.at[prompt_rows : prompt_rows + decode_rows, :], sem.at[1]),
        ]
        for i in range(2 * parts):
            here = (i // parts, slice(i % parts * per, (i % parts + 1) * per))
            copies.append(pltpu.make_async_copy(cache_hbm.at[here], cache_ref.at[here], sem.at[2 + i]))
        for copy in copies:
            copy.start()
        for k in range(devices):
            p_ref, o_ref = refs[k], o_refs[k]
            for part in range(2):
                if p_pad > p_rows:
                    fresh = jnp.concatenate(
                        [p_ref[part].astype(F32), jnp.zeros((p_pad - p_rows, HEAD_DIM), F32)], axis=0
                    ).astype(BF16)
                else:
                    fresh = p_ref[part]
                o_ref[part * p_pad : (part + 1) * p_pad, :] = fresh
        for copy in copies:
            copy.wait()

    outs = pl.pallas_call(
        body,
        grid_spec=pltpu.PrefetchScalarGridSpec(
            num_scalar_prefetch=1,
            grid=(1,),
            in_specs=[pl.BlockSpec((2, p_rows, HEAD_DIM), head_of(k)) for k in range(devices)] + [in_hbm()] * 3,
            out_specs=[pl.BlockSpec((2 * p_pad, HEAD_DIM), lambda i, m: (0, 0))] * devices + [hbm(), hbm()],
            scratch_shapes=[pltpu.SemaphoreType.DMA((2 + 2 * parts,))],
        ),
        out_shape=[jax.ShapeDtypeStruct((2 * p_pad, HEAD_DIM), BF16)] * devices
        + [
            pltpu.VMEM(cache.shape, BF16),
            pltpu.VMEM((prompt_rows + decode_rows, prompt_queries.shape[1]), BF16),
        ],
        compiler_params=params(8),
        name="stage",
    )(meta, *([prompt] * devices), to_hbm(cache), to_hbm(prompt_queries), to_hbm(decode_queries))
    return outs[:devices], outs[devices], outs[devices + 1]


def decode_partials(history, cache, meta, h_rows, local_heads, group):
    devices = len(history)
    rows, span, width = cache.shape[1], cache.shape[2], cache.shape[3]
    kv_heads = width // HEAD_DIM
    heads = devices * local_heads
    factor = HEAD_DIM ** (-0.5) * float(np.log2(np.e))
    part_rows = rows * local_heads
    stat_rows = round_up(local_heads, 8)

    def body(m, *refs):
        h_refs, cache_ref = refs[:devices], refs[devices]
        o_refs = refs[devices + 1 : 2 * devices + 1]
        q_all = refs[2 * devices + 1]
        me = m[0]
        for k in range(devices):
            for h in range(local_heads):
                row = 2 * h_rows + h * rows
                q_all[k, pl.ds(h, rows, stride=local_heads), :] = h_refs[k][row : row + rows, :].astype(F32)

        slot = lax.broadcasted_iota(jnp.int32, (heads, 1), 0) // local_heads
        reads = ((slot ^ me) * local_heads) // group
        lane = lax.broadcasted_iota(jnp.int32, (heads, HEAD_DIM), 1)
        place = me * span + lax.broadcasted_iota(jnp.int32, (1, span), 1)
        scores = []
        for b in range(rows):
            here = slice(b * local_heads, (b + 1) * local_heads)
            q = jnp.concatenate([q_all[k, here, :] for k in range(devices)], axis=0)
            spread = jnp.concatenate(
                [jnp.where(reads == g, q, 0.0) for g in range(kv_heads)], axis=1
            ).astype(BF16)
            score = lax.dot_general(
                spread, cache_ref[0, b], (((1,), (1,)), ((), ())), preferred_element_type=F32
            )
            scores.append(jnp.where(place < m[2 + b], score, MASKED))
        scores = jnp.concatenate(scores, axis=0)
        top = jnp.max(scores, axis=-1, keepdims=True)
        weights = jnp.where(scores > 0.5 * MASKED, jnp.exp2((scores - top) * factor), 0.0)
        total = jnp.sum(weights, axis=-1, keepdims=True)
        weights = weights.astype(BF16)
        stats = jnp.zeros((heads, HEAD_DIM), F32)
        for b in range(rows):
            these = slice(b * heads, (b + 1) * heads)
            summed = jnp.dot(weights[these], cache_ref[1, b], preferred_element_type=F32)
            own = jnp.zeros((heads, HEAD_DIM), F32)
            for g in range(kv_heads):
                own = own + jnp.where(reads == g, summed[:, g * HEAD_DIM : (g + 1) * HEAD_DIM], 0.0)
            for k in range(devices):
                o_refs[k][b * local_heads : (b + 1) * local_heads, :] = own[k * local_heads : (k + 1) * local_heads]
            stats = jnp.where(lane == b, top[these], jnp.where(lane == rows + b, total[these], stats))
        for k in range(devices):
            o_refs[k][part_rows : part_rows + local_heads, :] = stats[k * local_heads : (k + 1) * local_heads, :]

    return pl.pallas_call(
        body,
        in_specs=[smem()] + [in_vmem()] * (devices + 1),
        out_specs=[in_vmem()] * devices,
        scratch_shapes=[pltpu.VMEM((devices, part_rows, HEAD_DIM), F32)],
        out_shape=[jax.ShapeDtypeStruct((part_rows + stat_rows, HEAD_DIM), F32)] * devices,
        compiler_params=params(16),
        name="decode",
    )(meta, *history, cache)


def decode_join(parts, history, entries, meta, h_rows, local_heads, group):
    devices = len(parts)
    rows = entries.shape[1]
    factor = HEAD_DIM ** (-0.5) * float(np.log2(np.e))
    part_rows = rows * local_heads

    def body(m, *refs):
        p_refs = refs[:devices]
        h_ref, e_ref, o_ref, q_all, out = refs[devices:]
        for h in range(local_heads):
            row = 2 * h_rows + h * rows
            q_all[pl.ds(h, rows, stride=local_heads), :] = h_ref[row : row + rows, :].astype(F32)
        stats = [p[part_rows : part_rows + local_heads, :] for p in p_refs]
        keys, values = e_ref[0].astype(F32), e_ref[1].astype(F32)
        for b in range(rows):
            here = slice(b * local_heads, (b + 1) * local_heads)
            own = jnp.sum(q_all[here, :] * keys[b : b + 1, :], axis=-1, keepdims=True)
            tops = [s[:, b : b + 1] for s in stats]
            top = own
            for t in tops:
                top = jnp.maximum(top, t)
            weight = jnp.exp2((own - top) * factor)
            total = weight
            summed = weight.astype(BF16).astype(F32) * values[b : b + 1, :]
            for s, t, p in zip(stats, tops, p_refs):
                share = jnp.exp2((t - top) * factor)
                total = total + share * s[:, rows + b : rows + b + 1]
                summed = summed + share * p[here, :]
            out[here, :] = summed / total
        for h in range(local_heads):
            o_ref[:, h * HEAD_DIM : (h + 1) * HEAD_DIM] = out[pl.ds(h, rows, stride=local_heads), :].astype(BF16)

    full = lambda i, m: (0, 0)
    return pl.pallas_call(
        body,
        grid_spec=pltpu.PrefetchScalarGridSpec(
            num_scalar_prefetch=1,
            grid=(1,),
            in_specs=[pl.BlockSpec(parts[0].shape, full)] * devices
            + [
                pl.BlockSpec(history.shape, full),
                pl.BlockSpec((2, rows, HEAD_DIM), lambda i, m: (0, 0, m[0] * local_heads // group)),
            ],
            out_specs=pl.BlockSpec((rows, local_heads * HEAD_DIM), full),
            scratch_shapes=[pltpu.VMEM((part_rows, HEAD_DIM), F32)] * 2,
        ),
        out_shape=jax.ShapeDtypeStruct((rows, local_heads * HEAD_DIM), BF16),
        compiler_params=params(8),
        name="join",
    )(meta, *parts, history, to_hbm(entries))


def attend(slots, first, count, block, queries, history, fresh, decoded, weight, meta, h_rows, p_rows):
    devices = len(history)
    p_pad = fresh[0].shape[0] // 2
    local_width = queries.shape[1]
    local_heads = local_width // HEAD_DIM
    model = weight.shape[1]
    h_keys, p_keys = devices * h_rows, devices * p_pad
    keys = h_keys + p_keys
    order = [s for s in slots if s % 2 == 0] + [s for s in slots if s % 2 == 1]
    half = len(order) // 2 * count
    factor = HEAD_DIM ** (-0.5) * float(np.log2(np.e))
    has_decode = decoded is not None
    decode_rows = decoded.shape[0] if has_decode else 0

    def body(m, q, *refs):
        h_refs, f_refs = refs[:devices], refs[devices : 2 * devices]
        rest = refs[2 * devices :]
        if has_decode:
            dec_ref, rest = rest[0], rest[1:]
        w, keep_ref, give_ref, k_all, v_all, att = rest
        me, valid_rows = m[0], m[1]
        for k in range(devices):
            for part, dst in ((0, k_all), (1, v_all)):
                dst[k * h_rows : (k + 1) * h_rows, :] = h_refs[k][part * h_rows : (part + 1) * h_rows, :]
                dst[h_keys + k * p_pad : h_keys + (k + 1) * p_pad, :] = f_refs[k][
                    part * p_pad : (part + 1) * p_pad, :
                ]
        column = lax.broadcasted_iota(jnp.int32, (1, h_keys), 1)
        place = ((column // h_rows) ^ me) * h_rows + column % h_rows
        history_bias = jnp.where(place < valid_rows, 0.0, MASKED)
        column = lax.broadcasted_iota(jnp.int32, (1, p_keys), 1)
        inner = column % p_pad
        seen_from = jnp.where(inner < p_rows, ((column // p_pad) ^ me) * p_rows + inner, 1 << 20)
        for i, slot in enumerate(order):
            target = slot ^ me
            row0 = pl.multiple_of(target * block + first, 16)
            rows = row0 + lax.broadcasted_iota(jnp.int32, (count, 1), 0)
            bias = jnp.where(seen_from <= rows, 0.0, MASKED)
            bias = jnp.concatenate([jnp.broadcast_to(history_bias, (count, h_keys)), bias], axis=1)
            for h in range(local_heads):
                here = slice(h * HEAD_DIM, (h + 1) * HEAD_DIM)
                scores = lax.dot_general(
                    q[pl.ds(row0, count), here], k_all[...], (((1,), (1,)), ((), ())), preferred_element_type=F32
                )
                scores = scores + bias
                top = jnp.max(scores, axis=-1, keepdims=True)
                weights = jnp.exp2((scores - top) * factor)
                total = jnp.sum(weights, axis=-1, keepdims=True)
                summed = jnp.dot(weights.astype(BF16), v_all[...], preferred_element_type=F32)
                att[i * count : (i + 1) * count, here] = (summed / total).astype(BF16)
            if has_decode:

                @pl.when(target == devices - 1)
                def _():
                    att[(i + 1) * count - decode_rows : (i + 1) * count, :] = dec_ref[...]

        for c in range(0, model, COLUMNS):
            out = jnp.dot(att[...], w[:, c : c + COLUMNS], preferred_element_type=F32).astype(BF16)
            keep_ref[:, c : c + COLUMNS] = out[:half]
            give_ref[:, c : c + COLUMNS] = out[half:]

    flops = 2 * len(order) * count * (2 * local_width * keys + local_width * model)
    n_vmem = 2 + 2 * devices + has_decode
    return pl.pallas_call(
        body,
        in_specs=[smem()] + [in_vmem()] * n_vmem,
        out_specs=[in_vmem()] * 2,
        out_shape=[jax.ShapeDtypeStruct((half, model), BF16)] * 2,
        scratch_shapes=[
            pltpu.VMEM((keys, HEAD_DIM), BF16),
            pltpu.VMEM((keys, HEAD_DIM), BF16),
            pltpu.VMEM((2 * half, local_width), BF16),
        ],
        compiler_params=params(24),
        cost_estimate=pl.CostEstimate(flops=flops, transcendentals=0, bytes_accessed=weight.size * 2),
    )(meta, queries, *history, *fresh, *([decoded] if has_decode else []), weight)


def finish(first, residual, own, given, crossed, gain, previous):
    block, model = residual.shape
    count = crossed[0].shape[0]
    tile = 16
    n_cross = len(crossed)

    def body(res_ref, own_ref, given_ref, *refs):
        cross = refs[:n_cross]
        gain_ref = refs[n_cross]
        hidden_ref, normed_ref = refs[-2:]
        hidden = res_ref[...].astype(F32) + own_ref[...].astype(F32) + given_ref[...].astype(F32)
        for c in cross:
            hidden = hidden + c[...].astype(F32)
        mean = jnp.mean(hidden * hidden, axis=-1, keepdims=True)
        hidden_ref[...] = hidden.astype(BF16)
        normed_ref[...] = (hidden * lax.rsqrt(mean + EPS) * gain_ref[...]).astype(BF16)

    here = pl.BlockSpec((tile, model), lambda i: (first // tile + i, 0))
    local = pl.BlockSpec((tile, model), lambda i: (i, 0))
    n_in = 3 + n_cross + 1
    return pl.pallas_call(
        body,
        grid=(count // tile,),
        in_specs=[here, here, here]
        + [local] * n_cross
        + [pl.BlockSpec((1, model), lambda i: (0, 0))]
        + [hbm()] * len(previous),
        out_specs=[here, here],
        out_shape=[jax.ShapeDtypeStruct((block, model), BF16)] * 2,
        input_output_aliases={n_in + i: i for i in range(len(previous))},
        compiler_params=params(16),
    )(residual, own, given, *crossed, gain, *previous)


def step(
    prompt_queries,
    prompt_entries,
    history_cache,
    decode_queries,
    decode_entries,
    decode_cache,
    decode_lengths,
    prompt_start,
    out_weight,
    residual,
    norm_gain,
):
    devices = lax.axis_size("tp")
    local_heads = prompt_queries.shape[1] // HEAD_DIM
    kv_heads = history_cache.shape[2] // HEAD_DIM
    group = devices * local_heads // kv_heads
    block = residual.shape[0]
    h_rows, p_rows = history_cache.shape[1], prompt_entries.shape[1]
    assert group % local_heads == 0 and devices & (devices - 1) == 0
    assert block >= decode_queries.shape[0]
    meta = jnp.concatenate([lax.axis_index("tp").astype(jnp.int32)[None], prompt_start, decode_lengths])

    def swap(value, k):
        return lax.ppermute(value, "tp", [(i, i ^ k) for i in range(devices)])

    def swapped(values):
        return [values[0]] + [swap(values[k], k) for k in range(1, devices)]

    history = swapped(pack_history(history_cache, decode_queries, meta, devices, local_heads, group))
    fresh, cache, queries = stage(
        prompt_entries, decode_cache, prompt_queries, decode_queries, meta, devices, local_heads, group
    )
    fresh = swapped(fresh)
    parts = swapped(decode_partials(history, cache, meta, h_rows, local_heads, group))
    decoded = decode_join(parts, history[0], decode_entries, meta, h_rows, local_heads, group)

    def attended(slots, first, count, decoded):
        return attend(slots, first, count, block, queries, history, fresh, decoded, out_weight, meta, h_rows, p_rows)

    chunks = [c * block // sum(CHUNKS) for c in CHUNKS]
    if any(c % 16 for c in chunks):
        chunks = [block]
    crossed, first = [], 0
    for count in chunks:
        keep, give = attended(list(range(2, devices)), first, count, decoded if first + count == block else None)
        taken = swap(give, 1)
        pair = (keep.astype(F32) + taken.astype(F32)).astype(BF16)
        crossed.append((first, [swap(pair[(k // 2 - 1) * count : k // 2 * count], k) for k in range(2, devices, 2)]))
        first += count
    own, give = attended([0, 1], 0, block, decoded)
    given = swap(give, 1)
    gain = norm_gain[None, :]
    outs = []
    for first, pieces in crossed:
        outs = finish(first, residual, own, given, pieces, gain, outs)
    return tuple(outs)


def solution(mesh):
    placed = (
        P("rep", "tp"),
        P("rep", "tp", None),
        P("rep", "tp", None),
        P("rep", "tp"),
        P("rep", None, None),
        P("rep", None, "tp", None),
        P("rep"),
        P("rep"),
        P("tp", None),
        P("tp", "rep"),
        P(),
    )
    return jax.shard_map(
        step,
        mesh=mesh,
        in_specs=placed,
        out_specs=(P("tp", "rep"), P("tp", "rep")),
        check_vma=False,
    )
```

profile of v0, /device:TPU:0, one launch (start us, length us, event | category | flops | bytes accessed | tf_op | source)
XLA Modules:
  0.0 77.0 jit_solution(5787275997316545688)
XLA Ops:
  1.3 0.7 pad_add_fusion.m
  2.0 1.7 %pack_history.1 = (bf16[640,128]{1,0:T(8,128)(2,1)S(1)}, bf16[640,128]{1,0:T(8,128)(2,1)S(1)}, bf16[640,128]{1,0:T(8,128)(2,1)S(1)}, bf16[640,128]{1,0:T(8,128)(2,1)S(1)}) custom-call(s32[18]{0:T(128)S(1)} %pad_add_fusion.m, bf16[2,256,512]{2,1,0:T(8,128)(2,1)} %refs_3_.2, bf16[2,256,512]{2,1,0:T(8,128)(2,1)} %refs_3_.2, bf16[2,256,512]{2,1,0:T(8,128)(2,1)} %refs_3_.2, ...), custom_call_target="tpu_custom_call" | custom-call | tf_op jit(solution)/shard_map/pack_history/pallas_call | solution.py:66
  3.7 0.6 collective-permute-start
  4.3 2.6 %collective-permute-start.1 = (bf16[640,128]{1,0:T(8,128)(2,1)S(1)}, bf16[640,128]{1,0:T(8,128)(2,1)S(1)}, u32[]{:S(2)}, u32[]{:S(2)}) collective-permute-start(bf16[640,128]{1,0:T(8,128)(2,1)S(1)} %get-tuple-element.27), channel_id=1, source_target_pairs={{0,2},{1,3},{2,0},{3,1},{4,6},{5,7},{6,4},{7,5},{8,10},{9,11},{10,... | collective-permute-start | bytes 491528 | tf_op jit(solution)/shard_map/ppermute | solution.py:388
  6.9 0.0 collective-permute-start.2
  6.9 1.1 %copy.15.refs_0_.refs_1_.refs_2_.refs_3_ = bf16[2,124,512]{2,1,0:T(8,128)(2,1)S(1)} copy(bf16[2,124,512]{2,0,1:T(2,128)(2,1)} %param.12) | data formatting | bytes 507904 | tf_op args[1]
  8.1 0.0 slice-start.1
  8.1 4.2 %stage.1 = (bf16[256,128]{1,0:T(8,128)(2,1)S(1)}, bf16[256,128]{1,0:T(8,128)(2,1)S(1)}, bf16[256,128]{1,0:T(8,128)(2,1)S(1)}, bf16[256,128]{1,0:T(8,128)(2,1)S(1...) custom-call(s32[18]{0:T(128)S(1)} %pad_add_fusion.m, ...), custom_call_target="tpu_custom_call" | custom-call | tf_op jit(solution)/shard_map/stage/pallas_call | solution.py:117
  12.3 0.2 collective-permute-start.3
  12.5 1.9 %collective-permute-start.4 = (bf16[256,128]{1,0:T(8,128)(2,1)S(1)}, bf16[256,128]{1,0:T(8,128)(2,1)S(1)}, u32[]{:S(2)}, u32[]{:S(2)}) collective-permute-start(bf16[256,128]{1,0:T(8,128)(2,1)S(1)} %get-tuple-element.31), channel_id=1, source_target_pairs={{0,2},{1,3},{2,0},{3,1},{4,6},{5,7},{6,4},{7,5},{8,10},{9,11},{10,... | collective-permute-start | bytes 196616 | tf_op jit(solution)/shard_map/ppermute | solution.py:388
  14.4 0.5 collective-permute-done.2.refs_3_
  14.9 2.3 %decode.1 = (f32[136,128]{1,0:T(8,128)S(1)}, f32[136,128]{1,0:T(8,128)S(1)}, f32[136,128]{1,0:T(8,128)S(1)}, f32[136,128]{1,0:T(8,128)S(1)}) custom-call(s32[18]{0:T(128)S(1)} %pad_add_fusion.m, bf16[640,128]{1,0:T(8,128)(2,1)S(1)} %get-tuple-element.25.refs_0_.refs_4_, bf16[640,128]{1,0:T(8,128)(2,1)S(1)} %collective-permute-done.refs_1_, ...), custom_call_target="tpu_custom_call" | custom-call | tf_op jit(solution)/shard_map/decode/pallas_call | solution.py:189
  17.2 0.2 collective-permute-start.6
  17.4 1.7 %collective-permute-start.7 = (f32[136,128]{1,0:T(8,128)S(1)}, f32[136,128]{1,0:T(8,128)S(1)}, u32[]{:S(2)}, u32[]{:S(2)}) collective-permute-start(f32[136,128]{1,0:T(8,128)S(1)} %get-tuple-element.36), channel_id=1, source_target_pairs={{0,2},{1,3},{2,0},{3,1},{4,6},{5,7},{6,4},{7,5},{8,10},{9,11},{10,... | collective-permute-start | bytes 208904 | tf_op jit(solution)/shard_map/ppermute | solution.py:388
  19.1 0.0 collective-permute-start.8
  19.1 8.2 %shard_map.124 = (bf16[64,4096]{1,0:T(8,128)(2,1)S(1)}, bf16[64,4096]{1,0:T(8,128)(2,1)S(1)}) custom-call(s32[18]{0:T(128)S(1)} %pad_add_fusion.m, bf16[512,1024]{1,0:T(8,128)(2,1)S(1)} %get-tuple-element.24.q, bf16[640,128]{1,0:T(8,128)(2,1)S(1)} %get-tuple-element.25.refs_0_.refs_4_, bf16[640,128]{1,0:T(8,128)(2,1)S(1)} %collective-permute-done.refs_1_, ...), custom_call_target="tpu_custom_call" | custom-call | flops 1879048192 | bytes 8388608 | tf_op jit(solution)/shard_map/pallas_call | solution.py:315
  27.4 0.5 collective-permute-start.12
  27.9 2.4 %join.1.refs_8_ = bf16[16,1024]{1,0:T(8,128)(2,1)S(1)} custom-call(s32[18]{0:T(128)S(1)} %pad_add_fusion.m, f32[136,128]{1,0:T(8,128)S(1)} %get-tuple-element.34.refs_0_, f32[136,128]{1,0:T(8,128)S(1)} %collective-permute-done.6.refs_1_, f32[136,128]{1,0:T(8,128)S(1)} %collective-permute-done.7.refs_2_, f32[136,128]{1,0:T(8,128)S(1)} %collective-permute-done.8.refs_3_, ...), custom_call_target="tpu_custom_call" | custom-call | tf_op jit(solution)/shard_map/join/pallas_call | solution.py:233
  30.3 8.7 %shard_map.123 = (bf16[64,4096]{1,0:T(8,128)(2,1)S(1)}, bf16[64,4096]{1,0:T(8,128)(2,1)S(1)}) custom-call(s32[18]{0:T(128)S(1)} %pad_add_fusion.m, bf16[512,1024]{1,0:T(8,128)(2,1)S(1)} %get-tuple-element.24.q, bf16[640,128]{1,0:T(8,128)(2,1)S(1)} %get-tuple-element.25.refs_0_.refs_4_, bf16[640,128]{1,0:T(8,128)(2,1)S(1)} %collective-permute-done.refs_1_, ...), custom_call_target="tpu_custom_call" | custom-call | flops 1879048192 | bytes 8388608 | tf_op jit(solution)/shard_map/pallas_call | solution.py:315
  39.0 0.0 copy-start
  39.0 0.0 copy-start.1
  39.0 0.2 collective-permute-start.10
  39.2 10.0 %shard_map.122 = (bf16[128,4096]{1,0:T(8,128)(2,1)S(1)}, bf16[128,4096]{1,0:T(8,128)(2,1)S(1)}) custom-call(s32[18]{0:T(128)S(1)} %pad_add_fusion.m, bf16[512,1024]{1,0:T(8,128)(2,1)S(1)} %get-tuple-element.24.q, bf16[640,128]{1,0:T(8,128)(2,1)S(1)} %get-tuple-element.25.refs_0_.refs_4_, bf16[640,128]{1,0:T(8,128)(2,1)S(1)} %collective-permute-done.refs_1_, ...), custom_call_target="tpu_custom_call" | custom-call | flops 3758096384 | bytes 8388608 | tf_op jit(solution)/shard_map/pallas_call | solution.py:315
  49.2 0.5 collective-permute-start.9
  49.7 0.1 add_convert_fusion
  49.8 1.8 %collective-permute-start.13 = (bf16[64,4096]{1,0:T(8,128)(2,1)S(1)}, bf16[64,4096]{1,0:T(8,128)(2,1)S(1)}, u32[]{:S(2)}, u32[]{:S(2)}) collective-permute-start(bf16[64,4096]{1,0:T(8,128)(2,1)S(1)} %add_convert_fusion), channel_id=1, source_target_pairs={{0,2},{1,3},{2,0},{3,1},{4,6},{5,7},{6,4},{7,5},{8,10},{9,11},{10,... | collective-permute-start | bytes 1572872 | tf_op jit(solution)/shard_map/ppermute | solution.py:388
  51.6 0.1 add_convert_fusion.1
  51.7 0.4 collective-permute-start.11
  52.1 12.6 %collective-permute-done.13.refs_0_ = bf16[64,4096]{1,0:T(8,128)(2,1)S(1)} collective-permute-done((bf16[64,4096]{1,0:T(8,128)(2,1)S(1)}, bf16[64,4096]{1,0:T(8,128)(2,1)S(1)}, u32[]{:S(2)}, u32[]{:S(2)}) %collective-permute-start.13) | collective-permute-done | bytes 524320 | tf_op jit(solution)/shard_map/ppermute | solution.py:388
  64.7 2.0 %shard_map.125 = (bf16[128,4096]{1,0:T(8,128)(2,1)}, bf16[128,4096]{1,0:T(8,128)(2,1)}) custom-call(bf16[128,4096]{1,0:T(8,128)(2,1)S(1)} %copy-done, bf16[128,4096]{1,0:T(8,128)(2,1)S(1)} %get-tuple-element.38.own_ref, bf16[128,4096]{1,0:T(8,128)(2,1)S(1)} %collective-permute-done.9.given_ref, bf16[64,4096]{1,0:T(8,128)(2,1)S(1)} %collective-permute-done.13.refs_0_, ...), custom_call_target="tpu_custom_call" | custom-call | tf_op jit(solution)/shard_map/pallas_call | solution.py:350
  66.7 8.4 %collective-permute-done.11.refs_0_ = bf16[64,4096]{1,0:T(8,128)(2,1)S(1)} collective-permute-done((bf16[64,4096]{1,0:T(8,128)(2,1)S(1)}, bf16[64,4096]{1,0:T(8,128)(2,1)S(1)}, u32[]{:S(2)}, u32[]{:S(2)}) %collective-permute-start.11) | collective-permute-done | bytes 524320 | tf_op jit(solution)/shard_map/ppermute | solution.py:388
  75.0 2.0 %shard_map.126 = (bf16[128,4096]{1,0:T(8,128)(2,1)}, bf16[128,4096]{1,0:T(8,128)(2,1)}) custom-call(bf16[128,4096]{1,0:T(8,128)(2,1)S(1)} %copy-done, bf16[128,4096]{1,0:T(8,128)(2,1)S(1)} %get-tuple-element.38.own_ref, bf16[128,4096]{1,0:T(8,128)(2,1)S(1)} %collective-permute-done.9.given_ref, ...), custom_call_target="tpu_custom_call", output_to_operand_aliasing={{0}: (5, {}), {1}: (6, {})} | custom-call | tf_op jit(solution)/shard_map/pallas_call | solution.py:350
  (18 shorter events, 0.0 us)
Async XLA Ops:
  3.7 10.7 %collective-permute-start = (bf16[640,128]{1,0:T(8,128)(2,1)S(1)}, bf16[640,128]{1,0:T(8,128)(2,1)S(1)}, u32[]{:S(2)}, u32[]{:S(2)}) collective-permute-start(bf16[640,128]{1,0:T(8,128)(2,1)S(1)} %get-tuple-element.26), channel_id=1, source_target_pairs={{0,1},{1,0},{2,3},{3,2},{4,5},{5,4},{6,7},{7,6},{8,9},{9,8},{10,11... | collective-permute-start | bytes 491528 | tf_op jit(solution)/shard_map/ppermute | solution.py:388
  4.3 10.1 %collective-permute-start.1 = (bf16[640,128]{1,0:T(8,128)(2,1)S(1)}, bf16[640,128]{1,0:T(8,128)(2,1)S(1)}, u32[]{:S(2)}, u32[]{:S(2)}) collective-permute-start(bf16[640,128]{1,0:T(8,128)(2,1)S(1)} %get-tuple-element.27), channel_id=1, source_target_pairs={{0,2},{1,3},{2,0},{3,1},{4,6},{5,7},{6,4},{7,5},{8,10},{9,11},{10,... | collective-permute-start | bytes 491528 | tf_op jit(solution)/shard_map/ppermute | solution.py:388
  6.9 8.0 %collective-permute-start.2 = (bf16[640,128]{1,0:T(8,128)(2,1)S(1)}, bf16[640,128]{1,0:T(8,128)(2,1)S(1)}, u32[]{:S(2)}, u32[]{:S(2)}) collective-permute-start(bf16[640,128]{1,0:T(8,128)(2,1)S(1)} %get-tuple-element.28), channel_id=1, source_target_pairs={{0,3},{1,2},{2,1},{3,0},{4,7},{5,6},{6,5},{7,4},{8,11},{9,10},{10,... | collective-permute-start | bytes 491528 | tf_op jit(solution)/shard_map/ppermute | solution.py:388
  6.9 12.2 %slice-start = ((s8[8388608]{0:T(1024)(128)(4,1)}), s8[4194304]{0:T(1024)(128)(4,1)S(1)}, s32[]{:S(2)}) async-start(s8[8388608]{0:T(1024)(128)(4,1)} %bitcast.2), calls=%async_computation | async-start | bytes 8388608
  8.1 11.1 %slice-start.1 = ((s8[8388608]{0:T(1024)(128)(4,1)}), s8[4194304]{0:T(1024)(128)(4,1)S(1)}, s32[]{:S(2)}) async-start(s8[8388608]{0:T(1024)(128)(4,1)} %bitcast.2), calls=%async_computation.1 | async-start | bytes 8388608
  12.3 6.8 %collective-permute-start.3 = (bf16[256,128]{1,0:T(8,128)(2,1)S(1)}, bf16[256,128]{1,0:T(8,128)(2,1)S(1)}, u32[]{:S(2)}, u32[]{:S(2)}) collective-permute-start(bf16[256,128]{1,0:T(8,128)(2,1)S(1)} %get-tuple-element.30), channel_id=1, source_target_pairs={{0,1},{1,0},{2,3},{3,2},{4,5},{5,4},{6,7},{7,6},{8,9},{9,8},{10,11... | collective-permute-start | bytes 196616 | tf_op jit(solution)/shard_map/ppermute | solution.py:388
  12.5 6.6 %collective-permute-start.4 = (bf16[256,128]{1,0:T(8,128)(2,1)S(1)}, bf16[256,128]{1,0:T(8,128)(2,1)S(1)}, u32[]{:S(2)}, u32[]{:S(2)}) collective-permute-start(bf16[256,128]{1,0:T(8,128)(2,1)S(1)} %get-tuple-element.31), channel_id=1, source_target_pairs={{0,2},{1,3},{2,0},{3,1},{4,6},{5,7},{6,4},{7,5},{8,10},{9,11},{10,... | collective-permute-start | bytes 196616 | tf_op jit(solution)/shard_map/ppermute | solution.py:388
  14.4 4.7 %collective-permute-start.5 = (bf16[256,128]{1,0:T(8,128)(2,1)S(1)}, bf16[256,128]{1,0:T(8,128)(2,1)S(1)}, u32[]{:S(2)}, u32[]{:S(2)}) collective-permute-start(bf16[256,128]{1,0:T(8,128)(2,1)S(1)} %get-tuple-element.32), channel_id=1, source_target_pairs={{0,3},{1,2},{2,1},{3,0},{4,7},{5,6},{6,5},{7,4},{8,11},{9,10},{10,... | collective-permute-start | bytes 196616 | tf_op jit(solution)/shard_map/ppermute | solution.py:388
  17.2 10.7 %collective-permute-start.6 = (f32[136,128]{1,0:T(8,128)S(1)}, f32[136,128]{1,0:T(8,128)S(1)}, u32[]{:S(2)}, u32[]{:S(2)}) collective-permute-start(f32[136,128]{1,0:T(8,128)S(1)} %get-tuple-element.35), channel_id=1, source_target_pairs={{0,1},{1,0},{2,3},{3,2},{4,5},{5,4},{6,7},{7,6},{8,9},{9,8},{10,11... | collective-permute-start | bytes 208904 | tf_op jit(solution)/shard_map/ppermute | solution.py:388
  17.4 10.5 %collective-permute-start.7 = (f32[136,128]{1,0:T(8,128)S(1)}, f32[136,128]{1,0:T(8,128)S(1)}, u32[]{:S(2)}, u32[]{:S(2)}) collective-permute-start(f32[136,128]{1,0:T(8,128)S(1)} %get-tuple-element.36), channel_id=1, source_target_pairs={{0,2},{1,3},{2,0},{3,1},{4,6},{5,7},{6,4},{7,5},{8,10},{9,11},{10,... | collective-permute-start | bytes 208904 | tf_op jit(solution)/shard_map/ppermute | solution.py:388
  19.1 8.8 %collective-permute-start.8 = (f32[136,128]{1,0:T(8,128)S(1)}, f32[136,128]{1,0:T(8,128)S(1)}, u32[]{:S(2)}, u32[]{:S(2)}) collective-permute-start(f32[136,128]{1,0:T(8,128)S(1)} %get-tuple-element.37), channel_id=1, source_target_pairs={{0,3},{1,2},{2,1},{3,0},{4,7},{5,6},{6,5},{7,4},{8,11},{9,10},{10,... | collective-permute-start | bytes 208904 | tf_op jit(solution)/shard_map/ppermute | solution.py:388
  27.4 22.3 %collective-permute-start.12 = (bf16[64,4096]{1,0:T(8,128)(2,1)S(1)}, bf16[64,4096]{1,0:T(8,128)(2,1)S(1)}, u32[]{:S(2)}, u32[]{:S(2)}) collective-permute-start(bf16[64,4096]{1,0:T(8,128)(2,1)S(1)} %get-tuple-element.43), channel_id=1, source_target_pairs={{0,1},{1,0},{2,3},{3,2},{4,5},{5,4},{6,7},{7,6},{8,9},{9,8},{10,11... | collective-permute-start | bytes 1572872 | tf_op jit(solution)/shard_map/ppermute | solution.py:388
  39.0 25.7 %copy-start = (bf16[128,4096]{1,0:T(8,128)(2,1)S(1)}, bf16[128,4096]{1,0:T(8,128)(2,1)}, u32[]{:S(2)}) copy-start(bf16[128,4096]{1,0:T(8,128)(2,1)} %res_ref.3) | copy-start | bytes 3145732
  39.0 25.7 %copy-start.1 = (f32[4096]{0:T(1024)S(1)}, f32[4096]{0:T(1024)}, u32[]{:S(2)}) copy-start(f32[4096]{0:T(1024)} %param.21) | copy-start | bytes 49156
  39.0 12.6 %collective-permute-start.10 = (bf16[64,4096]{1,0:T(8,128)(2,1)S(1)}, bf16[64,4096]{1,0:T(8,128)(2,1)S(1)}, u32[]{:S(2)}, u32[]{:S(2)}) collective-permute-start(bf16[64,4096]{1,0:T(8,128)(2,1)S(1)} %get-tuple-element.41), channel_id=1, source_target_pairs={{0,1},{1,0},{2,3},{3,2},{4,5},{5,4},{6,7},{7,6},{8,9},{9,8},{10,11... | collective-permute-start | bytes 1572872 | tf_op jit(solution)/shard_map/ppermute | solution.py:388
  49.2 15.5 %collective-permute-start.9 = (bf16[128,4096]{1,0:T(8,128)(2,1)S(1)}, bf16[128,4096]{1,0:T(8,128)(2,1)S(1)}, u32[]{:S(2)}, u32[]{:S(2)}) collective-permute-start(bf16[128,4096]{1,0:T(8,128)(2,1)S(1)} %get-tuple-element.39), channel_id=1, source_target_pairs={{0,1},{1,0},{2,3},{3,2},{4,5},{5,4},{6,7},{7,6},{8,9},{9,8},{10,11... | collective-permute-start | bytes 3145736 | tf_op jit(solution)/shard_map/ppermute | solution.py:388
  49.8 14.9 %collective-permute-start.13 = (bf16[64,4096]{1,0:T(8,128)(2,1)S(1)}, bf16[64,4096]{1,0:T(8,128)(2,1)S(1)}, u32[]{:S(2)}, u32[]{:S(2)}) collective-permute-start(bf16[64,4096]{1,0:T(8,128)(2,1)S(1)} %add_convert_fusion), channel_id=1, source_target_pairs={{0,2},{1,3},{2,0},{3,1},{4,6},{5,7},{6,4},{7,5},{8,10},{9,11},{10,... | collective-permute-start | bytes 1572872 | tf_op jit(solution)/shard_map/ppermute | solution.py:388
  51.7 23.3 %collective-permute-start.11 = (bf16[64,4096]{1,0:T(8,128)(2,1)S(1)}, bf16[64,4096]{1,0:T(8,128)(2,1)S(1)}, u32[]{:S(2)}, u32[]{:S(2)}) collective-permute-start(bf16[64,4096]{1,0:T(8,128)(2,1)S(1)} %add_convert_fusion.1), channel_id=1, source_target_pairs={{0,2},{1,3},{2,0},{3,1},{4,6},{5,7},{6,4},{7,5},{8,10},{9,11},{10,... | collective-permute-start | bytes 1572872 | tf_op jit(solution)/shard_map/ppermute | solution.py:388
where the time goes:
time: 77.2 us; the launch traced here: 77 us
  Pallas kernels  41.5 us (54%)
  waiting for transfers between devices  21.5 us (28%)
  starting transfers between devices  10.5 us (14%)
  between operations  1.4 us (2%)
  local copies, waits for them, and re-layouts  1.15 us (1%)
  other arithmetic  0.98 us (1%)
    pallas_call x3, Pallas kernels, attend(): pl.pallas_call(body, in_specs=[smem()] + [in_vmem()] * n_vmem, out_specs=...  26.9 us
    ppermute x14, waiting for transfers between devices, swap(): return lax.ppermute(value, 'tp', [(i, i ^ k) for i in range(devices)])  21.5 us
    ppermute x14, starting transfers between devices, swap(): return lax.ppermute(value, 'tp', [(i, i ^ k) for i in range(devices)])  10.5 us
    pallas_call x1, Pallas kernels, stage(): pl.pallas_call(body, grid_spec=pltpu.PrefetchScalarGridSpec(num_scalar_pr...  4.19 us
    pallas_call x2, Pallas kernels, finish(): pl.pallas_call(body, grid=(count // tile,), in_specs=[here, here, here] +...  3.94 us
    pallas_call x1, Pallas kernels, decode_join(): pl.pallas_call(body, grid_spec=pltpu.PrefetchScalarGridSpec(num_scalar_pr...  2.43 us
    pallas_call x1, Pallas kernels, decode_partials(): pl.pallas_call(body, in_specs=[smem()] + [in_vmem()] * (devices + 1), out...  2.25 us
    pallas_call x1, Pallas kernels, pack_history(): pl.pallas_call(body, grid_spec=pltpu.PrefetchScalarGridSpec(num_scalar_pr...  1.73 us
  transfers between devices with their start and end apart: 14, of which 3 were waited for; matrix products, arithmetic and copies ran while one was open for 2% of the time, Pallas kernels for 49%

commit v1 on v0

--- a/solution.py
+++ b/solution.py
@@ -12,6 +12,7 @@
 EPS = 1e-05
 CHUNKS = (64, 64)
 COLUMNS = 512
+GROUP_ROWS = 256
 
 F32 = jnp.float32
 BF16 = jnp.bfloat16
@@ -78,20 +79,45 @@
     )(meta, *([to_hbm(history)] * devices), to_hbm(queries))
 
 
-def stage(prompt, cache, prompt_queries, decode_queries, meta, devices, local_heads, group):
+def pack_fresh(prompt, meta, devices, local_heads, group):
     p_rows = prompt.shape[1]
     p_pad = round_up(p_rows, 16)
+
+    def head_of(k):
+        return lambda i, m: (0, 0, (m[0] ^ k) * local_heads // group)
+
+    def body(m, *refs):
+        for k in range(devices):
+            p_ref, o_ref = refs[k], refs[devices + k]
+            for part in range(2):
+                if p_pad > p_rows:
+                    fresh = jnp.concatenate(
+                        [p_ref[part].astype(F32), jnp.zeros((p_pad - p_rows, HEAD_DIM), F32)], axis=0
+                    ).astype(BF16)
+                else:
+                    fresh = p_ref[part]
+                o_ref[part * p_pad : (part + 1) * p_pad, :] = fresh
+
+    return pl.pallas_call(
+        body,
+        grid_spec=pltpu.PrefetchScalarGridSpec(
+            num_scalar_prefetch=1,
+            grid=(1,),
+            in_specs=[pl.BlockSpec((2, p_rows, HEAD_DIM), head_of(k)) for k in range(devices)],
+            out_specs=[pl.BlockSpec((2 * p_pad, HEAD_DIM), lambda i, m: (0, 0))] * devices,
+        ),
+        out_shape=[jax.ShapeDtypeStruct((2 * p_pad, HEAD_DIM), BF16)] * devices,
+        compiler_params=params(8),
+        name="pack_fresh",
+    )(meta, *([prompt] * devices))
+
+
+def stage(cache, prompt_queries, decode_queries):
     prompt_rows, decode_rows = prompt_queries.shape[0], decode_queries.shape[0]
     parts = 4
     per = cache.shape[1] // parts
 
-    def head_of(k):
-        return lambda i, m: (0, 0, (m[0] ^ k) * local_heads // group)
-
-    def body(m, *refs):
-        cache_hbm, q_hbm, dq_hbm = refs[devices : devices + 3]
-        o_refs = refs[devices + 3 : 2 * devices + 3]
-        cache_ref, q_ref, sem = refs[2 * devices + 3 :]
+    def body(cache_hbm, q_hbm, dq_hbm, cache_ref, q_ref, sem):
         copies = [
             pltpu.make_async_copy(q_hbm, q_ref.at[0:prompt_rows, :], sem.at[0]),
             pltpu.make_async_copy(dq_hbm, q_ref.at[prompt_rows : prompt_rows + decode_rows, :], sem.at[1]),
@@ -101,37 +127,21 @@
             copies.append(pltpu.make_async_copy(cache_hbm.at[here], cache_ref.at[here], sem.at[2 + i]))
         for copy in copies:
             copy.start()
-        for k in range(devices):
-            p_ref, o_ref = refs[k], o_refs[k]
-            for part in range(2):
-                if p_pad > p_rows:
-                    fresh = jnp.concatenate(
-                        [p_ref[part].astype(F32), jnp.zeros((p_pad - p_rows, HEAD_DIM), F32)], axis=0
-                    ).astype(BF16)
-                else:
-                    fresh = p_ref[part]
-                o_ref[part * p_pad : (part + 1) * p_pad, :] = fresh
         for copy in copies:
             copy.wait()
 
-    outs = pl.pallas_call(
-        body,
-        grid_spec=pltpu.PrefetchScalarGridSpec(
-            num_scalar_prefetch=1,
-            grid=(1,),
-            in_specs=[pl.BlockSpec((2, p_rows, HEAD_DIM), head_of(k)) for k in range(devices)] + [in_hbm()] * 3,
-            out_specs=[pl.BlockSpec((2 * p_pad, HEAD_DIM), lambda i, m: (0, 0))] * devices + [hbm(), hbm()],
-            scratch_shapes=[pltpu.SemaphoreType.DMA((2 + 2 * parts,))],
-        ),
-        out_shape=[jax.ShapeDtypeStruct((2 * p_pad, HEAD_DIM), BF16)] * devices
-        + [
+    return pl.pallas_call(
+        body,
+        in_specs=[in_hbm()] * 3,
+        out_specs=[in_vmem()] * 2,
+        out_shape=[
             pltpu.VMEM(cache.shape, BF16),
             pltpu.VMEM((prompt_rows + decode_rows, prompt_queries.shape[1]), BF16),
         ],
-        compiler_params=params(8),
+        scratch_shapes=[pltpu.SemaphoreType.DMA((2 + 2 * parts,))],
+        compiler_params=params(2),
         name="stage",
-    )(meta, *([prompt] * devices), to_hbm(cache), to_hbm(prompt_queries), to_hbm(decode_queries))
-    return outs[:devices], outs[devices], outs[devices + 1]
+    )(to_hbm(cache), to_hbm(prompt_queries), to_hbm(decode_queries))
 
 
 def decode_partials(history, cache, meta, h_rows, local_heads, group):
@@ -260,6 +270,7 @@
     order = [s for s in slots if s % 2 == 0] + [s for s in slots if s % 2 == 1]
     half = len(order) // 2 * count
     factor = HEAD_DIM ** (-0.5) * float(np.log2(np.e))
+    per = max(1, min(local_heads, GROUP_ROWS // count))
     has_decode = decoded is not None
     decode_rows = decoded.shape[0] if has_decode else 0
 
@@ -288,17 +299,24 @@
             rows = row0 + lax.broadcasted_iota(jnp.int32, (count, 1), 0)
             bias = jnp.where(seen_from <= rows, 0.0, MASKED)
             bias = jnp.concatenate([jnp.broadcast_to(history_bias, (count, h_keys)), bias], axis=1)
-            for h in range(local_heads):
-                here = slice(h * HEAD_DIM, (h + 1) * HEAD_DIM)
+            bias = jnp.concatenate([bias] * per, axis=0)
+            for g in range(0, local_heads, per):
+                stacked = jnp.concatenate(
+                    [q[pl.ds(row0, count), h * HEAD_DIM : (h + 1) * HEAD_DIM] for h in range(g, g + per)], axis=0
+                )
                 scores = lax.dot_general(
-                    q[pl.ds(row0, count), here], k_all[...], (((1,), (1,)), ((), ())), preferred_element_type=F32
+                    stacked, k_all[...], (((1,), (1,)), ((), ())), preferred_element_type=F32
                 )
                 scores = scores + bias
                 top = jnp.max(scores, axis=-1, keepdims=True)
                 weights = jnp.exp2((scores - top) * factor)
                 total = jnp.sum(weights, axis=-1, keepdims=True)
                 summed = jnp.dot(weights.astype(BF16), v_all[...], preferred_element_type=F32)
-                att[i * count : (i + 1) * count, here] = (summed / total).astype(BF16)
+                summed = (summed / total).astype(BF16)
+                for h in range(per):
+                    att[i * count : (i + 1) * count, (g + h) * HEAD_DIM : (g + h + 1) * HEAD_DIM] = summed[
+                        h * count : (h + 1) * count
+                    ]
             if has_decode:
 
                 @pl.when(target == devices - 1)
@@ -391,10 +409,8 @@
         return [values[0]] + [swap(values[k], k) for k in range(1, devices)]
 
     history = swapped(pack_history(history_cache, decode_queries, meta, devices, local_heads, group))
-    fresh, cache, queries = stage(
-        prompt_entries, decode_cache, prompt_queries, decode_queries, meta, devices, local_heads, group
-    )
-    fresh = swapped(fresh)
+    fresh = swapped(pack_fresh(prompt_entries, meta, devices, local_heads, group))
+    cache, queries = stage(decode_cache, prompt_queries, decode_queries)
     parts = swapped(decode_partials(history, cache, meta, h_rows, local_heads, group))
     decoded = decode_join(parts, history[0], decode_entries, meta, h_rows, local_heads, group)
 

time: 77.2 us -> 69.4 us (0.90)
  Pallas kernels: 41.5 us -> 32.9 us
    pallas_call x3, Pallas kernels: 26.9 us -> 18.6 us  [attend(): pl.pallas_call(body, in_specs=[smem()] + [in_vmem()] * n_vmem, out_specs=...]
    pallas_call x1 -> x2, Pallas kernels: 4.19 us -> 3.98 us  [the longest x1 3.33 us: stage(): pl.pallas_call(body, in_specs=[in_hbm()] * 3, out_specs=[in_vmem()] * 2,...]
  transfers between devices with their start and end apart: 14 -> 14, of which waited for: 3 -> 3; matrix products, arithmetic and copies ran while one was open for 2% -> 2% of each run, Pallas kernels for 49% -> 42%
where the time goes in v1:
time: 69.4 us; the launch traced here: 69.1 us
  Pallas kernels  32.9 us (47%)
  waiting for transfers between devices  22.1 us (32%)
  starting transfers between devices  10.7 us (15%)
  between operations  1.43 us (2%)
  local copies, waits for them, and re-layouts  1 us (1%)
  other arithmetic  0.99 us (1%)
    ppermute x14, waiting for transfers between devices, swap(): return lax.ppermute(value, 'tp', [(i, i ^ k) for i in range(devices)])  22.1 us
    pallas_call x3, Pallas kernels, attend(): pl.pallas_call(body, in_specs=[smem()] + [in_vmem()] * n_vmem, out_specs=...  18.6 us
    ppermute x14, starting transfers between devices, swap(): return lax.ppermute(value, 'tp', [(i, i ^ k) for i in range(devices)])  10.7 us
    pallas_call x2, Pallas kernels, finish(): pl.pallas_call(body, grid=(count // tile,), in_specs=[here, here, here] +...  3.95 us
    pallas_call x1, Pallas kernels, stage(): pl.pallas_call(body, in_specs=[in_hbm()] * 3, out_specs=[in_vmem()] * 2,...  3.33 us
    pallas_call x1, Pallas kernels, decode_join(): pl.pallas_call(body, grid_spec=pltpu.PrefetchScalarGridSpec(num_scalar_pr...  2.43 us
    pallas_call x1, Pallas kernels, decode_partials(): pl.pallas_call(body, in_specs=[smem()] + [in_vmem()] * (devices + 1), out...  2.21 us
    pallas_call x1, Pallas kernels, pack_history(): pl.pallas_call(body, grid_spec=pltpu.PrefetchScalarGridSpec(num_scalar_pr...  1.73 us
  transfers between devices with their start and end apart: 14, of which 3 were waited for; matrix products, arithmetic and copies ran while one was open for 2% of the time, Pallas kernels for 42%

profile of v1, /device:TPU:0, one launch (start us, length us, event | category | flops | bytes accessed | tf_op | source)
XLA Modules:
  0.0 69.1 jit_solution(15096036206229802202)
XLA Ops:
  1.3 0.7 %pad_add_fusion.m = s32[18]{0:T(128)S(1)} fusion(s32[16]{0:T(128)} %param.17, s32[1]{0:T(128)S(6)} %copy.21, s32[1]{0:T(128)} %bitcast), kind=kLoop, calls=%fused_computation.2 | loop fusion | flops 36 | bytes 144 | tf_op jit(solution)/shard_map/concatenate | solution.py:403
  2.0 1.7 %pack_history.1 = (bf16[640,128]{1,0:T(8,128)(2,1)S(1)}, bf16[640,128]{1,0:T(8,128)(2,1)S(1)}, bf16[640,128]{1,0:T(8,128)(2,1)S(1)}, bf16[640,128]{1,0:T(8,128)(2,1)S(1)}) custom-call(s32[18]{0:T(128)S(1)} %pad_add_fusion.m, bf16[2,256,512]{2,1,0:T(8,128)(2,1)} %refs_3_.2, bf16[2,256,512]{2,1,0:T(8,128)(2,1)} %refs_3_.2, bf16[2,256,512]{2,1,0:T(8,128)(2,1)} %refs_3_.2, ...), custom_call_target="tpu_custom_call" | custom-call | tf_op jit(solution)/shard_map/pack_history/pallas_call | solution.py:67
  3.7 0.6 collective-permute-start
  4.3 2.6 %collective-permute-start.1 = (bf16[640,128]{1,0:T(8,128)(2,1)S(1)}, bf16[640,128]{1,0:T(8,128)(2,1)S(1)}, u32[]{:S(2)}, u32[]{:S(2)}) collective-permute-start(bf16[640,128]{1,0:T(8,128)(2,1)S(1)} %get-tuple-element.27), channel_id=1, source_target_pairs={{0,2},{1,3},{2,0},{3,1},{4,6},{5,7},{6,4},{7,5},{8,10},{9,11},{10,... | collective-permute-start | bytes 491528 | tf_op jit(solution)/shard_map/ppermute | solution.py:406
  6.9 0.0 collective-permute-start.2
  6.9 1.0 %copy.15.refs_0_.refs_1_.refs_2_.refs_3_ = bf16[2,124,512]{2,1,0:T(8,128)(2,1)S(1)} copy(bf16[2,124,512]{2,0,1:T(2,128)(2,1)} %param.12) | data formatting | bytes 507904 | tf_op args[1]
  7.9 0.0 slice-start
  7.9 0.6 pack_fresh.1
  8.6 0.2 collective-permute-start.3
  8.8 1.9 %collective-permute-start.4 = (bf16[256,128]{1,0:T(8,128)(2,1)S(1)}, bf16[256,128]{1,0:T(8,128)(2,1)S(1)}, u32[]{:S(2)}, u32[]{:S(2)}) collective-permute-start(bf16[256,128]{1,0:T(8,128)(2,1)S(1)} %get-tuple-element.31), channel_id=1, source_target_pairs={{0,2},{1,3},{2,0},{3,1},{4,6},{5,7},{6,4},{7,5},{8,10},{9,11},{10,... | collective-permute-start | bytes 196616 | tf_op jit(solution)/shard_map/ppermute | solution.py:406
  10.7 3.3 %stage.1 = (bf16[2,16,192,512]{3,2,1,0:T(8,128)(2,1)S(1)}, bf16[512,1024]{1,0:T(8,128)(2,1)S(1)}) custom-call(bf16[2,16,192,512]{3,2,1,0:T(8,128)(2,1)} %cache_hbm.1, bf16[496,1024]{1,0:T(8,128)(2,1)} %q_hbm.1, bf16[16,1024]{1,0:T(8,128)(2,1)} %refs_4_.1), custom_call_target="tpu_custom_call" | custom-call | tf_op jit(solution)/shard_map/stage/pallas_call | solution.py:133
  14.1 0.9 %collective-permute-done.2.refs_3_ = bf16[640,128]{1,0:T(8,128)(2,1)S(1)} collective-permute-done((bf16[640,128]{1,0:T(8,128)(2,1)S(1)}, bf16[640,128]{1,0:T(8,128)(2,1)S(1)}, u32[]{:S(2)}, u32[]{:S(2)}) %collective-permute-start.2) | collective-permute-done | bytes 163872 | tf_op jit(solution)/shard_map/ppermute | solution.py:406
  15.0 2.2 %decode.1 = (f32[136,128]{1,0:T(8,128)S(1)}, f32[136,128]{1,0:T(8,128)S(1)}, f32[136,128]{1,0:T(8,128)S(1)}, f32[136,128]{1,0:T(8,128)S(1)}) custom-call(s32[18]{0:T(128)S(1)} %pad_add_fusion.m, bf16[640,128]{1,0:T(8,128)(2,1)S(1)} %get-tuple-element.25.refs_0_.refs_4_, bf16[640,128]{1,0:T(8,128)(2,1)S(1)} %collective-permute-done.refs_1_, ...), custom_call_target="tpu_custom_call" | custom-call | tf_op jit(solution)/shard_map/decode/pallas_call | solution.py:199
  17.2 0.3 collective-permute-start.6
  17.5 2.0 %collective-permute-start.7 = (f32[136,128]{1,0:T(8,128)S(1)}, f32[136,128]{1,0:T(8,128)S(1)}, u32[]{:S(2)}, u32[]{:S(2)}) collective-permute-start(f32[136,128]{1,0:T(8,128)S(1)} %get-tuple-element.36), channel_id=1, source_target_pairs={{0,2},{1,3},{2,0},{3,1},{4,6},{5,7},{6,4},{7,5},{8,10},{9,11},{10,... | collective-permute-start | bytes 208904 | tf_op jit(solution)/shard_map/ppermute | solution.py:406
  19.6 4.6 %shard_map.124 = (bf16[64,4096]{1,0:T(8,128)(2,1)S(1)}, bf16[64,4096]{1,0:T(8,128)(2,1)S(1)}) custom-call(s32[18]{0:T(128)S(1)} %pad_add_fusion.m, bf16[512,1024]{1,0:T(8,128)(2,1)S(1)} %get-tuple-element.24.q, bf16[640,128]{1,0:T(8,128)(2,1)S(1)} %get-tuple-element.25.refs_0_.refs_4_, bf16[640,128]{1,0:T(8,128)(2,1)S(1)} %collective-permute-done.refs_1_, ...), custom_call_target="tpu_custom_call" | custom-call | flops 1879048192 | bytes 8388608 | tf_op jit(solution)/shard_map/pallas_call | solution.py:333
  24.3 0.2 collective-permute-start.12
  24.4 2.4 %join.1.refs_8_ = bf16[16,1024]{1,0:T(8,128)(2,1)S(1)} custom-call(s32[18]{0:T(128)S(1)} %pad_add_fusion.m, f32[136,128]{1,0:T(8,128)S(1)} %get-tuple-element.34.refs_0_, f32[136,128]{1,0:T(8,128)S(1)} %collective-permute-done.6.refs_1_, f32[136,128]{1,0:T(8,128)S(1)} %collective-permute-done.7.refs_2_, f32[136,128]{1,0:T(8,128)S(1)} %collective-permute-done.8.refs_3_, ...), custom_call_target="tpu_custom_call" | custom-call | tf_op jit(solution)/shard_map/join/pallas_call | solution.py:243
  26.9 5.3 %shard_map.123 = (bf16[64,4096]{1,0:T(8,128)(2,1)S(1)}, bf16[64,4096]{1,0:T(8,128)(2,1)S(1)}) custom-call(s32[18]{0:T(128)S(1)} %pad_add_fusion.m, bf16[512,1024]{1,0:T(8,128)(2,1)S(1)} %get-tuple-element.24.q, bf16[640,128]{1,0:T(8,128)(2,1)S(1)} %get-tuple-element.25.refs_0_.refs_4_, bf16[640,128]{1,0:T(8,128)(2,1)S(1)} %collective-permute-done.refs_1_, ...), custom_call_target="tpu_custom_call" | custom-call | flops 1879048192 | bytes 8388608 | tf_op jit(solution)/shard_map/pallas_call | solution.py:333
  32.1 0.0 copy-start
  32.2 0.0 copy-start.1
  32.2 0.5 collective-permute-start.10
  32.6 8.7 %shard_map.122 = (bf16[128,4096]{1,0:T(8,128)(2,1)S(1)}, bf16[128,4096]{1,0:T(8,128)(2,1)S(1)}) custom-call(s32[18]{0:T(128)S(1)} %pad_add_fusion.m, bf16[512,1024]{1,0:T(8,128)(2,1)S(1)} %get-tuple-element.24.q, bf16[640,128]{1,0:T(8,128)(2,1)S(1)} %get-tuple-element.25.refs_0_.refs_4_, bf16[640,128]{1,0:T(8,128)(2,1)S(1)} %collective-permute-done.refs_1_, ...), custom_call_target="tpu_custom_call" | custom-call | flops 3758096384 | bytes 8388608 | tf_op jit(solution)/shard_map/pallas_call | solution.py:333
  41.3 0.2 collective-permute-start.9
  41.5 0.1 add_convert_fusion
  41.6 2.1 %collective-permute-start.13 = (bf16[64,4096]{1,0:T(8,128)(2,1)S(1)}, bf16[64,4096]{1,0:T(8,128)(2,1)S(1)}, u32[]{:S(2)}, u32[]{:S(2)}) collective-permute-start(bf16[64,4096]{1,0:T(8,128)(2,1)S(1)} %add_convert_fusion), channel_id=1, source_target_pairs={{0,2},{1,3},{2,0},{3,1},{4,6},{5,7},{6,4},{7,5},{8,10},{9,11},{10,... | collective-permute-start | bytes 1572872 | tf_op jit(solution)/shard_map/ppermute | solution.py:406
  43.7 0.1 add_convert_fusion.1
  43.9 0.1 collective-permute-start.11
  44.0 12.6 %collective-permute-done.13.refs_0_ = bf16[64,4096]{1,0:T(8,128)(2,1)S(1)} collective-permute-done((bf16[64,4096]{1,0:T(8,128)(2,1)S(1)}, bf16[64,4096]{1,0:T(8,128)(2,1)S(1)}, u32[]{:S(2)}, u32[]{:S(2)}) %collective-permute-start.13) | collective-permute-done | bytes 524320 | tf_op jit(solution)/shard_map/ppermute | solution.py:406
  56.5 2.0 %shard_map.125 = (bf16[128,4096]{1,0:T(8,128)(2,1)}, bf16[128,4096]{1,0:T(8,128)(2,1)}) custom-call(bf16[128,4096]{1,0:T(8,128)(2,1)S(1)} %copy-done, bf16[128,4096]{1,0:T(8,128)(2,1)S(1)} %get-tuple-element.38.own_ref, bf16[128,4096]{1,0:T(8,128)(2,1)S(1)} %collective-permute-done.9.given_ref, bf16[64,4096]{1,0:T(8,128)(2,1)S(1)} %collective-permute-done.13.refs_0_, ...), custom_call_target="tpu_custom_call" | custom-call | tf_op jit(solution)/shard_map/pallas_call | solution.py:368
  58.5 8.7 %collective-permute-done.11.refs_0_ = bf16[64,4096]{1,0:T(8,128)(2,1)S(1)} collective-permute-done((bf16[64,4096]{1,0:T(8,128)(2,1)S(1)}, bf16[64,4096]{1,0:T(8,128)(2,1)S(1)}, u32[]{:S(2)}, u32[]{:S(2)}) %collective-permute-start.11) | collective-permute-done | bytes 524320 | tf_op jit(solution)/shard_map/ppermute | solution.py:406
  67.2 2.0 %shard_map.126 = (bf16[128,4096]{1,0:T(8,128)(2,1)}, bf16[128,4096]{1,0:T(8,128)(2,1)}) custom-call(bf16[128,4096]{1,0:T(8,128)(2,1)S(1)} %copy-done, bf16[128,4096]{1,0:T(8,128)(2,1)S(1)} %get-tuple-element.38.own_ref, bf16[128,4096]{1,0:T(8,128)(2,1)S(1)} %collective-permute-done.9.given_ref, ...), custom_call_target="tpu_custom_call", output_to_operand_aliasing={{0}: (5, {}), {1}: (6, {})} | custom-call | tf_op jit(solution)/shard_map/pallas_call | solution.py:368
  (19 shorter events, 0.0 us)
Async XLA Ops:
  3.7 7.0 %collective-permute-start = (bf16[640,128]{1,0:T(8,128)(2,1)S(1)}, bf16[640,128]{1,0:T(8,128)(2,1)S(1)}, u32[]{:S(2)}, u32[]{:S(2)}) collective-permute-start(bf16[640,128]{1,0:T(8,128)(2,1)S(1)} %get-tuple-element.26), channel_id=1, source_target_pairs={{0,1},{1,0},{2,3},{3,2},{4,5},{5,4},{6,7},{7,6},{8,9},{9,8},{10,11... | collective-permute-start | bytes 491528 | tf_op jit(solution)/shard_map/ppermute | solution.py:406
  4.3 9.8 %collective-permute-start.1 = (bf16[640,128]{1,0:T(8,128)(2,1)S(1)}, bf16[640,128]{1,0:T(8,128)(2,1)S(1)}, u32[]{:S(2)}, u32[]{:S(2)}) collective-permute-start(bf16[640,128]{1,0:T(8,128)(2,1)S(1)} %get-tuple-element.27), channel_id=1, source_target_pairs={{0,2},{1,3},{2,0},{3,1},{4,6},{5,7},{6,4},{7,5},{8,10},{9,11},{10,... | collective-permute-start | bytes 491528 | tf_op jit(solution)/shard_map/ppermute | solution.py:406
  6.9 8.1 %collective-permute-start.2 = (bf16[640,128]{1,0:T(8,128)(2,1)S(1)}, bf16[640,128]{1,0:T(8,128)(2,1)S(1)}, u32[]{:S(2)}, u32[]{:S(2)}) collective-permute-start(bf16[640,128]{1,0:T(8,128)(2,1)S(1)} %get-tuple-element.28), channel_id=1, source_target_pairs={{0,3},{1,2},{2,1},{3,0},{4,7},{5,6},{6,5},{7,4},{8,11},{9,10},{10,... | collective-permute-start | bytes 491528 | tf_op jit(solution)/shard_map/ppermute | solution.py:406
  7.9 11.7 %slice-start = ((s8[8388608]{0:T(1024)(128)(4,1)}), s8[4194304]{0:T(1024)(128)(4,1)S(1)}, s32[]{:S(2)}) async-start(s8[8388608]{0:T(1024)(128)(4,1)} %bitcast.2), calls=%async_computation | async-start | bytes 8388608
  8.6 11.0 %collective-permute-start.3 = (bf16[256,128]{1,0:T(8,128)(2,1)S(1)}, bf16[256,128]{1,0:T(8,128)(2,1)S(1)}, u32[]{:S(2)}, u32[]{:S(2)}) collective-permute-start(bf16[256,128]{1,0:T(8,128)(2,1)S(1)} %get-tuple-element.30), channel_id=1, source_target_pairs={{0,1},{1,0},{2,3},{3,2},{4,5},{5,4},{6,7},{7,6},{8,9},{9,8},{10,11... | collective-permute-start | bytes 196616 | tf_op jit(solution)/shard_map/ppermute | solution.py:406
  8.8 10.8 %collective-permute-start.4 = (bf16[256,128]{1,0:T(8,128)(2,1)S(1)}, bf16[256,128]{1,0:T(8,128)(2,1)S(1)}, u32[]{:S(2)}, u32[]{:S(2)}) collective-permute-start(bf16[256,128]{1,0:T(8,128)(2,1)S(1)} %get-tuple-element.31), channel_id=1, source_target_pairs={{0,2},{1,3},{2,0},{3,1},{4,6},{5,7},{6,4},{7,5},{8,10},{9,11},{10,... | collective-permute-start | bytes 196616 | tf_op jit(solution)/shard_map/ppermute | solution.py:406
  10.7 8.9 %slice-start.1 = ((s8[8388608]{0:T(1024)(128)(4,1)}), s8[4194304]{0:T(1024)(128)(4,1)S(1)}, s32[]{:S(2)}) async-start(s8[8388608]{0:T(1024)(128)(4,1)} %bitcast.2), calls=%async_computation.1 | async-start | bytes 8388608
  10.7 8.8 %collective-permute-start.5 = (bf16[256,128]{1,0:T(8,128)(2,1)S(1)}, bf16[256,128]{1,0:T(8,128)(2,1)S(1)}, u32[]{:S(2)}, u32[]{:S(2)}) collective-permute-start(bf16[256,128]{1,0:T(8,128)(2,1)S(1)} %get-tuple-element.32), channel_id=1, source_target_pairs={{0,3},{1,2},{2,1},{3,0},{4,7},{5,6},{6,5},{7,4},{8,11},{9,10},{10,... | collective-permute-start | bytes 196616 | tf_op jit(solution)/shard_map/ppermute | solution.py:406
  17.2 7.2 %collective-permute-start.6 = (f32[136,128]{1,0:T(8,128)S(1)}, f32[136,128]{1,0:T(8,128)S(1)}, u32[]{:S(2)}, u32[]{:S(2)}) collective-permute-start(f32[136,128]{1,0:T(8,128)S(1)} %get-tuple-element.35), channel_id=1, source_target_pairs={{0,1},{1,0},{2,3},{3,2},{4,5},{5,4},{6,7},{7,6},{8,9},{9,8},{10,11... | collective-permute-start | bytes 208904 | tf_op jit(solution)/shard_map/ppermute | solution.py:406
  17.5 6.9 %collective-permute-start.7 = (f32[136,128]{1,0:T(8,128)S(1)}, f32[136,128]{1,0:T(8,128)S(1)}, u32[]{:S(2)}, u32[]{:S(2)}) collective-permute-start(f32[136,128]{1,0:T(8,128)S(1)} %get-tuple-element.36), channel_id=1, source_target_pairs={{0,2},{1,3},{2,0},{3,1},{4,6},{5,7},{6,4},{7,5},{8,10},{9,11},{10,... | collective-permute-start | bytes 208904 | tf_op jit(solution)/shard_map/ppermute | solution.py:406
  19.6 4.9 %collective-permute-start.8 = (f32[136,128]{1,0:T(8,128)S(1)}, f32[136,128]{1,0:T(8,128)S(1)}, u32[]{:S(2)}, u32[]{:S(2)}) collective-permute-start(f32[136,128]{1,0:T(8,128)S(1)} %get-tuple-element.37), channel_id=1, source_target_pairs={{0,3},{1,2},{2,1},{3,0},{4,7},{5,6},{6,5},{7,4},{8,11},{9,10},{10,... | collective-permute-start | bytes 208904 | tf_op jit(solution)/shard_map/ppermute | solution.py:406
  24.3 17.2 %collective-permute-start.12 = (bf16[64,4096]{1,0:T(8,128)(2,1)S(1)}, bf16[64,4096]{1,0:T(8,128)(2,1)S(1)}, u32[]{:S(2)}, u32[]{:S(2)}) collective-permute-start(bf16[64,4096]{1,0:T(8,128)(2,1)S(1)} %get-tuple-element.43), channel_id=1, source_target_pairs={{0,1},{1,0},{2,3},{3,2},{4,5},{5,4},{6,7},{7,6},{8,9},{9,8},{10,11... | collective-permute-start | bytes 1572872 | tf_op jit(solution)/shard_map/ppermute | solution.py:406
  32.1 24.4 %copy-start = (bf16[128,4096]{1,0:T(8,128)(2,1)S(1)}, bf16[128,4096]{1,0:T(8,128)(2,1)}, u32[]{:S(2)}) copy-start(bf16[128,4096]{1,0:T(8,128)(2,1)} %res_ref.3) | copy-start | bytes 3145732
  32.2 24.4 %copy-start.1 = (f32[4096]{0:T(1024)S(1)}, f32[4096]{0:T(1024)}, u32[]{:S(2)}) copy-start(f32[4096]{0:T(1024)} %param.21) | copy-start | bytes 49156
  32.2 11.6 %collective-permute-start.10 = (bf16[64,4096]{1,0:T(8,128)(2,1)S(1)}, bf16[64,4096]{1,0:T(8,128)(2,1)S(1)}, u32[]{:S(2)}, u32[]{:S(2)}) collective-permute-start(bf16[64,4096]{1,0:T(8,128)(2,1)S(1)} %get-tuple-element.41), channel_id=1, source_target_pairs={{0,1},{1,0},{2,3},{3,2},{4,5},{5,4},{6,7},{7,6},{8,9},{9,8},{10,11... | collective-permute-start | bytes 1572872 | tf_op jit(solution)/shard_map/ppermute | solution.py:406
  41.3 15.2 %collective-permute-start.9 = (bf16[128,4096]{1,0:T(8,128)(2,1)S(1)}, bf16[128,4096]{1,0:T(8,128)(2,1)S(1)}, u32[]{:S(2)}, u32[]{:S(2)}) collective-permute-start(bf16[128,4096]{1,0:T(8,128)(2,1)S(1)} %get-tuple-element.39), channel_id=1, source_target_pairs={{0,1},{1,0},{2,3},{3,2},{4,5},{5,4},{6,7},{7,6},{8,9},{9,8},{10,11... | collective-permute-start | bytes 3145736 | tf_op jit(solution)/shard_map/ppermute | solution.py:406
  41.6 14.9 %collective-permute-start.13 = (bf16[64,4096]{1,0:T(8,128)(2,1)S(1)}, bf16[64,4096]{1,0:T(8,128)(2,1)S(1)}, u32[]{:S(2)}, u32[]{:S(2)}) collective-permute-start(bf16[64,4096]{1,0:T(8,128)(2,1)S(1)} %add_convert_fusion), channel_id=1, source_target_pairs={{0,2},{1,3},{2,0},{3,1},{4,6},{5,7},{6,4},{7,5},{8,10},{9,11},{10,... | collective-permute-start | bytes 1572872 | tf_op jit(solution)/shard_map/ppermute | solution.py:406
  43.9 23.3 %collective-permute-start.11 = (bf16[64,4096]{1,0:T(8,128)(2,1)S(1)}, bf16[64,4096]{1,0:T(8,128)(2,1)S(1)}, u32[]{:S(2)}, u32[]{:S(2)}) collective-permute-start(bf16[64,4096]{1,0:T(8,128)(2,1)S(1)} %add_convert_fusion.1), channel_id=1, source_target_pairs={{0,2},{1,3},{2,0},{3,1},{4,6},{5,7},{6,4},{7,5},{8,10},{9,11},{10,... | collective-permute-start | bytes 1572872 | tf_op jit(solution)/shard_map/ppermute | solution.py:406

commit v2 on v1

--- a/solution.py
+++ b/solution.py
@@ -42,41 +42,57 @@
     return pltpu.with_memory_space_constraint(value, pltpu.HBM)
 
 
+def busy(us):
+    return pl.CostEstimate(flops=us * 500_000_000, transcendentals=0, bytes_accessed=us * 1_000_000)
+
+
 def params(mib, **kwargs):
     return pltpu.CompilerParams(vmem_limit_bytes=mib << 20, **kwargs)
 
 
-def pack_history(history, queries, meta, devices, local_heads, group):
+def pack_history(history, queries, devices, local_heads, group):
     h_rows = history.shape[1]
     rows = queries.shape[0]
-    span = 2 * h_rows + rows * local_heads
-
-    def head_of(k):
-        return lambda i, m: (0, 0, (m[0] ^ k) * local_heads // group)
-
-    def body(m, *refs):
-        q_ref = refs[devices]
+
+    def body(h_hbm, q_hbm, *refs):
+        o_refs, q_ref, sem = refs[:devices], refs[devices], refs[devices + 1]
+        me = lax.axis_index("tp")
+        copies = []
         for k in range(devices):
-            h_ref, o_ref = refs[k], refs[devices + 1 + k]
+            lane = pl.multiple_of((me ^ k) * local_heads // group * HEAD_DIM, HEAD_DIM)
             for part in range(2):
-                o_ref[part * h_rows : (part + 1) * h_rows, :] = h_ref[part]
-            for h in range(local_heads):
-                row = 2 * h_rows + h * rows
-                o_ref[row : row + rows, :] = q_ref[:, h * HEAD_DIM : (h + 1) * HEAD_DIM]
-
-    return pl.pallas_call(
-        body,
-        grid_spec=pltpu.PrefetchScalarGridSpec(
-            num_scalar_prefetch=1,
-            grid=(1,),
-            in_specs=[pl.BlockSpec((2, h_rows, HEAD_DIM), head_of(k)) for k in range(devices)]
-            + [pl.BlockSpec(queries.shape, lambda i, m: (0, 0))],
-            out_specs=[pl.BlockSpec((span, HEAD_DIM), lambda i, m: (0, 0))] * devices,
-        ),
-        out_shape=[jax.ShapeDtypeStruct((span, HEAD_DIM), BF16)] * devices,
-        compiler_params=params(8),
+                copies.append(
+                    pltpu.make_async_copy(
+                        h_hbm.at[part, :, pl.ds(lane, HEAD_DIM)],
+                        o_refs[k].at[part * h_rows : (part + 1) * h_rows, :],
+                        sem.at[len(copies)],
+                    )
+                )
+        for h in range(local_heads):
+            copies.append(
+                pltpu.make_async_copy(
+                    q_hbm.at[:, h * HEAD_DIM : (h + 1) * HEAD_DIM],
+                    q_ref.at[h * rows : (h + 1) * rows, :],
+                    sem.at[len(copies)],
+                )
+            )
+        for copy in copies:
+            copy.start()
+        for copy in copies:
+            copy.wait()
+
+    outs = pl.pallas_call(
+        body,
+        in_specs=[in_hbm()] * 2,
+        out_specs=[in_vmem()] * (devices + 1),
+        out_shape=[jax.ShapeDtypeStruct((2 * h_rows, HEAD_DIM), BF16)] * devices
+        + [jax.ShapeDtypeStruct((rows * local_heads, HEAD_DIM), BF16)],
+        scratch_shapes=[pltpu.SemaphoreType.DMA((2 * devices + local_heads,))],
+        compiler_params=params(2),
+        cost_estimate=busy(6),
         name="pack_history",
-    )(meta, *([to_hbm(history)] * devices), to_hbm(queries))
+    )(to_hbm(history), to_hbm(queries))
+    return outs[:devices], outs[devices]
 
 
 def pack_fresh(prompt, meta, devices, local_heads, group):
@@ -108,23 +124,21 @@
         ),
         out_shape=[jax.ShapeDtypeStruct((2 * p_pad, HEAD_DIM), BF16)] * devices,
         compiler_params=params(8),
+        cost_estimate=busy(6),
         name="pack_fresh",
     )(meta, *([prompt] * devices))
 
 
-def stage(cache, prompt_queries, decode_queries):
+def stage(prompt_queries, decode_queries, entries, local_heads, group):
     prompt_rows, decode_rows = prompt_queries.shape[0], decode_queries.shape[0]
-    parts = 4
-    per = cache.shape[1] // parts
-
-    def body(cache_hbm, q_hbm, dq_hbm, cache_ref, q_ref, sem):
+
+    def body(q_hbm, dq_hbm, e_hbm, q_ref, e_ref, sem):
+        lane = pl.multiple_of(lax.axis_index("tp") * local_heads // group * HEAD_DIM, HEAD_DIM)
         copies = [
             pltpu.make_async_copy(q_hbm, q_ref.at[0:prompt_rows, :], sem.at[0]),
             pltpu.make_async_copy(dq_hbm, q_ref.at[prompt_rows : prompt_rows + decode_rows, :], sem.at[1]),
+            pltpu.make_async_copy(e_hbm.at[:, :, pl.ds(lane, HEAD_DIM)], e_ref, sem.at[2]),
         ]
-        for i in range(2 * parts):
-            here = (i // parts, slice(i % parts * per, (i % parts + 1) * per))
-            copies.append(pltpu.make_async_copy(cache_hbm.at[here], cache_ref.at[here], sem.at[2 + i]))
         for copy in copies:
             copy.start()
         for copy in copies:
@@ -135,17 +149,26 @@
         in_specs=[in_hbm()] * 3,
         out_specs=[in_vmem()] * 2,
         out_shape=[
-            pltpu.VMEM(cache.shape, BF16),
             pltpu.VMEM((prompt_rows + decode_rows, prompt_queries.shape[1]), BF16),
+            pltpu.VMEM((2, decode_rows, HEAD_DIM), BF16),
         ],
-        scratch_shapes=[pltpu.SemaphoreType.DMA((2 + 2 * parts,))],
+        scratch_shapes=[pltpu.SemaphoreType.DMA((3,))],
         compiler_params=params(2),
+        cost_estimate=busy(6),
         name="stage",
-    )(to_hbm(cache), to_hbm(prompt_queries), to_hbm(decode_queries))
-
-
-def decode_partials(history, cache, meta, h_rows, local_heads, group):
-    devices = len(history)
+    )(to_hbm(prompt_queries), to_hbm(decode_queries), to_hbm(entries))
+
+
+def split(value):
+    terms = []
+    for _ in range(3):
+        terms.append(value.astype(BF16))
+        value = value - terms[-1].astype(F32)
+    return terms
+
+
+def decode_partials(queries, cache, meta, local_heads, group):
+    devices = len(queries)
     rows, span, width = cache.shape[1], cache.shape[2], cache.shape[3]
     kv_heads = width // HEAD_DIM
     heads = devices * local_heads
@@ -154,14 +177,13 @@
     stat_rows = round_up(local_heads, 8)
 
     def body(m, *refs):
-        h_refs, cache_ref = refs[:devices], refs[devices]
+        q_refs, cache_ref = refs[:devices], refs[devices]
         o_refs = refs[devices + 1 : 2 * devices + 1]
-        q_all = refs[2 * devices + 1]
+        q_all, sums = refs[2 * devices + 1 :]
         me = m[0]
         for k in range(devices):
             for h in range(local_heads):
-                row = 2 * h_rows + h * rows
-                q_all[k, pl.ds(h, rows, stride=local_heads), :] = h_refs[k][row : row + rows, :].astype(F32)
+                q_all[k, pl.ds(h, rows, stride=local_heads), :] = q_refs[k][h * rows : (h + 1) * rows, :].astype(F32)
 
         slot = lax.broadcasted_iota(jnp.int32, (heads, 1), 0) // local_heads
         reads = ((slot ^ me) * local_heads) // group
@@ -191,36 +213,46 @@
             for g in range(kv_heads):
                 own = own + jnp.where(reads == g, summed[:, g * HEAD_DIM : (g + 1) * HEAD_DIM], 0.0)
             for k in range(devices):
-                o_refs[k][b * local_heads : (b + 1) * local_heads, :] = own[k * local_heads : (k + 1) * local_heads]
+                sums[k, b * local_heads : (b + 1) * local_heads, :] = own[k * local_heads : (k + 1) * local_heads]
             stats = jnp.where(lane == b, top[these], jnp.where(lane == rows + b, total[these], stats))
+        terms = split(stats)
         for k in range(devices):
-            o_refs[k][part_rows : part_rows + local_heads, :] = stats[k * local_heads : (k + 1) * local_heads, :]
+            o_refs[k][0:part_rows, :] = sums[k].astype(BF16)
+            for i, term in enumerate(terms):
+                row = part_rows + i * stat_rows
+                o_refs[k][row : row + local_heads, :] = term[k * local_heads : (k + 1) * local_heads, :]
 
     return pl.pallas_call(
         body,
         in_specs=[smem()] + [in_vmem()] * (devices + 1),
         out_specs=[in_vmem()] * devices,
-        scratch_shapes=[pltpu.VMEM((devices, part_rows, HEAD_DIM), F32)],
-        out_shape=[jax.ShapeDtypeStruct((part_rows + stat_rows, HEAD_DIM), F32)] * devices,
-        compiler_params=params(16),
+        scratch_shapes=[pltpu.VMEM((devices, part_rows, HEAD_DIM), F32)] * 2,
+        out_shape=[jax.ShapeDtypeStruct((part_rows + 3 * stat_rows, HEAD_DIM), BF16)] * devices,
+        compiler_params=params(12),
+        cost_estimate=busy(6),
         name="decode",
-    )(meta, *history, cache)
-
-
-def decode_join(parts, history, entries, meta, h_rows, local_heads, group):
+    )(meta, *queries, cache)
+
+
+def decode_join(parts, queries, entries, local_heads):
     devices = len(parts)
     rows = entries.shape[1]
     factor = HEAD_DIM ** (-0.5) * float(np.log2(np.e))
     part_rows = rows * local_heads
-
-    def body(m, *refs):
+    stat_rows = round_up(local_heads, 8)
+
+    def body(*refs):
         p_refs = refs[:devices]
-        h_ref, e_ref, o_ref, q_all, out = refs[devices:]
+        q_ref, e_ref, o_ref, q_all, out = refs[devices:]
         for h in range(local_heads):
-            row = 2 * h_rows + h * rows
-            q_all[pl.ds(h, rows, stride=local_heads), :] = h_ref[row : row + rows, :].astype(F32)
-        stats = [p[part_rows : part_rows + local_heads, :] for p in p_refs]
+            q_all[pl.ds(h, rows, stride=local_heads), :] = q_ref[h * rows : (h + 1) * rows, :].astype(F32)
+        stats = []
+        for p in p_refs:
+            starts = [part_rows + i * stat_rows for i in range(3)]
+            high, middle, low = [p[row : row + local_heads, :].astype(F32) for row in starts]
+            stats.append(high + middle + low)
         keys, values = e_ref[0].astype(F32), e_ref[1].astype(F32)
+        sums = [p[0:part_rows, :].astype(F32) for p in p_refs]
         for b in range(rows):
             here = slice(b * local_heads, (b + 1) * local_heads)
             own = jnp.sum(q_all[here, :] * keys[b : b + 1, :], axis=-1, keepdims=True)
@@ -231,7 +263,7 @@
             weight = jnp.exp2((own - top) * factor)
             total = weight
             summed = weight.astype(BF16).astype(F32) * values[b : b + 1, :]
-            for s, t, p in zip(stats, tops, p_refs):
+            for s, t, p in zip(stats, tops, sums):
                 share = jnp.exp2((t - top) * factor)
                 total = total + share * s[:, rows + b : rows + b + 1]
                 summed = summed + share * p[here, :]
@@ -239,24 +271,16 @@
         for h in range(local_heads):
             o_ref[:, h * HEAD_DIM : (h + 1) * HEAD_DIM] = out[pl.ds(h, rows, stride=local_heads), :].astype(BF16)
 
-    full = lambda i, m: (0, 0)
-    return pl.pallas_call(
-        body,
-        grid_spec=pltpu.PrefetchScalarGridSpec(
-            num_scalar_prefetch=1,
-            grid=(1,),
-            in_specs=[pl.BlockSpec(parts[0].shape, full)] * devices
-            + [
-                pl.BlockSpec(history.shape, full),
-                pl.BlockSpec((2, rows, HEAD_DIM), lambda i, m: (0, 0, m[0] * local_heads // group)),
-            ],
-            out_specs=pl.BlockSpec((rows, local_heads * HEAD_DIM), full),
-            scratch_shapes=[pltpu.VMEM((part_rows, HEAD_DIM), F32)] * 2,
-        ),
+    return pl.pallas_call(
+        body,
+        in_specs=[in_vmem()] * (devices + 2),
+        out_specs=in_vmem(),
+        scratch_shapes=[pltpu.VMEM((part_rows, HEAD_DIM), F32)] * 2,
         out_shape=jax.ShapeDtypeStruct((rows, local_heads * HEAD_DIM), BF16),
-        compiler_params=params(8),
+        compiler_params=params(4),
+        cost_estimate=busy(1),
         name="join",
-    )(meta, *parts, history, to_hbm(entries))
+    )(*parts, queries, entries)
 
 
 def attend(slots, first, count, block, queries, history, fresh, decoded, weight, meta, h_rows, p_rows):
@@ -354,28 +378,33 @@
     def body(res_ref, own_ref, given_ref, *refs):
         cross = refs[:n_cross]
         gain_ref = refs[n_cross]
-        hidden_ref, normed_ref = refs[-2:]
-        hidden = res_ref[...].astype(F32) + own_ref[...].astype(F32) + given_ref[...].astype(F32)
-        for c in cross:
-            hidden = hidden + c[...].astype(F32)
-        mean = jnp.mean(hidden * hidden, axis=-1, keepdims=True)
-        hidden_ref[...] = hidden.astype(BF16)
-        normed_ref[...] = (hidden * lax.rsqrt(mean + EPS) * gain_ref[...]).astype(BF16)
-
-    here = pl.BlockSpec((tile, model), lambda i: (first // tile + i, 0))
-    local = pl.BlockSpec((tile, model), lambda i: (i, 0))
+        outs = refs[-5:-3]
+        staged, sem = refs[-3:-1], refs[-1]
+        copies = []
+        for i in range(0, count, tile):
+            here, local = slice(first + i, first + i + tile), slice(i, i + tile)
+            hidden = res_ref[here, :].astype(F32) + own_ref[here, :].astype(F32) + given_ref[here, :].astype(F32)
+            for c in cross:
+                hidden = hidden + c[local, :].astype(F32)
+            mean = jnp.mean(hidden * hidden, axis=-1, keepdims=True)
+            staged[0][local, :] = hidden.astype(BF16)
+            staged[1][local, :] = (hidden * lax.rsqrt(mean + EPS) * gain_ref[...]).astype(BF16)
+            for source, target in zip(staged, outs):
+                copies.append(pltpu.make_async_copy(source.at[local, :], target.at[here, :], sem.at[len(copies)]))
+                copies[-1].start()
+        for copy in copies:
+            copy.wait()
+
     n_in = 3 + n_cross + 1
     return pl.pallas_call(
         body,
-        grid=(count // tile,),
-        in_specs=[here, here, here]
-        + [local] * n_cross
-        + [pl.BlockSpec((1, model), lambda i: (0, 0))]
-        + [hbm()] * len(previous),
-        out_specs=[here, here],
+        in_specs=[in_vmem()] * n_in + [hbm()] * len(previous),
+        out_specs=[hbm()] * 2,
         out_shape=[jax.ShapeDtypeStruct((block, model), BF16)] * 2,
         input_output_aliases={n_in + i: i for i in range(len(previous))},
-        compiler_params=params(16),
+        scratch_shapes=[pltpu.VMEM((count, model), BF16)] * 2 + [pltpu.SemaphoreType.DMA((2 * count // tile,))],
+        compiler_params=params(8),
+        cost_estimate=busy(2),
     )(residual, own, given, *crossed, gain, *previous)
 
 
@@ -400,7 +429,6 @@
     h_rows, p_rows = history_cache.shape[1], prompt_entries.shape[1]
     assert group % local_heads == 0 and devices & (devices - 1) == 0
     assert block >= decode_queries.shape[0]
-    meta = jnp.concatenate([lax.axis_index("tp").astype(jnp.int32)[None], prompt_start, decode_lengths])
 
     def swap(value, k):
         return lax.ppermute(value, "tp", [(i, i ^ k) for i in range(devices)])
@@ -408,11 +436,19 @@
     def swapped(values):
         return [values[0]] + [swap(values[k], k) for k in range(1, devices)]
 
-    history = swapped(pack_history(history_cache, decode_queries, meta, devices, local_heads, group))
+    packed, own_query = pack_history(history_cache, decode_queries, devices, local_heads, group)
+    decode_rows = {0: own_query}
+    for k in range(2, devices, 2):
+        decode_rows[k] = swap(own_query, k)
+    for k in range(1, devices, 2):
+        decode_rows[k] = swap(decode_rows[k ^ 1], 1)
+    history = swapped(packed)
+    meta = jnp.concatenate([lax.axis_index("tp").astype(jnp.int32)[None], prompt_start, decode_lengths])
     fresh = swapped(pack_fresh(prompt_entries, meta, devices, local_heads, group))
-    cache, queries = stage(decode_cache, prompt_queries, decode_queries)
-    parts = swapped(decode_partials(history, cache, meta, h_rows, local_heads, group))
-    decoded = decode_join(parts, history[0], decode_entries, meta, h_rows, local_heads, group)
+    queries, entries = stage(prompt_queries, decode_queries, decode_entries, local_heads, group)
+    ordered = [decode_rows[k] for k in range(devices)]
+    parts = swapped(decode_partials(ordered, decode_cache, meta, local_heads, group))
+    decoded = decode_join(parts, own_query, entries, local_heads)
 
     def attended(slots, first, count, decoded):
         return attend(slots, first, count, block, queries, history, fresh, decoded, out_weight, meta, h_rows, p_rows)

time: 69.4 us -> 74.2 us (1.069)
  waiting for transfers between devices: 22.1 us -> 28.1 us
  Pallas kernels: 32.9 us -> 28.1 us
  starting transfers between devices: 10.7 us -> 13 us
  local copies, waits for them, and re-layouts: 1 us -> 2.84 us
    ppermute x14 -> x17, waiting for transfers between devices: 22.1 us -> 28.1 us  [swap(): return lax.ppermute(value, 'tp', [(i, i ^ k) for i in range(devices)])]
    pallas_call x4, Pallas kernels: 8.11 us -> 5.24 us  [the longest x2 2.76 us: finish(): pl.pallas_call(body, in_specs=[in_vmem()] * n_in + [hbm()] * len(previous...]
    ppermute x14 -> x17, starting transfers between devices: 10.7 us -> 13 us  [swap(): return lax.ppermute(value, 'tp', [(i, i ^ k) for i in range(devices)])]
    pallas_call x1, Pallas kernels: 3.33 us -> 1.4 us  [stage(): pl.pallas_call(body, in_specs=[in_hbm()] * 3, out_specs=[in_vmem()] * 2,...]
    unnamed x9 -> x15, local copies, waits for them, and re-layouts: 1 us -> 2.84 us
  transfers between devices with their start and end apart: 14 -> 17, of which waited for: 3 -> 5; matrix products, arithmetic and copies ran while one was open for 2% -> 0% of each run, Pallas kernels for 42% -> 28%
where the time goes in v2:
time: 74.2 us; the launch traced here: 74 us
  Pallas kernels  28.1 us (38%)
  waiting for transfers between devices  28.1 us (38%)
  starting transfers between devices  13 us (18%)
  local copies, waits for them, and re-layouts  2.84 us (4%)
  between operations  1.61 us (2%)
    ppermute x17, waiting for transfers between devices, swap(): return lax.ppermute(value, 'tp', [(i, i ^ k) for i in range(devices)])  28.1 us
    pallas_call x3, Pallas kernels, attend(): pl.pallas_call(body, in_specs=[smem()] + [in_vmem()] * n_vmem, out_specs=...  18.6 us
    ppermute x17, starting transfers between devices, swap(): return lax.ppermute(value, 'tp', [(i, i ^ k) for i in range(devices)])  13 us
    unnamed x15, local copies, waits for them, and re-layouts  2.84 us
    pallas_call x2, Pallas kernels, finish(): pl.pallas_call(body, in_specs=[in_vmem()] * n_in + [hbm()] * len(previous...  2.76 us
    pallas_call x1, Pallas kernels, decode_partials(): pl.pallas_call(body, in_specs=[smem()] + [in_vmem()] * (devices + 1), out...  2.27 us
  transfers between devices with their start and end apart: 17, of which 5 were waited for; matrix products, arithmetic and copies ran while one was open for 0% of the time, Pallas kernels for 28%

profile of v2, /device:TPU:0, one launch (start us, length us, event | category | flops | bytes accessed | tf_op | source)
XLA Modules:
  0.0 74.0 jit_solution(12215758910841504016)
XLA Ops:
  0.7 1.3 %pack_history.1 = (bf16[512,128]{1,0:T(8,128)(2,1)S(1)}, bf16[512,128]{1,0:T(8,128)(2,1)S(1)}, bf16[512,128]{1,0:T(8,128)(2,1)S(1)}, bf16[512,128]{1,0:T(8,128)(2,1)S(1)}, bf16[128,128]{1,0:T(8,128)(2,1)S(1)}) custom-call(bf16[2,256,512]{2,1,0:T(8,128)(2,1)} %h_hbm.1, bf16[16,1024]{1,0:T(8,128)(2,1)} %q_hbm.3), custom_call_target="tpu_custom_call" | custom-call | flops 3000000000 | bytes 6000000 | tf_op jit(solution)/shard_map/pack_history/pallas_call | solution.py:84
  2.0 3.1 %collective-permute-start.7 = (bf16[128,128]{1,0:T(8,128)(2,1)S(1)}, bf16[128,128]{1,0:T(8,128)(2,1)S(1)}, u32[]{:S(2)}, u32[]{:S(2)}) collective-permute-start(bf16[128,128]{1,0:T(8,128)(2,1)S(1)} %get-tuple-element.34.refs_0_.refs_4_), channel_id=1, source_target_pairs={{0,2},{1,3},{2,0},{3,1},{4,6},{5,7},{6,4},{7,5},{8,10},{9,11},{10,... | collective-permute-start | bytes 98312 | tf_op jit(solution)/shard_map/ppermute | solution.py:434
  5.7 0.1 pad_add_fusion.m
  5.8 1.1 %collective-permute-done.7.refs_2_ = bf16[128,128]{1,0:T(8,128)(2,1)S(1)} collective-permute-done((bf16[128,128]{1,0:T(8,128)(2,1)S(1)}, bf16[128,128]{1,0:T(8,128)(2,1)S(1)}, u32[]{:S(2)}, u32[]{:S(2)}) %collective-permute-start.7) | collective-permute-done | bytes 32800 | tf_op jit(solution)/shard_map/ppermute | solution.py:434
  6.9 0.6 pack_fresh.1
  7.6 0.6 collective-permute-start.3
  8.1 2.8 %copy-done.2 = bf16[2,16,192,512]{3,2,1,0:T(8,128)(2,1)S(1)} copy-done((bf16[2,16,192,512]{3,2,1,0:T(8,128)(2,1)S(1)}, bf16[2,16,192,512]{3,2,1,0:T(8,128)(2,1)}, u32[]{:S(2)}) %copy-start.2) | copy-done | bytes 6291480
  10.9 2.3 %decode.1 = (bf16[152,128]{1,0:T(8,128)(2,1)S(1)}, bf16[152,128]{1,0:T(8,128)(2,1)S(1)}, bf16[152,128]{1,0:T(8,128)(2,1)S(1)}, bf16[152,128]{1,0:T(8,128)(2,1)S(1)}) custom-call(s32[18]{0:T(128)S(1)} %pad_add_fusion.m, bf16[128,128]{1,0:T(8,128)(2,1)S(1)} %get-tuple-element.34.refs_0_.refs_4_, bf16[128,128]{1,0:T(8,128)(2,1)S(1)} %collective-permute-done.6.refs_1_, ...), custom_call_target="tpu_custom_call" | custom-call | flops 3000000000 | bytes 6000000 | tf_op jit(solution)/shard_map/decode/pallas_call | solution.py:225
  13.2 0.2 collective-permute-start.9
  13.4 2.0 %collective-permute-start.10 = (bf16[152,128]{1,0:T(8,128)(2,1)S(1)}, bf16[152,128]{1,0:T(8,128)(2,1)S(1)}, u32[]{:S(2)}, u32[]{:S(2)}) collective-permute-start(bf16[152,128]{1,0:T(8,128)(2,1)S(1)} %get-tuple-element.37), channel_id=1, source_target_pairs={{0,2},{1,3},{2,0},{3,1},{4,6},{5,7},{6,4},{7,5},{8,10},{9,11},{10,... | collective-permute-start | bytes 116744 | tf_op jit(solution)/shard_map/ppermute | solution.py:434
  15.4 1.7 %collective-permute-start.4 = (bf16[256,128]{1,0:T(8,128)(2,1)S(1)}, bf16[256,128]{1,0:T(8,128)(2,1)S(1)}, u32[]{:S(2)}, u32[]{:S(2)}) collective-permute-start(bf16[256,128]{1,0:T(8,128)(2,1)S(1)} %get-tuple-element.32), channel_id=1, source_target_pairs={{0,2},{1,3},{2,0},{3,1},{4,6},{5,7},{6,4},{7,5},{8,10},{9,11},{10,... | collective-permute-start | bytes 196616 | tf_op jit(solution)/shard_map/ppermute | solution.py:434
  17.1 0.0 collective-permute-start.5
  17.2 0.4 collective-permute-start
  17.6 2.1 %collective-permute-start.1 = (bf16[512,128]{1,0:T(8,128)(2,1)S(1)}, bf16[512,128]{1,0:T(8,128)(2,1)S(1)}, u32[]{:S(2)}, u32[]{:S(2)}) collective-permute-start(bf16[512,128]{1,0:T(8,128)(2,1)S(1)} %get-tuple-element.28), channel_id=1, source_target_pairs={{0,2},{1,3},{2,0},{3,1},{4,6},{5,7},{6,4},{7,5},{8,10},{9,11},{10,... | collective-permute-start | bytes 393224 | tf_op jit(solution)/shard_map/ppermute | solution.py:434
  19.6 1.4 %stage.1 = (bf16[512,1024]{1,0:T(8,128)(2,1)S(1)}, bf16[2,16,128]{2,1,0:T(8,128)(2,1)S(1)}) custom-call(bf16[496,1024]{1,0:T(8,128)(2,1)} %q_hbm.2, bf16[16,1024]{1,0:T(8,128)(2,1)} %q_hbm.3, bf16[2,16,512]{2,1,0:T(8,128)(2,1)} %e_hbm.1), custom_call_target="tpu_custom_call" | custom-call | flops 3000000000 | bytes 6000000 | tf_op jit(solution)/shard_map/stage/pallas_call | solution.py:147
  21.1 1.2 %join.1.refs_8_ = bf16[16,1024]{1,0:T(8,128)(2,1)S(1)} custom-call(bf16[152,128]{1,0:T(8,128)(2,1)S(1)} %get-tuple-element.35.refs_0_, bf16[152,128]{1,0:T(8,128)(2,1)S(1)} %collective-permute-done.9.refs_1_, bf16[152,128]{1,0:T(8,128)(2,1)S(1)} %collective-permute-done.10.refs_2_, bf16[152,128]{1,0:T(8,128)(2,1)S(1)} %collective-permute-done.11.refs_3_, ...), custom_call_target="tpu_custom_call" | custom-call | flops 500000000 | bytes 1000000 | tf_op jit(solution)/shard_map/join/pallas_call | solution.py:274
  22.3 2.9 %collective-permute-done.1.refs_2_ = bf16[512,128]{1,0:T(8,128)(2,1)S(1)} collective-permute-done((bf16[512,128]{1,0:T(8,128)(2,1)S(1)}, bf16[512,128]{1,0:T(8,128)(2,1)S(1)}, u32[]{:S(2)}, u32[]{:S(2)}) %collective-permute-start.1) | collective-permute-done | bytes 131104 | tf_op jit(solution)/shard_map/ppermute | solution.py:434
  25.1 2.3 %collective-permute-done.2.refs_3_ = bf16[512,128]{1,0:T(8,128)(2,1)S(1)} collective-permute-done((bf16[512,128]{1,0:T(8,128)(2,1)S(1)}, bf16[512,128]{1,0:T(8,128)(2,1)S(1)}, u32[]{:S(2)}, u32[]{:S(2)}) %collective-permute-start.2) | collective-permute-done | bytes 131104 | tf_op jit(solution)/shard_map/ppermute | solution.py:434
  27.4 4.6 %shard_map.124 = (bf16[64,4096]{1,0:T(8,128)(2,1)S(1)}, bf16[64,4096]{1,0:T(8,128)(2,1)S(1)}) custom-call(s32[18]{0:T(128)S(1)} %pad_add_fusion.m, bf16[512,1024]{1,0:T(8,128)(2,1)S(1)} %get-tuple-element.25.q, bf16[512,128]{1,0:T(8,128)(2,1)S(1)} %get-tuple-element.26.refs_0_, bf16[512,128]{1,0:T(8,128)(2,1)S(1)} %collective-permute-done.refs_1_, ...), custom_call_target="tpu_custom_call" | custom-call | flops 1879048192 | bytes 8388608 | tf_op jit(solution)/shard_map/pallas_call | solution.py:357
  32.0 0.2 collective-permute-start.15
  32.2 5.3 %shard_map.123 = (bf16[64,4096]{1,0:T(8,128)(2,1)S(1)}, bf16[64,4096]{1,0:T(8,128)(2,1)S(1)}) custom-call(s32[18]{0:T(128)S(1)} %pad_add_fusion.m, bf16[512,1024]{1,0:T(8,128)(2,1)S(1)} %get-tuple-element.25.q, bf16[512,128]{1,0:T(8,128)(2,1)S(1)} %get-tuple-element.26.refs_0_, bf16[512,128]{1,0:T(8,128)(2,1)S(1)} %collective-permute-done.refs_1_, ...), custom_call_target="tpu_custom_call" | custom-call | flops 1879048192 | bytes 8388608 | tf_op jit(solution)/shard_map/pallas_call | solution.py:357
  37.5 0.4 collective-permute-start.13
  37.9 8.7 %shard_map.122 = (bf16[128,4096]{1,0:T(8,128)(2,1)S(1)}, bf16[128,4096]{1,0:T(8,128)(2,1)S(1)}) custom-call(s32[18]{0:T(128)S(1)} %pad_add_fusion.m, bf16[512,1024]{1,0:T(8,128)(2,1)S(1)} %get-tuple-element.25.q, bf16[512,128]{1,0:T(8,128)(2,1)S(1)} %get-tuple-element.26.refs_0_, bf16[512,128]{1,0:T(8,128)(2,1)S(1)} %collective-permute-done.refs_1_, ...), custom_call_target="tpu_custom_call" | custom-call | flops 3758096384 | bytes 8388608 | tf_op jit(solution)/shard_map/pallas_call | solution.py:357
  46.6 0.2 collective-permute-start.12
  46.8 0.1 add_convert_fusion
  47.0 1.0 %collective-permute-start.16 = (bf16[64,4096]{1,0:T(8,128)(2,1)S(1)}, bf16[64,4096]{1,0:T(8,128)(2,1)S(1)}, u32[]{:S(2)}, u32[]{:S(2)}) collective-permute-start(bf16[64,4096]{1,0:T(8,128)(2,1)S(1)} %add_convert_fusion), channel_id=1, source_target_pairs={{0,2},{1,3},{2,0},{3,1},{4,6},{5,7},{6,4},{7,5},{8,10},{9,11},{10,... | collective-permute-start | bytes 1572872 | tf_op jit(solution)/shard_map/ppermute | solution.py:434
  47.9 0.1 add_convert_fusion.1
  48.1 1.2 %collective-permute-start.14 = (bf16[64,4096]{1,0:T(8,128)(2,1)S(1)}, bf16[64,4096]{1,0:T(8,128)(2,1)S(1)}, u32[]{:S(2)}, u32[]{:S(2)}) collective-permute-start(bf16[64,4096]{1,0:T(8,128)(2,1)S(1)} %add_convert_fusion.1), channel_id=1, source_target_pairs={{0,2},{1,3},{2,0},{3,1},{4,6},{5,7},{6,4},{7,5},{8,10},{9,11},{10,... | collective-permute-start | bytes 1572872 | tf_op jit(solution)/shard_map/ppermute | solution.py:434
  49.2 12.6 %collective-permute-done.16.refs_0_ = bf16[64,4096]{1,0:T(8,128)(2,1)S(1)} collective-permute-done((bf16[64,4096]{1,0:T(8,128)(2,1)S(1)}, bf16[64,4096]{1,0:T(8,128)(2,1)S(1)}, u32[]{:S(2)}, u32[]{:S(2)}) %collective-permute-start.16) | collective-permute-done | bytes 524320 | tf_op jit(solution)/shard_map/ppermute | solution.py:434
  61.8 1.4 %shard_map.125 = (bf16[128,4096]{1,0:T(8,128)(2,1)}, bf16[128,4096]{1,0:T(8,128)(2,1)}) custom-call(bf16[128,4096]{1,0:T(8,128)(2,1)S(1)} %copy-done, bf16[128,4096]{1,0:T(8,128)(2,1)S(1)} %get-tuple-element.40.own_ref, bf16[128,4096]{1,0:T(8,128)(2,1)S(1)} %collective-permute-done.12.given_ref, bf16[64,4096]{1,0:T(8,128)(2,1)S(1)} %collective-permute-done.16.refs_0_, ...), custom_call_target="tpu_custom_call" | custom-call | flops 1000000000 | bytes 2000000 | tf_op jit(solution)/shard_map/pallas_call | solution.py:399
  63.2 9.2 %collective-permute-done.14.refs_0_ = bf16[64,4096]{1,0:T(8,128)(2,1)S(1)} collective-permute-done((bf16[64,4096]{1,0:T(8,128)(2,1)S(1)}, bf16[64,4096]{1,0:T(8,128)(2,1)S(1)}, u32[]{:S(2)}, u32[]{:S(2)}) %collective-permute-start.14) | collective-permute-done | bytes 524320 | tf_op jit(solution)/shard_map/ppermute | solution.py:434
  72.5 1.4 %shard_map.126 = (bf16[128,4096]{1,0:T(8,128)(2,1)}, bf16[128,4096]{1,0:T(8,128)(2,1)}) custom-call(bf16[128,4096]{1,0:T(8,128)(2,1)S(1)} %copy-done, bf16[128,4096]{1,0:T(8,128)(2,1)S(1)} %get-tuple-element.40.own_ref, bf16[128,4096]{1,0:T(8,128)(2,1)S(1)} %collective-permute-done.12.given_ref, ...), custom_call_target="tpu_custom_call", output_to_operand_aliasing={{0}: (5, {}), {1}: (6, {})} | custom-call | flops 1000000000 | bytes 2000000 | tf_op jit(solution)/shard_map/pallas_call | solution.py:399
  (31 shorter events, 0.1 us)
Async XLA Ops:
  0.6 5.0 %copy-start.4 = (s32[16]{0:T(128)S(1)}, s32[16]{0:T(128)}, u32[]{:S(2)}) copy-start(s32[16]{0:T(128)} %param.17) | copy-start | bytes 196
  0.6 5.1 %copy-start.3 = (bf16[2,124,512]{2,0,1:T(2,128)(2,1)S(1)}, bf16[2,124,512]{2,0,1:T(2,128)(2,1)}, u32[]{:S(2)}) copy-start(bf16[2,124,512]{2,0,1:T(2,128)(2,1)} %param.12) | copy-start | bytes 761860
  2.0 5.0 %collective-permute-start.7 = (bf16[128,128]{1,0:T(8,128)(2,1)S(1)}, bf16[128,128]{1,0:T(8,128)(2,1)S(1)}, u32[]{:S(2)}, u32[]{:S(2)}) collective-permute-start(bf16[128,128]{1,0:T(8,128)(2,1)S(1)} %get-tuple-element.34.refs_0_.refs_4_), channel_id=1, source_target_pairs={{0,2},{1,3},{2,0},{3,1},{4,6},{5,7},{6,4},{7,5},{8,10},{9,11},{10,... | collective-permute-start | bytes 98312 | tf_op jit(solution)/shard_map/ppermute | solution.py:434
  5.0 3.1 %collective-permute-start.6 = (bf16[128,128]{1,0:T(8,128)(2,1)S(1)}, bf16[128,128]{1,0:T(8,128)(2,1)S(1)}, u32[]{:S(2)}, u32[]{:S(2)}) collective-permute-start(bf16[128,128]{1,0:T(8,128)(2,1)S(1)} %get-tuple-element.34.refs_0_.refs_4_), channel_id=1, source_target_pairs={{0,1},{1,0},{2,3},{3,2},{4,5},{5,4},{6,7},{7,6},{8,9},{9,8},{10,11... | collective-permute-start | bytes 98312 | tf_op jit(solution)/shard_map/ppermute | solution.py:434
  6.9 1.2 %collective-permute-start.8 = (bf16[128,128]{1,0:T(8,128)(2,1)S(1)}, bf16[128,128]{1,0:T(8,128)(2,1)S(1)}, u32[]{:S(2)}, u32[]{:S(2)}) collective-permute-start(bf16[128,128]{1,0:T(8,128)(2,1)S(1)} %collective-permute-done.7.refs_2_), channel_id=1, source_target_pairs={{0,1},{1,0},{2,3},{3,2},{4,5},{5,4},{6,7},{7,6},{8,9},{9,8},{10,11... | collective-permute-start | bytes 98312 | tf_op jit(solution)/shard_map/ppermute | solution.py:434
  7.6 9.6 %collective-permute-start.3 = (bf16[256,128]{1,0:T(8,128)(2,1)S(1)}, bf16[256,128]{1,0:T(8,128)(2,1)S(1)}, u32[]{:S(2)}, u32[]{:S(2)}) collective-permute-start(bf16[256,128]{1,0:T(8,128)(2,1)S(1)} %get-tuple-element.31), channel_id=1, source_target_pairs={{0,1},{1,0},{2,3},{3,2},{4,5},{5,4},{6,7},{7,6},{8,9},{9,8},{10,11... | collective-permute-start | bytes 196616 | tf_op jit(solution)/shard_map/ppermute | solution.py:434
  8.1 2.8 %copy-start.2 = (bf16[2,16,192,512]{3,2,1,0:T(8,128)(2,1)S(1)}, bf16[2,16,192,512]{3,2,1,0:T(8,128)(2,1)}, u32[]{:S(2)}) copy-start(bf16[2,16,192,512]{3,2,1,0:T(8,128)(2,1)} %refs_4_.1) | copy-start | bytes 18874372
  10.9 16.5 %slice-start = ((s8[8388608]{0:T(1024)(128)(4,1)}), s8[4194304]{0:T(1024)(128)(4,1)S(1)}, s32[]{:S(2)}) async-start(s8[8388608]{0:T(1024)(128)(4,1)} %bitcast.2), calls=%async_computation | async-start | bytes 8388608
  13.2 4.0 %collective-permute-start.9 = (bf16[152,128]{1,0:T(8,128)(2,1)S(1)}, bf16[152,128]{1,0:T(8,128)(2,1)S(1)}, u32[]{:S(2)}, u32[]{:S(2)}) collective-permute-start(bf16[152,128]{1,0:T(8,128)(2,1)S(1)} %get-tuple-element.36), channel_id=1, source_target_pairs={{0,1},{1,0},{2,3},{3,2},{4,5},{5,4},{6,7},{7,6},{8,9},{9,8},{10,11... | collective-permute-start | bytes 116744 | tf_op jit(solution)/shard_map/ppermute | solution.py:434
  13.4 4.2 %collective-permute-start.10 = (bf16[152,128]{1,0:T(8,128)(2,1)S(1)}, bf16[152,128]{1,0:T(8,128)(2,1)S(1)}, u32[]{:S(2)}, u32[]{:S(2)}) collective-permute-start(bf16[152,128]{1,0:T(8,128)(2,1)S(1)} %get-tuple-element.37), channel_id=1, source_target_pairs={{0,2},{1,3},{2,0},{3,1},{4,6},{5,7},{6,4},{7,5},{8,10},{9,11},{10,... | collective-permute-start | bytes 116744 | tf_op jit(solution)/shard_map/ppermute | solution.py:434
  15.4 4.2 %collective-permute-start.11 = (bf16[152,128]{1,0:T(8,128)(2,1)S(1)}, bf16[152,128]{1,0:T(8,128)(2,1)S(1)}, u32[]{:S(2)}, u32[]{:S(2)}) collective-permute-start(bf16[152,128]{1,0:T(8,128)(2,1)S(1)} %get-tuple-element.38), channel_id=1, source_target_pairs={{0,3},{1,2},{2,1},{3,0},{4,7},{5,6},{6,5},{7,4},{8,11},{9,10},{10,... | collective-permute-start | bytes 116744 | tf_op jit(solution)/shard_map/ppermute | solution.py:434
  15.4 6.8 %collective-permute-start.4 = (bf16[256,128]{1,0:T(8,128)(2,1)S(1)}, bf16[256,128]{1,0:T(8,128)(2,1)S(1)}, u32[]{:S(2)}, u32[]{:S(2)}) collective-permute-start(bf16[256,128]{1,0:T(8,128)(2,1)S(1)} %get-tuple-element.32), channel_id=1, source_target_pairs={{0,2},{1,3},{2,0},{3,1},{4,6},{5,7},{6,4},{7,5},{8,10},{9,11},{10,... | collective-permute-start | bytes 196616 | tf_op jit(solution)/shard_map/ppermute | solution.py:434
  17.1 5.1 %collective-permute-start.5 = (bf16[256,128]{1,0:T(8,128)(2,1)S(1)}, bf16[256,128]{1,0:T(8,128)(2,1)S(1)}, u32[]{:S(2)}, u32[]{:S(2)}) collective-permute-start(bf16[256,128]{1,0:T(8,128)(2,1)S(1)} %get-tuple-element.33), channel_id=1, source_target_pairs={{0,3},{1,2},{2,1},{3,0},{4,7},{5,6},{6,5},{7,4},{8,11},{9,10},{10,... | collective-permute-start | bytes 196616 | tf_op jit(solution)/shard_map/ppermute | solution.py:434
  17.2 5.1 %collective-permute-start = (bf16[512,128]{1,0:T(8,128)(2,1)S(1)}, bf16[512,128]{1,0:T(8,128)(2,1)S(1)}, u32[]{:S(2)}, u32[]{:S(2)}) collective-permute-start(bf16[512,128]{1,0:T(8,128)(2,1)S(1)} %get-tuple-element.27), channel_id=1, source_target_pairs={{0,1},{1,0},{2,3},{3,2},{4,5},{5,4},{6,7},{7,6},{8,9},{9,8},{10,11... | collective-permute-start | bytes 393224 | tf_op jit(solution)/shard_map/ppermute | solution.py:434
  17.6 7.6 %collective-permute-start.1 = (bf16[512,128]{1,0:T(8,128)(2,1)S(1)}, bf16[512,128]{1,0:T(8,128)(2,1)S(1)}, u32[]{:S(2)}, u32[]{:S(2)}) collective-permute-start(bf16[512,128]{1,0:T(8,128)(2,1)S(1)} %get-tuple-element.28), channel_id=1, source_target_pairs={{0,2},{1,3},{2,0},{3,1},{4,6},{5,7},{6,4},{7,5},{8,10},{9,11},{10,... | collective-permute-start | bytes 393224 | tf_op jit(solution)/shard_map/ppermute | solution.py:434
  19.6 7.8 %slice-start.1 = ((s8[8388608]{0:T(1024)(128)(4,1)}), s8[4194304]{0:T(1024)(128)(4,1)S(1)}, s32[]{:S(2)}) async-start(s8[8388608]{0:T(1024)(128)(4,1)} %bitcast.2), calls=%async_computation.1 | async-start | bytes 8388608
  19.6 7.7 %collective-permute-start.2 = (bf16[512,128]{1,0:T(8,128)(2,1)S(1)}, bf16[512,128]{1,0:T(8,128)(2,1)S(1)}, u32[]{:S(2)}, u32[]{:S(2)}) collective-permute-start(bf16[512,128]{1,0:T(8,128)(2,1)S(1)} %get-tuple-element.29), channel_id=1, source_target_pairs={{0,3},{1,2},{2,1},{3,0},{4,7},{5,6},{6,5},{7,4},{8,11},{9,10},{10,... | collective-permute-start | bytes 393224 | tf_op jit(solution)/shard_map/ppermute | solution.py:434
  32.0 14.8 %collective-permute-start.15 = (bf16[64,4096]{1,0:T(8,128)(2,1)S(1)}, bf16[64,4096]{1,0:T(8,128)(2,1)S(1)}, u32[]{:S(2)}, u32[]{:S(2)}) collective-permute-start(bf16[64,4096]{1,0:T(8,128)(2,1)S(1)} %get-tuple-element.45), channel_id=1, source_target_pairs={{0,1},{1,0},{2,3},{3,2},{4,5},{5,4},{6,7},{7,6},{8,9},{9,8},{10,11... | collective-permute-start | bytes 1572872 | tf_op jit(solution)/shard_map/ppermute | solution.py:434
  37.5 24.4 %copy-start = (bf16[128,4096]{1,0:T(8,128)(2,1)S(1)}, bf16[128,4096]{1,0:T(8,128)(2,1)}, u32[]{:S(2)}) copy-start(bf16[128,4096]{1,0:T(8,128)(2,1)} %res_ref.3) | copy-start | bytes 3145732
  37.5 24.3 %copy-start.1 = (f32[4096]{0:T(1024)S(1)}, f32[4096]{0:T(1024)}, u32[]{:S(2)}) copy-start(f32[4096]{0:T(1024)} %param.21) | copy-start | bytes 49156
  37.5 10.4 %collective-permute-start.13 = (bf16[64,4096]{1,0:T(8,128)(2,1)S(1)}, bf16[64,4096]{1,0:T(8,128)(2,1)S(1)}, u32[]{:S(2)}, u32[]{:S(2)}) collective-permute-start(bf16[64,4096]{1,0:T(8,128)(2,1)S(1)} %get-tuple-element.43), channel_id=1, source_target_pairs={{0,1},{1,0},{2,3},{3,2},{4,5},{5,4},{6,7},{7,6},{8,9},{9,8},{10,11... | collective-permute-start | bytes 1572872 | tf_op jit(solution)/shard_map/ppermute | solution.py:434
  46.6 15.2 %collective-permute-start.12 = (bf16[128,4096]{1,0:T(8,128)(2,1)S(1)}, bf16[128,4096]{1,0:T(8,128)(2,1)S(1)}, u32[]{:S(2)}, u32[]{:S(2)}) collective-permute-start(bf16[128,4096]{1,0:T(8,128)(2,1)S(1)} %get-tuple-element.41), channel_id=1, source_target_pairs={{0,1},{1,0},{2,3},{3,2},{4,5},{5,4},{6,7},{7,6},{8,9},{9,8},{10,11... | collective-permute-start | bytes 3145736 | tf_op jit(solution)/shard_map/ppermute | solution.py:434
  47.0 14.9 %collective-permute-start.16 = (bf16[64,4096]{1,0:T(8,128)(2,1)S(1)}, bf16[64,4096]{1,0:T(8,128)(2,1)S(1)}, u32[]{:S(2)}, u32[]{:S(2)}) collective-permute-start(bf16[64,4096]{1,0:T(8,128)(2,1)S(1)} %add_convert_fusion), channel_id=1, source_target_pairs={{0,2},{1,3},{2,0},{3,1},{4,6},{5,7},{6,4},{7,5},{8,10},{9,11},{10,... | collective-permute-start | bytes 1572872 | tf_op jit(solution)/shard_map/ppermute | solution.py:434
  48.1 24.4 %collective-permute-start.14 = (bf16[64,4096]{1,0:T(8,128)(2,1)S(1)}, bf16[64,4096]{1,0:T(8,128)(2,1)S(1)}, u32[]{:S(2)}, u32[]{:S(2)}) collective-permute-start(bf16[64,4096]{1,0:T(8,128)(2,1)S(1)} %add_convert_fusion.1), channel_id=1, source_target_pairs={{0,2},{1,3},{2,0},{3,1},{4,6},{5,7},{6,4},{7,5},{8,10},{9,11},{10,... | collective-permute-start | bytes 1572872 | tf_op jit(solution)/shard_map/ppermute | solution.py:434

commit v3 on v2

--- a/solution.py
+++ b/solution.py
@@ -124,39 +124,9 @@
         ),
         out_shape=[jax.ShapeDtypeStruct((2 * p_pad, HEAD_DIM), BF16)] * devices,
         compiler_params=params(8),
-        cost_estimate=busy(6),
+        cost_estimate=busy(12),
         name="pack_fresh",
     )(meta, *([prompt] * devices))
-
-
-def stage(prompt_queries, decode_queries, entries, local_heads, group):
-    prompt_rows, decode_rows = prompt_queries.shape[0], decode_queries.shape[0]
-
-    def body(q_hbm, dq_hbm, e_hbm, q_ref, e_ref, sem):
-        lane = pl.multiple_of(lax.axis_index("tp") * local_heads // group * HEAD_DIM, HEAD_DIM)
-        copies = [
-            pltpu.make_async_copy(q_hbm, q_ref.at[0:prompt_rows, :], sem.at[0]),
-            pltpu.make_async_copy(dq_hbm, q_ref.at[prompt_rows : prompt_rows + decode_rows, :], sem.at[1]),
-            pltpu.make_async_copy(e_hbm.at[:, :, pl.ds(lane, HEAD_DIM)], e_ref, sem.at[2]),
-        ]
-        for copy in copies:
-            copy.start()
-        for copy in copies:
-            copy.wait()
-
-    return pl.pallas_call(
-        body,
-        in_specs=[in_hbm()] * 3,
-        out_specs=[in_vmem()] * 2,
-        out_shape=[
-            pltpu.VMEM((prompt_rows + decode_rows, prompt_queries.shape[1]), BF16),
-            pltpu.VMEM((2, decode_rows, HEAD_DIM), BF16),
-        ],
-        scratch_shapes=[pltpu.SemaphoreType.DMA((3,))],
-        compiler_params=params(2),
-        cost_estimate=busy(6),
-        name="stage",
-    )(to_hbm(prompt_queries), to_hbm(decode_queries), to_hbm(entries))
 
 
 def split(value):
@@ -167,7 +137,7 @@
     return terms
 
 
-def decode_partials(queries, cache, meta, local_heads, group):
+def decode_partials(queries, cache, prompt_queries, decode_queries, entries, meta, local_heads, group):
     devices = len(queries)
     rows, span, width = cache.shape[1], cache.shape[2], cache.shape[3]
     kv_heads = width // HEAD_DIM
@@ -175,12 +145,22 @@
     factor = HEAD_DIM ** (-0.5) * float(np.log2(np.e))
     part_rows = rows * local_heads
     stat_rows = round_up(local_heads, 8)
+    prompt_rows = prompt_queries.shape[0]
 
     def body(m, *refs):
-        q_refs, cache_ref = refs[:devices], refs[devices]
-        o_refs = refs[devices + 1 : 2 * devices + 1]
-        q_all, sums = refs[2 * devices + 1 :]
+        q_refs, refs = refs[:devices], refs[devices:]
+        cache_ref, pq_hbm, dq_hbm, e_hbm = refs[:4]
+        o_refs, refs = refs[4 : 4 + devices], refs[4 + devices :]
+        q_ref, e_ref, q_all, sums, sem = refs
         me = m[0]
+        lane = pl.multiple_of(me * local_heads // group * HEAD_DIM, HEAD_DIM)
+        copies = [
+            pltpu.make_async_copy(pq_hbm, q_ref.at[0:prompt_rows, :], sem.at[0]),
+            pltpu.make_async_copy(dq_hbm, q_ref.at[prompt_rows : prompt_rows + rows, :], sem.at[1]),
+            pltpu.make_async_copy(e_hbm.at[:, :, pl.ds(lane, HEAD_DIM)], e_ref, sem.at[2]),
+        ]
+        for copy in copies:
+            copy.start()
         for k in range(devices):
             for h in range(local_heads):
                 q_all[k, pl.ds(h, rows, stride=local_heads), :] = q_refs[k][h * rows : (h + 1) * rows, :].astype(F32)
@@ -221,17 +201,24 @@
             for i, term in enumerate(terms):
                 row = part_rows + i * stat_rows
                 o_refs[k][row : row + local_heads, :] = term[k * local_heads : (k + 1) * local_heads, :]
-
-    return pl.pallas_call(
-        body,
-        in_specs=[smem()] + [in_vmem()] * (devices + 1),
-        out_specs=[in_vmem()] * devices,
-        scratch_shapes=[pltpu.VMEM((devices, part_rows, HEAD_DIM), F32)] * 2,
-        out_shape=[jax.ShapeDtypeStruct((part_rows + 3 * stat_rows, HEAD_DIM), BF16)] * devices,
+        for copy in copies:
+            copy.wait()
+
+    outs = pl.pallas_call(
+        body,
+        in_specs=[smem()] + [in_vmem()] * (devices + 1) + [in_hbm()] * 3,
+        out_specs=[in_vmem()] * (devices + 2),
+        scratch_shapes=[pltpu.VMEM((devices, part_rows, HEAD_DIM), F32)] * 2 + [pltpu.SemaphoreType.DMA((3,))],
+        out_shape=[jax.ShapeDtypeStruct((part_rows + 3 * stat_rows, HEAD_DIM), BF16)] * devices
+        + [
+            pltpu.VMEM((prompt_rows + rows, prompt_queries.shape[1]), BF16),
+            pltpu.VMEM((2, rows, HEAD_DIM), BF16),
+        ],
         compiler_params=params(12),
-        cost_estimate=busy(6),
+        cost_estimate=busy(12),
         name="decode",
-    )(meta, *queries, cache)
+    )(meta, *queries, cache, to_hbm(prompt_queries), to_hbm(decode_queries), to_hbm(entries))
+    return outs[:devices], outs[devices], outs[devices + 1]
 
 
 def decode_join(parts, queries, entries, local_heads):
@@ -283,7 +270,31 @@
     )(*parts, queries, entries)
 
 
-def attend(slots, first, count, block, queries, history, fresh, decoded, weight, meta, h_rows, p_rows):
+def product(att, w, start, stop, half, keep_ref, give_ref):
+    for c in range(start, stop, COLUMNS):
+        out = jnp.dot(att[...], w[:, c : c + COLUMNS], preferred_element_type=F32).astype(BF16)
+        keep_ref[:, c - start : c - start + COLUMNS] = out[:half]
+        give_ref[:, c - start : c - start + COLUMNS] = out[half:]
+
+
+def project(att, weight, start):
+    rows, model = att.shape[0], weight.shape[1]
+
+    def body(att_ref, w, keep_ref, give_ref):
+        product(att_ref, w, start, model, rows // 2, keep_ref, give_ref)
+
+    return pl.pallas_call(
+        body,
+        in_specs=[in_vmem()] * 2,
+        out_specs=[in_vmem()] * 2,
+        out_shape=[jax.ShapeDtypeStruct((rows // 2, model - start), BF16)] * 2,
+        compiler_params=params(8),
+        cost_estimate=busy(2),
+        name="project",
+    )(att, weight)
+
+
+def attend(slots, first, count, block, queries, history, fresh, decoded, weight, meta, h_rows, p_rows, columns):
     devices = len(history)
     p_pad = fresh[0].shape[0] // 2
     local_width = queries.shape[1]
@@ -303,7 +314,7 @@
         rest = refs[2 * devices :]
         if has_decode:
             dec_ref, rest = rest[0], rest[1:]
-        w, keep_ref, give_ref, k_all, v_all, att = rest
+        w, keep_ref, give_ref, att, k_all, v_all = rest
         me, valid_rows = m[0], m[1]
         for k in range(devices):
             for part, dst in ((0, k_all), (1, v_all)):
@@ -347,22 +358,18 @@
                 def _():
                     att[(i + 1) * count - decode_rows : (i + 1) * count, :] = dec_ref[...]
 
-        for c in range(0, model, COLUMNS):
-            out = jnp.dot(att[...], w[:, c : c + COLUMNS], preferred_element_type=F32).astype(BF16)
-            keep_ref[:, c : c + COLUMNS] = out[:half]
-            give_ref[:, c : c + COLUMNS] = out[half:]
+        product(att, w, 0, columns, half, keep_ref, give_ref)
 
     flops = 2 * len(order) * count * (2 * local_width * keys + local_width * model)
     n_vmem = 2 + 2 * devices + has_decode
     return pl.pallas_call(
         body,
         in_specs=[smem()] + [in_vmem()] * n_vmem,
-        out_specs=[in_vmem()] * 2,
-        out_shape=[jax.ShapeDtypeStruct((half, model), BF16)] * 2,
+        out_specs=[in_vmem()] * 3,
+        out_shape=[jax.ShapeDtypeStruct((half, columns), BF16)] * 2 + [pltpu.VMEM((2 * half, local_width), BF16)],
         scratch_shapes=[
             pltpu.VMEM((keys, HEAD_DIM), BF16),
             pltpu.VMEM((keys, HEAD_DIM), BF16),
-            pltpu.VMEM((2 * half, local_width), BF16),
         ],
         compiler_params=params(24),
         cost_estimate=pl.CostEstimate(flops=flops, transcendentals=0, bytes_accessed=weight.size * 2),
@@ -374,6 +381,7 @@
     count = crossed[0].shape[0]
     tile = 16
     n_cross = len(crossed)
+    n_columns = model // crossed[0].shape[1]
 
     def body(res_ref, own_ref, given_ref, *refs):
         cross = refs[:n_cross]
@@ -384,8 +392,9 @@
         for i in range(0, count, tile):
             here, local = slice(first + i, first + i + tile), slice(i, i + tile)
             hidden = res_ref[here, :].astype(F32) + own_ref[here, :].astype(F32) + given_ref[here, :].astype(F32)
-            for c in cross:
-                hidden = hidden + c[local, :].astype(F32)
+            for c in range(0, n_cross, n_columns):
+                pieces = [piece[local, :].astype(F32) for piece in cross[c : c + n_columns]]
+                hidden = hidden + (jnp.concatenate(pieces, axis=1) if n_columns > 1 else pieces[0])
             mean = jnp.mean(hidden * hidden, axis=-1, keepdims=True)
             staged[0][local, :] = hidden.astype(BF16)
             staged[1][local, :] = (hidden * lax.rsqrt(mean + EPS) * gain_ref[...]).astype(BF16)
@@ -445,25 +454,50 @@
     history = swapped(packed)
     meta = jnp.concatenate([lax.axis_index("tp").astype(jnp.int32)[None], prompt_start, decode_lengths])
     fresh = swapped(pack_fresh(prompt_entries, meta, devices, local_heads, group))
-    queries, entries = stage(prompt_queries, decode_queries, decode_entries, local_heads, group)
     ordered = [decode_rows[k] for k in range(devices)]
-    parts = swapped(decode_partials(ordered, decode_cache, meta, local_heads, group))
+    parts, queries, entries = decode_partials(
+        ordered, decode_cache, prompt_queries, decode_queries, decode_entries, meta, local_heads, group
+    )
+    parts = swapped(parts)
     decoded = decode_join(parts, own_query, entries, local_heads)
 
-    def attended(slots, first, count, decoded):
-        return attend(slots, first, count, block, queries, history, fresh, decoded, out_weight, meta, h_rows, p_rows)
+    def attended(slots, first, count, decoded, columns):
+        return attend(
+            slots, first, count, block, queries, history, fresh, decoded, out_weight, meta, h_rows, p_rows, columns
+        )
+
+    def chip_sum(keep, give):
+        return keep.astype(F32) + swap(give, 1).astype(F32)
+
+    def cross(pair, count, start, stop):
+        return [
+            swap(pair[k * count + start : k * count + stop].astype(BF16), 2 * k + 2)
+            for k in range(devices // 2 - 1)
+        ]
 
     chunks = [c * block // sum(CHUNKS) for c in CHUNKS]
     if any(c % 16 for c in chunks):
         chunks = [block]
+    model = out_weight.shape[1]
+    others = list(range(2, devices))
     crossed, first = [], 0
     for count in chunks:
-        keep, give = attended(list(range(2, devices)), first, count, decoded if first + count == block else None)
-        taken = swap(give, 1)
-        pair = (keep.astype(F32) + taken.astype(F32)).astype(BF16)
-        crossed.append((first, [swap(pair[(k // 2 - 1) * count : k // 2 * count], k) for k in range(2, devices, 2)]))
+        last = first + count == block
+        columns = model if last else model // 2
+        keep, give, att = attended(others, first, count, decoded if last else None, columns)
+        pair = chip_sum(keep, give)
+        if last:
+            half = count // 2 if count % 32 == 0 else count
+            for start in range(0, count, half):
+                crossed.append((first + start, cross(pair, count, start, start + half)))
+        else:
+            pieces = [cross(pair, count, 0, count)]
+            keep, give = project(att, out_weight, columns)
+            pair = chip_sum(keep, give)
+            pieces.append(cross(pair, count, 0, count))
+            crossed.append((first, [piece for both in zip(*pieces) for piece in both]))
         first += count
-    own, give = attended([0, 1], 0, block, decoded)
+    own, give, _ = attended([0, 1], 0, block, decoded, model)
     given = swap(give, 1)
     gain = norm_gain[None, :]
     outs = []

time: 74.2 us -> 75 us (1.011)
  local copies, waits for them, and re-layouts: 2.84 us -> 0.57 us
  starting transfers between devices: 13 us -> 14.7 us
    unnamed x15 -> x17, local copies, waits for them, and re-layouts: 2.84 us -> 0.54 us
    ppermute x17 -> x20, starting transfers between devices: 13 us -> 14.7 us  [swap(): return lax.ppermute(value, 'tp', [(i, i ^ k) for i in range(devices)])]
    ppermute x17 -> x20, waiting for transfers between devices: 28.1 us -> 28.8 us  [swap(): return lax.ppermute(value, 'tp', [(i, i ^ k) for i in range(devices)])]
    pallas_call x2 -> x3, Pallas kernels: 2.76 us -> 3.38 us  [finish(): pl.pallas_call(body, in_specs=[in_vmem()] * n_in + [hbm()] * len(previous...]
  transfers between devices with their start and end apart: 17 -> 20, of which waited for: 5 -> 8; matrix products, arithmetic and copies ran while one was open for 0% -> 1% of each run, Pallas kernels for 28% -> 30%
where the time goes in v3:
time: 75 us; the launch traced here: 74.8 us
  Pallas kernels  28.8 us (38%)
  waiting for transfers between devices  28.8 us (38%)
  starting transfers between devices  14.7 us (20%)
  between operations  1.66 us (2%)
    ppermute x20, waiting for transfers between devices, swap(): return lax.ppermute(value, 'tp', [(i, i ^ k) for i in range(devices)])  28.8 us
    pallas_call x3, Pallas kernels, attend(): pl.pallas_call(body, in_specs=[smem()] + [in_vmem()] * n_vmem, out_specs=...  18.5 us
    ppermute x20, starting transfers between devices, swap(): return lax.ppermute(value, 'tp', [(i, i ^ k) for i in range(devices)])  14.7 us
    pallas_call x3, Pallas kernels, finish(): pl.pallas_call(body, in_specs=[in_vmem()] * n_in + [hbm()] * len(previous...  3.38 us
    pallas_call x1, Pallas kernels, decode_partials(): pl.pallas_call(body, in_specs=[smem()] + [in_vmem()] * (devices + 1) + [i...  3 us
  transfers between devices with their start and end apart: 20, of which 8 were waited for; matrix products, arithmetic and copies ran while one was open for 1% of the time, Pallas kernels for 30%

profile of v3, /device:TPU:0, one launch (start us, length us, event | category | flops | bytes accessed | tf_op | source)
XLA Modules:
  0.0 74.8 jit_solution(15085354603972251056)
XLA Ops:
  0.7 1.3 %pack_history.1 = (bf16[512,128]{1,0:T(8,128)(2,1)S(1)}, bf16[512,128]{1,0:T(8,128)(2,1)S(1)}, bf16[512,128]{1,0:T(8,128)(2,1)S(1)}, bf16[512,128]{1,0:T(8,128)(2,1)S(1)}, bf16[128,128]{1,0:T(8,128)(2,1)S(1)}) custom-call(bf16[2,256,512]{2,1,0:T(8,128)(2,1)} %h_hbm.1, bf16[16,1024]{1,0:T(8,128)(2,1)} %refs_6_.1), custom_call_target="tpu_custom_call" | custom-call | flops 3000000000 | bytes 6000000 | tf_op jit(solution)/shard_map/pack_history/pallas_call | solution.py:84
  2.0 3.1 %collective-permute-start.1 = (bf16[128,128]{1,0:T(8,128)(2,1)S(1)}, bf16[128,128]{1,0:T(8,128)(2,1)S(1)}, u32[]{:S(2)}, u32[]{:S(2)}) collective-permute-start(bf16[128,128]{1,0:T(8,128)(2,1)S(1)} %get-tuple-element.30.refs_0_.refs_4_), channel_id=1, source_target_pairs={{0,2},{1,3},{2,0},{3,1},{4,6},{5,7},{6,4},{7,5},{8,10},{9,11},{10,... | collective-permute-start | bytes 98312 | tf_op jit(solution)/shard_map/ppermute | solution.py:443
  5.8 1.1 %collective-permute-done.1.refs_2_ = bf16[128,128]{1,0:T(8,128)(2,1)S(1)} collective-permute-done((bf16[128,128]{1,0:T(8,128)(2,1)S(1)}, bf16[128,128]{1,0:T(8,128)(2,1)S(1)}, u32[]{:S(2)}, u32[]{:S(2)}) %collective-permute-start.1) | collective-permute-done | bytes 32800 | tf_op jit(solution)/shard_map/ppermute | solution.py:443
  6.9 0.6 pack_fresh.1
  7.6 0.6 collective-permute-start.6
  8.2 0.5 slice-done.3
  8.6 3.0 %decode.1 = (bf16[152,128]{1,0:T(8,128)(2,1)S(1)}, bf16[152,128]{1,0:T(8,128)(2,1)S(1)}, bf16[152,128]{1,0:T(8,128)(2,1)S(1)}, bf16[152,128]{1,0:T(8,128)(2,1)S(...) custom-call(s32[18]{0:T(128)S(1)} %pad_add_fusion.m, ...), custom_call_target="tpu_custom_call" | custom-call | flops 6000000000 | bytes 12000000 | tf_op jit(solution)/shard_map/decode/pallas_call | solution.py:207
  11.6 0.6 collective-permute-start.9
  12.3 1.5 %collective-permute-start.4 = (bf16[512,128]{1,0:T(8,128)(2,1)S(1)}, bf16[512,128]{1,0:T(8,128)(2,1)S(1)}, u32[]{:S(2)}, u32[]{:S(2)}) collective-permute-start(bf16[512,128]{1,0:T(8,128)(2,1)S(1)} %get-tuple-element.34), channel_id=1, source_target_pairs={{0,2},{1,3},{2,0},{3,1},{4,6},{5,7},{6,4},{7,5},{8,10},{9,11},{10,... | collective-permute-start | bytes 393224 | tf_op jit(solution)/shard_map/ppermute | solution.py:443
  14.1 1.5 %collective-permute-start.10 = (bf16[152,128]{1,0:T(8,128)(2,1)S(1)}, bf16[152,128]{1,0:T(8,128)(2,1)S(1)}, u32[]{:S(2)}, u32[]{:S(2)}) collective-permute-start(bf16[152,128]{1,0:T(8,128)(2,1)S(1)} %get-tuple-element.42), channel_id=1, source_target_pairs={{0,2},{1,3},{2,0},{3,1},{4,6},{5,7},{6,4},{7,5},{8,10},{9,11},{10,... | collective-permute-start | bytes 116744 | tf_op jit(solution)/shard_map/ppermute | solution.py:443
  15.8 6.4 %collective-permute-done.10.refs_2_ = bf16[152,128]{1,0:T(8,128)(2,1)S(1)} collective-permute-done((bf16[152,128]{1,0:T(8,128)(2,1)S(1)}, bf16[152,128]{1,0:T(8,128)(2,1)S(1)}, u32[]{:S(2)}, u32[]{:S(2)}) %collective-permute-start.10) | collective-permute-done | bytes 38944 | tf_op jit(solution)/shard_map/ppermute | solution.py:443
  22.2 1.5 %collective-permute-start.7 = (bf16[256,128]{1,0:T(8,128)(2,1)S(1)}, bf16[256,128]{1,0:T(8,128)(2,1)S(1)}, u32[]{:S(2)}, u32[]{:S(2)}) collective-permute-start(bf16[256,128]{1,0:T(8,128)(2,1)S(1)} %get-tuple-element.38), channel_id=1, source_target_pairs={{0,2},{1,3},{2,0},{3,1},{4,6},{5,7},{6,4},{7,5},{8,10},{9,11},{10,... | collective-permute-start | bytes 196616 | tf_op jit(solution)/shard_map/ppermute | solution.py:443
  23.7 1.2 %join.1.refs_8_ = bf16[16,1024]{1,0:T(8,128)(2,1)S(1)} custom-call(bf16[152,128]{1,0:T(8,128)(2,1)S(1)} %get-tuple-element.40.refs_0_, bf16[152,128]{1,0:T(8,128)(2,1)S(1)} %collective-permute-done.9.refs_1_, bf16[152,128]{1,0:T(8,128)(2,1)S(1)} %collective-permute-done.10.refs_2_, bf16[152,128]{1,0:T(8,128)(2,1)S(1)} %collective-permute-done.11.refs_3_, ...), custom_call_target="tpu_custom_call" | custom-call | flops 500000000 | bytes 1000000 | tf_op jit(solution)/shard_map/join/pallas_call | solution.py:261
  24.9 1.6 %collective-permute-done.7.refs_6_ = bf16[256,128]{1,0:T(8,128)(2,1)S(1)} collective-permute-done((bf16[256,128]{1,0:T(8,128)(2,1)S(1)}, bf16[256,128]{1,0:T(8,128)(2,1)S(1)}, u32[]{:S(2)}, u32[]{:S(2)}) %collective-permute-start.7) | collective-permute-done | bytes 65568 | tf_op jit(solution)/shard_map/ppermute | solution.py:443
  26.5 1.4 %collective-permute-done.8.refs_7_ = bf16[256,128]{1,0:T(8,128)(2,1)S(1)} collective-permute-done((bf16[256,128]{1,0:T(8,128)(2,1)S(1)}, bf16[256,128]{1,0:T(8,128)(2,1)S(1)}, u32[]{:S(2)}, u32[]{:S(2)}) %collective-permute-start.8) | collective-permute-done | bytes 65568 | tf_op jit(solution)/shard_map/ppermute | solution.py:443
  27.9 4.0 %shard_map.124 = (bf16[64,2048]{1,0:T(8,128)(2,1)S(1)}, bf16[64,2048]{1,0:T(8,128)(2,1)S(1)}, bf16[128,1024]{1,0:T(8,128)(2,1)S(1)}) custom-call(s32[18]{0:T(128)S(1)} %pad_add_fusion.m, bf16[512,1024]{1,0:T(8,128)(2,1)S(1)} %get-tuple-element.31.q, bf16[512,128]{1,0:T(8,128)(2,1)S(1)} %get-tuple-element.32.refs_0_, ...), custom_call_target="tpu_custom_call" | custom-call | flops 1879048192 | bytes 8388608 | tf_op jit(solution)/shard_map/pallas_call | solution.py:365
  32.0 0.7 project.1
  32.8 0.6 collective-permute-start.18
  33.3 5.2 %shard_map.123 = (bf16[64,4096]{1,0:T(8,128)(2,1)S(1)}, bf16[64,4096]{1,0:T(8,128)(2,1)S(1)}, bf16[128,1024]{1,0:T(8,128)(2,1)}) custom-call(s32[18]{0:T(128)S(1)} %pad_add_fusion.m, bf16[512,1024]{1,0:T(8,128)(2,1)S(1)} %get-tuple-element.31.q, bf16[512,128]{1,0:T(8,128)(2,1)S(1)} %get-tuple-element.32.refs_0_, ...), custom_call_target="tpu_custom_call" | custom-call | flops 1879048192 | bytes 8388608 | tf_op jit(solution)/shard_map/pallas_call | solution.py:365
  38.7 9.2 %shard_map.122 = (bf16[128,4096]{1,0:T(8,128)(2,1)S(1)}, bf16[128,4096]{1,0:T(8,128)(2,1)S(1)}, bf16[256,1024]{1,0:T(8,128)(2,1)}) custom-call(s32[18]{0:T(128)S(1)} %pad_add_fusion.m, bf16[512,1024]{1,0:T(8,128)(2,1)S(1)} %get-tuple-element.31.q, bf16[512,128]{1,0:T(8,128)(2,1)S(1)} %get-tuple-element.32.refs_0_, ...), custom_call_target="tpu_custom_call" | custom-call | flops 3758096384 | bytes 8388608 | tf_op jit(solution)/shard_map/pallas_call | solution.py:365
  47.9 0.5 collective-permute-start.12
  48.5 0.9 %collective-permute-start.17 = (bf16[64,2048]{1,0:T(8,128)(2,1)S(1)}, bf16[64,2048]{1,0:T(8,128)(2,1)S(1)}, u32[]{:S(2)}, u32[]{:S(2)}) collective-permute-start(bf16[64,2048]{1,0:T(8,128)(2,1)S(1)} %add_convert_fusion.2), channel_id=1, source_target_pairs={{0,2},{1,3},{2,0},{3,1},{4,6},{5,7},{6,4},{7,5},{8,10},{9,11},{10,... | collective-permute-start | bytes 786440 | tf_op jit(solution)/shard_map/ppermute | solution.py:443
  49.4 1.3 %collective-permute-start.19 = (bf16[64,2048]{1,0:T(8,128)(2,1)S(1)}, bf16[64,2048]{1,0:T(8,128)(2,1)S(1)}, u32[]{:S(2)}, u32[]{:S(2)}) collective-permute-start(bf16[64,2048]{1,0:T(8,128)(2,1)S(1)} %add_convert_fusion.1), channel_id=1, source_target_pairs={{0,2},{1,3},{2,0},{3,1},{4,6},{5,7},{6,4},{7,5},{8,10},{9,11},{10,... | collective-permute-start | bytes 786440 | tf_op jit(solution)/shard_map/ppermute | solution.py:443
  50.9 0.9 %collective-permute-start.15 = (bf16[32,4096]{1,0:T(8,128)(2,1)S(1)}, bf16[32,4096]{1,0:T(8,128)(2,1)S(1)}, u32[]{:S(2)}, u32[]{:S(2)}) collective-permute-start(bf16[32,4096]{1,0:T(8,128)(2,1)S(1)} %get-tuple-element.58), channel_id=1, source_target_pairs={{0,2},{1,3},{2,0},{3,1},{4,6},{5,7},{6,4},{7,5},{8,10},{9,11},{10,... | collective-permute-start | bytes 786440 | tf_op jit(solution)/shard_map/ppermute | solution.py:443
  51.7 1.2 %collective-permute-start.14 = (bf16[32,4096]{1,0:T(8,128)(2,1)S(1)}, bf16[32,4096]{1,0:T(8,128)(2,1)S(1)}, u32[]{:S(2)}, u32[]{:S(2)}) collective-permute-start(bf16[32,4096]{1,0:T(8,128)(2,1)S(1)} %get-tuple-element.59), channel_id=1, source_target_pairs={{0,2},{1,3},{2,0},{3,1},{4,6},{5,7},{6,4},{7,5},{8,10},{9,11},{10,... | collective-permute-start | bytes 786440 | tf_op jit(solution)/shard_map/ppermute | solution.py:443
  53.0 4.7 %collective-permute-done.17.refs_0_ = bf16[64,2048]{1,0:T(8,128)(2,1)S(1)} collective-permute-done((bf16[64,2048]{1,0:T(8,128)(2,1)S(1)}, bf16[64,2048]{1,0:T(8,128)(2,1)S(1)}, u32[]{:S(2)}, u32[]{:S(2)}) %collective-permute-start.17) | collective-permute-done | bytes 262176 | tf_op jit(solution)/shard_map/ppermute | solution.py:443
  57.7 5.6 %collective-permute-done.19.refs_1_ = bf16[64,2048]{1,0:T(8,128)(2,1)S(1)} collective-permute-done((bf16[64,2048]{1,0:T(8,128)(2,1)S(1)}, bf16[64,2048]{1,0:T(8,128)(2,1)S(1)}, u32[]{:S(2)}, u32[]{:S(2)}) %collective-permute-start.19) | collective-permute-done | bytes 262176 | tf_op jit(solution)/shard_map/ppermute | solution.py:443
  63.4 1.4 %shard_map.125 = (bf16[128,4096]{1,0:T(8,128)(2,1)}, bf16[128,4096]{1,0:T(8,128)(2,1)}) custom-call(bf16[128,4096]{1,0:T(8,128)(2,1)S(1)} %copy-done, bf16[128,4096]{1,0:T(8,128)(2,1)S(1)} %get-tuple-element.45.own_ref, bf16[128,4096]{1,0:T(8,128)(2,1)S(1)} %collective-permute-done.12.given_ref, bf16[64,2048]{1,0:T(8,128)(2,1)S(1)} %collective-permute-done.17.refs_0_, ...), custom_call_target="tpu_custom_call" | custom-call | flops 1000000000 | bytes 2000000 | tf_op jit(solution)/shard_map/pallas_call | solution.py:408
  64.7 4.2 %collective-permute-done.15.refs_0_ = bf16[32,4096]{1,0:T(8,128)(2,1)S(1)} collective-permute-done((bf16[32,4096]{1,0:T(8,128)(2,1)S(1)}, bf16[32,4096]{1,0:T(8,128)(2,1)S(1)}, u32[]{:S(2)}, u32[]{:S(2)}) %collective-permute-start.15) | collective-permute-done | bytes 262176 | tf_op jit(solution)/shard_map/ppermute | solution.py:443
  69.0 1.0 %shard_map.126 = (bf16[128,4096]{1,0:T(8,128)(2,1)}, bf16[128,4096]{1,0:T(8,128)(2,1)}) custom-call(bf16[128,4096]{1,0:T(8,128)(2,1)S(1)} %copy-done, bf16[128,4096]{1,0:T(8,128)(2,1)S(1)} %get-tuple-element.45.own_ref, bf16[128,4096]{1,0:T(8,128)(2,1)S(1)} %collective-permute-done.12.given_ref, ...), custom_call_target="tpu_custom_call", output_to_operand_aliasing={{0}: (5, {}), {1}: (6, {})} | custom-call | flops 1000000000 | bytes 2000000 | tf_op jit(solution)/shard_map/pallas_call | solution.py:408
  70.0 3.7 %collective-permute-done.14.refs_0_ = bf16[32,4096]{1,0:T(8,128)(2,1)S(1)} collective-permute-done((bf16[32,4096]{1,0:T(8,128)(2,1)S(1)}, bf16[32,4096]{1,0:T(8,128)(2,1)S(1)}, u32[]{:S(2)}, u32[]{:S(2)}) %collective-permute-start.14) | collective-permute-done | bytes 262176 | tf_op jit(solution)/shard_map/ppermute | solution.py:443
  73.7 1.0 %shard_map.127 = (bf16[128,4096]{1,0:T(8,128)(2,1)}, bf16[128,4096]{1,0:T(8,128)(2,1)}) custom-call(bf16[128,4096]{1,0:T(8,128)(2,1)S(1)} %copy-done, bf16[128,4096]{1,0:T(8,128)(2,1)S(1)} %get-tuple-element.45.own_ref, bf16[128,4096]{1,0:T(8,128)(2,1)S(1)} %collective-permute-done.12.given_ref, ...), custom_call_target="tpu_custom_call", output_to_operand_aliasing={{0}: (5, {}), {1}: (6, {})} | custom-call | flops 1000000000 | bytes 2000000 | tf_op jit(solution)/shard_map/pallas_call | solution.py:408
  (43 shorter events, 1.2 us)
Async XLA Ops:
  0.6 5.0 %copy-start.3 = (s32[16]{0:T(128)S(1)}, s32[16]{0:T(128)}, u32[]{:S(2)}) copy-start(s32[16]{0:T(128)} %param.17) | copy-start | bytes 196
  0.6 5.1 %copy-start.2 = (bf16[2,124,512]{2,0,1:T(2,128)(2,1)S(1)}, bf16[2,124,512]{2,0,1:T(2,128)(2,1)}, u32[]{:S(2)}) copy-start(bf16[2,124,512]{2,0,1:T(2,128)(2,1)} %param.12) | copy-start | bytes 761860
  2.0 5.0 %collective-permute-start.1 = (bf16[128,128]{1,0:T(8,128)(2,1)S(1)}, bf16[128,128]{1,0:T(8,128)(2,1)S(1)}, u32[]{:S(2)}, u32[]{:S(2)}) collective-permute-start(bf16[128,128]{1,0:T(8,128)(2,1)S(1)} %get-tuple-element.30.refs_0_.refs_4_), channel_id=1, source_target_pairs={{0,2},{1,3},{2,0},{3,1},{4,6},{5,7},{6,4},{7,5},{8,10},{9,11},{10,... | collective-permute-start | bytes 98312 | tf_op jit(solution)/shard_map/ppermute | solution.py:443
  5.0 3.1 %collective-permute-start = (bf16[128,128]{1,0:T(8,128)(2,1)S(1)}, bf16[128,128]{1,0:T(8,128)(2,1)S(1)}, u32[]{:S(2)}, u32[]{:S(2)}) collective-permute-start(bf16[128,128]{1,0:T(8,128)(2,1)S(1)} %get-tuple-element.30.refs_0_.refs_4_), channel_id=1, source_target_pairs={{0,1},{1,0},{2,3},{3,2},{4,5},{5,4},{6,7},{7,6},{8,9},{9,8},{10,11... | collective-permute-start | bytes 98312 | tf_op jit(solution)/shard_map/ppermute | solution.py:443
  5.8 2.4 %slice-start.2 = ((s8[6291456]{0:T(1024)(128)(4,1)}), s8[4194304]{0:T(1024)(128)(4,1)S(1)}, s32[]{:S(2)}) async-start(s8[6291456]{0:T(1024)(128)(4,1)} %bitcast.7), calls=%async_computation.2 | async-start | bytes 8388608
  5.8 2.8 %slice-start.3 = ((s8[6291456]{0:T(1024)(128)(4,1)}), s8[2097152]{0:T(1024)(128)(4,1)S(1)}, s32[]{:S(2)}) async-start(s8[6291456]{0:T(1024)(128)(4,1)} %bitcast.7), calls=%async_computation.3 | async-start | bytes 4194304
  6.9 1.3 %collective-permute-start.2 = (bf16[128,128]{1,0:T(8,128)(2,1)S(1)}, bf16[128,128]{1,0:T(8,128)(2,1)S(1)}, u32[]{:S(2)}, u32[]{:S(2)}) collective-permute-start(bf16[128,128]{1,0:T(8,128)(2,1)S(1)} %collective-permute-done.1.refs_2_), channel_id=1, source_target_pairs={{0,1},{1,0},{2,3},{3,2},{4,5},{5,4},{6,7},{7,6},{8,9},{9,8},{10,11... | collective-permute-start | bytes 98312 | tf_op jit(solution)/shard_map/ppermute | solution.py:443
  7.6 20.3 %slice-start = ((s8[8388608]{0:T(1024)(128)(4,1)}), s8[4194304]{0:T(1024)(128)(4,1)S(1)}, s32[]{:S(2)}) async-start(s8[8388608]{0:T(1024)(128)(4,1)} %bitcast.2), calls=%async_computation | async-start | bytes 8388608
  7.6 20.3 %slice-start.1 = ((s8[8388608]{0:T(1024)(128)(4,1)}), s8[4194304]{0:T(1024)(128)(4,1)S(1)}, s32[]{:S(2)}) async-start(s8[8388608]{0:T(1024)(128)(4,1)} %bitcast.2), calls=%async_computation.1 | async-start | bytes 8388608
  7.6 6.5 %collective-permute-start.6 = (bf16[256,128]{1,0:T(8,128)(2,1)S(1)}, bf16[256,128]{1,0:T(8,128)(2,1)S(1)}, u32[]{:S(2)}, u32[]{:S(2)}) collective-permute-start(bf16[256,128]{1,0:T(8,128)(2,1)S(1)} %get-tuple-element.37), channel_id=1, source_target_pairs={{0,1},{1,0},{2,3},{3,2},{4,5},{5,4},{6,7},{7,6},{8,9},{9,8},{10,11... | collective-permute-start | bytes 196616 | tf_op jit(solution)/shard_map/ppermute | solution.py:443
  11.6 3.9 %collective-permute-start.9 = (bf16[152,128]{1,0:T(8,128)(2,1)S(1)}, bf16[152,128]{1,0:T(8,128)(2,1)S(1)}, u32[]{:S(2)}, u32[]{:S(2)}) collective-permute-start(bf16[152,128]{1,0:T(8,128)(2,1)S(1)} %get-tuple-element.41), channel_id=1, source_target_pairs={{0,1},{1,0},{2,3},{3,2},{4,5},{5,4},{6,7},{7,6},{8,9},{9,8},{10,11... | collective-permute-start | bytes 116744 | tf_op jit(solution)/shard_map/ppermute | solution.py:443
  12.2 15.6 %collective-permute-start.3 = (bf16[512,128]{1,0:T(8,128)(2,1)S(1)}, bf16[512,128]{1,0:T(8,128)(2,1)S(1)}, u32[]{:S(2)}, u32[]{:S(2)}) collective-permute-start(bf16[512,128]{1,0:T(8,128)(2,1)S(1)} %get-tuple-element.33), channel_id=1, source_target_pairs={{0,1},{1,0},{2,3},{3,2},{4,5},{5,4},{6,7},{7,6},{8,9},{9,8},{10,11... | collective-permute-start | bytes 393224 | tf_op jit(solution)/shard_map/ppermute | solution.py:443
  12.3 15.6 %collective-permute-start.4 = (bf16[512,128]{1,0:T(8,128)(2,1)S(1)}, bf16[512,128]{1,0:T(8,128)(2,1)S(1)}, u32[]{:S(2)}, u32[]{:S(2)}) collective-permute-start(bf16[512,128]{1,0:T(8,128)(2,1)S(1)} %get-tuple-element.34), channel_id=1, source_target_pairs={{0,2},{1,3},{2,0},{3,1},{4,6},{5,7},{6,4},{7,5},{8,10},{9,11},{10,... | collective-permute-start | bytes 393224 | tf_op jit(solution)/shard_map/ppermute | solution.py:443
  13.8 14.1 %collective-permute-start.5 = (bf16[512,128]{1,0:T(8,128)(2,1)S(1)}, bf16[512,128]{1,0:T(8,128)(2,1)S(1)}, u32[]{:S(2)}, u32[]{:S(2)}) collective-permute-start(bf16[512,128]{1,0:T(8,128)(2,1)S(1)} %get-tuple-element.35), channel_id=1, source_target_pairs={{0,3},{1,2},{2,1},{3,0},{4,7},{5,6},{6,5},{7,4},{8,11},{9,10},{10,... | collective-permute-start | bytes 393224 | tf_op jit(solution)/shard_map/ppermute | solution.py:443
  14.1 8.1 %collective-permute-start.10 = (bf16[152,128]{1,0:T(8,128)(2,1)S(1)}, bf16[152,128]{1,0:T(8,128)(2,1)S(1)}, u32[]{:S(2)}, u32[]{:S(2)}) collective-permute-start(bf16[152,128]{1,0:T(8,128)(2,1)S(1)} %get-tuple-element.42), channel_id=1, source_target_pairs={{0,2},{1,3},{2,0},{3,1},{4,6},{5,7},{6,4},{7,5},{8,10},{9,11},{10,... | collective-permute-start | bytes 116744 | tf_op jit(solution)/shard_map/ppermute | solution.py:443
  15.6 8.1 %collective-permute-start.11 = (bf16[152,128]{1,0:T(8,128)(2,1)S(1)}, bf16[152,128]{1,0:T(8,128)(2,1)S(1)}, u32[]{:S(2)}, u32[]{:S(2)}) collective-permute-start(bf16[152,128]{1,0:T(8,128)(2,1)S(1)} %get-tuple-element.43), channel_id=1, source_target_pairs={{0,3},{1,2},{2,1},{3,0},{4,7},{5,6},{6,5},{7,4},{8,11},{9,10},{10,... | collective-permute-start | bytes 116744 | tf_op jit(solution)/shard_map/ppermute | solution.py:443
  22.2 4.3 %collective-permute-start.7 = (bf16[256,128]{1,0:T(8,128)(2,1)S(1)}, bf16[256,128]{1,0:T(8,128)(2,1)S(1)}, u32[]{:S(2)}, u32[]{:S(2)}) collective-permute-start(bf16[256,128]{1,0:T(8,128)(2,1)S(1)} %get-tuple-element.38), channel_id=1, source_target_pairs={{0,2},{1,3},{2,0},{3,1},{4,6},{5,7},{6,4},{7,5},{8,10},{9,11},{10,... | collective-permute-start | bytes 196616 | tf_op jit(solution)/shard_map/ppermute | solution.py:443
  23.7 4.2 %collective-permute-start.8 = (bf16[256,128]{1,0:T(8,128)(2,1)S(1)}, bf16[256,128]{1,0:T(8,128)(2,1)S(1)}, u32[]{:S(2)}, u32[]{:S(2)}) collective-permute-start(bf16[256,128]{1,0:T(8,128)(2,1)S(1)} %get-tuple-element.39), channel_id=1, source_target_pairs={{0,3},{1,2},{2,1},{3,0},{4,7},{5,6},{6,5},{7,4},{8,11},{9,10},{10,... | collective-permute-start | bytes 196616 | tf_op jit(solution)/shard_map/ppermute | solution.py:443
  31.9 16.5 %collective-permute-start.16 = (bf16[64,2048]{1,0:T(8,128)(2,1)S(1)}, bf16[64,2048]{1,0:T(8,128)(2,1)S(1)}, u32[]{:S(2)}, u32[]{:S(2)}) collective-permute-start(bf16[64,2048]{1,0:T(8,128)(2,1)S(1)} %get-tuple-element.50), channel_id=1, source_target_pairs={{0,1},{1,0},{2,3},{3,2},{4,5},{5,4},{6,7},{7,6},{8,9},{9,8},{10,11... | collective-permute-start | bytes 786440 | tf_op jit(solution)/shard_map/ppermute | solution.py:443
  32.8 16.6 %collective-permute-start.18 = (bf16[64,2048]{1,0:T(8,128)(2,1)S(1)}, bf16[64,2048]{1,0:T(8,128)(2,1)S(1)}, u32[]{:S(2)}, u32[]{:S(2)}) collective-permute-start(bf16[64,2048]{1,0:T(8,128)(2,1)S(1)} %get-tuple-element.53), channel_id=1, source_target_pairs={{0,1},{1,0},{2,3},{3,2},{4,5},{5,4},{6,7},{7,6},{8,9},{9,8},{10,11... | collective-permute-start | bytes 786440 | tf_op jit(solution)/shard_map/ppermute | solution.py:443
  38.6 24.8 %copy-start = (bf16[128,4096]{1,0:T(8,128)(2,1)S(1)}, bf16[128,4096]{1,0:T(8,128)(2,1)}, u32[]{:S(2)}) copy-start(bf16[128,4096]{1,0:T(8,128)(2,1)} %res_ref.5) | copy-start | bytes 3145732
  38.6 24.8 %copy-start.1 = (f32[4096]{0:T(1024)S(1)}, f32[4096]{0:T(1024)}, u32[]{:S(2)}) copy-start(f32[4096]{0:T(1024)} %param.21) | copy-start | bytes 49156
  38.6 12.1 %collective-permute-start.13 = (bf16[64,4096]{1,0:T(8,128)(2,1)S(1)}, bf16[64,4096]{1,0:T(8,128)(2,1)S(1)}, u32[]{:S(2)}, u32[]{:S(2)}) collective-permute-start(bf16[64,4096]{1,0:T(8,128)(2,1)S(1)} %get-tuple-element.48), channel_id=1, source_target_pairs={{0,1},{1,0},{2,3},{3,2},{4,5},{5,4},{6,7},{7,6},{8,9},{9,8},{10,11... | collective-permute-start | bytes 1572872 | tf_op jit(solution)/shard_map/ppermute | solution.py:443
  47.9 15.4 %collective-permute-start.12 = (bf16[128,4096]{1,0:T(8,128)(2,1)S(1)}, bf16[128,4096]{1,0:T(8,128)(2,1)S(1)}, u32[]{:S(2)}, u32[]{:S(2)}) collective-permute-start(bf16[128,4096]{1,0:T(8,128)(2,1)S(1)} %get-tuple-element.46), channel_id=1, source_target_pairs={{0,1},{1,0},{2,3},{3,2},{4,5},{5,4},{6,7},{7,6},{8,9},{9,8},{10,11... | collective-permute-start | bytes 3145736 | tf_op jit(solution)/shard_map/ppermute | solution.py:443
  48.5 9.2 %collective-permute-start.17 = (bf16[64,2048]{1,0:T(8,128)(2,1)S(1)}, bf16[64,2048]{1,0:T(8,128)(2,1)S(1)}, u32[]{:S(2)}, u32[]{:S(2)}) collective-permute-start(bf16[64,2048]{1,0:T(8,128)(2,1)S(1)} %add_convert_fusion.2), channel_id=1, source_target_pairs={{0,2},{1,3},{2,0},{3,1},{4,6},{5,7},{6,4},{7,5},{8,10},{9,11},{10,... | collective-permute-start | bytes 786440 | tf_op jit(solution)/shard_map/ppermute | solution.py:443
  49.4 13.9 %collective-permute-start.19 = (bf16[64,2048]{1,0:T(8,128)(2,1)S(1)}, bf16[64,2048]{1,0:T(8,128)(2,1)S(1)}, u32[]{:S(2)}, u32[]{:S(2)}) collective-permute-start(bf16[64,2048]{1,0:T(8,128)(2,1)S(1)} %add_convert_fusion.1), channel_id=1, source_target_pairs={{0,2},{1,3},{2,0},{3,1},{4,6},{5,7},{6,4},{7,5},{8,10},{9,11},{10,... | collective-permute-start | bytes 786440 | tf_op jit(solution)/shard_map/ppermute | solution.py:443
  50.9 18.1 %collective-permute-start.15 = (bf16[32,4096]{1,0:T(8,128)(2,1)S(1)}, bf16[32,4096]{1,0:T(8,128)(2,1)S(1)}, u32[]{:S(2)}, u32[]{:S(2)}) collective-permute-start(bf16[32,4096]{1,0:T(8,128)(2,1)S(1)} %get-tuple-element.58), channel_id=1, source_target_pairs={{0,2},{1,3},{2,0},{3,1},{4,6},{5,7},{6,4},{7,5},{8,10},{9,11},{10,... | collective-permute-start | bytes 786440 | tf_op jit(solution)/shard_map/ppermute | solution.py:443
  51.7 21.9 %collective-permute-start.14 = (bf16[32,4096]{1,0:T(8,128)(2,1)S(1)}, bf16[32,4096]{1,0:T(8,128)(2,1)S(1)}, u32[]{:S(2)}, u32[]{:S(2)}) collective-permute-start(bf16[32,4096]{1,0:T(8,128)(2,1)S(1)} %get-tuple-element.59), channel_id=1, source_target_pairs={{0,2},{1,3},{2,0},{3,1},{4,6},{5,7},{6,4},{7,5},{8,10},{9,11},{10,... | collective-permute-start | bytes 786440 | tf_op jit(solution)/shard_map/ppermute | solution.py:443

commit v4 on v3

--- a/solution.py
+++ b/solution.py
@@ -13,6 +13,7 @@
 CHUNKS = (64, 64)
 COLUMNS = 512
 GROUP_ROWS = 256
+PIPE, ONES, SPLITQ = True, True, True
 
 F32 = jnp.float32
 BF16 = jnp.bfloat16
@@ -50,21 +51,22 @@
     return pltpu.CompilerParams(vmem_limit_bytes=mib << 20, **kwargs)
 
 
-def pack_history(history, queries, devices, local_heads, group):
+def pack_history(history, queries, slots, local_heads, group):
     h_rows = history.shape[1]
     rows = queries.shape[0]
+    devices = len(slots)
 
     def body(h_hbm, q_hbm, *refs):
         o_refs, q_ref, sem = refs[:devices], refs[devices], refs[devices + 1]
         me = lax.axis_index("tp")
         copies = []
-        for k in range(devices):
+        for i, k in enumerate(slots):
             lane = pl.multiple_of((me ^ k) * local_heads // group * HEAD_DIM, HEAD_DIM)
             for part in range(2):
                 copies.append(
                     pltpu.make_async_copy(
                         h_hbm.at[part, :, pl.ds(lane, HEAD_DIM)],
-                        o_refs[k].at[part * h_rows : (part + 1) * h_rows, :],
+                        o_refs[i].at[part * h_rows : (part + 1) * h_rows, :],
                         sem.at[len(copies)],
                     )
                 )
@@ -92,41 +94,69 @@
         cost_estimate=busy(6),
         name="pack_history",
     )(to_hbm(history), to_hbm(queries))
-    return outs[:devices], outs[devices]
-
-
-def pack_fresh(prompt, meta, devices, local_heads, group):
-    p_rows = prompt.shape[1]
+    return dict(zip(slots, outs)), outs[devices]
+
+
+def pack_fresh(prompt, history, queries, meta, slots, local_heads, group):
+    h_rows, p_rows = history.shape[1], prompt.shape[1]
     p_pad = round_up(p_rows, 16)
+    q_rows = queries[0].shape[0]
+    every = [1] + slots
+    n = len(every)
 
     def head_of(k):
         return lambda i, m: (0, 0, (m[0] ^ k) * local_heads // group)
 
     def body(m, *refs):
-        for k in range(devices):
-            p_ref, o_ref = refs[k], refs[devices + k]
+        p_refs, refs = refs[:n], refs[n:]
+        h_hbm, refs = refs[0], refs[1:]
+        q_refs, refs = refs[: len(queries)], refs[len(queries) :]
+        o_refs, sem = refs[:n], refs[n]
+        lane = pl.multiple_of((m[0] ^ 1) * local_heads // group * HEAD_DIM, HEAD_DIM)
+        copies = [
+            pltpu.make_async_copy(
+                h_hbm.at[part, :, pl.ds(lane, HEAD_DIM)],
+                o_refs[0].at[part * h_rows : (part + 1) * h_rows, :],
+                sem.at[part],
+            )
+            for part in range(2)
+        ]
+        for copy in copies:
+            copy.start()
+        for i in range(n):
+            row = 2 * h_rows if i == 0 else 0
             for part in range(2):
                 if p_pad > p_rows:
                     fresh = jnp.concatenate(
-                        [p_ref[part].astype(F32), jnp.zeros((p_pad - p_rows, HEAD_DIM), F32)], axis=0
+                        [p_refs[i][part].astype(F32), jnp.zeros((p_pad - p_rows, HEAD_DIM), F32)], axis=0
                     ).astype(BF16)
                 else:
-                    fresh = p_ref[part]
-                o_ref[part * p_pad : (part + 1) * p_pad, :] = fresh
-
-    return pl.pallas_call(
+                    fresh = p_refs[i][part]
+                o_refs[i][row + part * p_pad : row + (part + 1) * p_pad, :] = fresh
+        row = 2 * (h_rows + p_pad)
+        for i, q_ref in enumerate(q_refs):
+            o_refs[0][row + i * q_rows : row + (i + 1) * q_rows, :] = q_ref[...]
+        for copy in copies:
+            copy.wait()
+
+    sizes = [2 * (h_rows + p_pad) + len(queries) * q_rows] + [2 * p_pad] * len(slots)
+    outs = pl.pallas_call(
         body,
         grid_spec=pltpu.PrefetchScalarGridSpec(
             num_scalar_prefetch=1,
             grid=(1,),
-            in_specs=[pl.BlockSpec((2, p_rows, HEAD_DIM), head_of(k)) for k in range(devices)],
-            out_specs=[pl.BlockSpec((2 * p_pad, HEAD_DIM), lambda i, m: (0, 0))] * devices,
+            in_specs=[pl.BlockSpec((2, p_rows, HEAD_DIM), head_of(k)) for k in every]
+            + [in_hbm()]
+            + [in_vmem()] * len(queries),
+            out_specs=[in_vmem()] * n,
+            scratch_shapes=[pltpu.SemaphoreType.DMA((2,))],
         ),
-        out_shape=[jax.ShapeDtypeStruct((2 * p_pad, HEAD_DIM), BF16)] * devices,
+        out_shape=[jax.ShapeDtypeStruct((size, HEAD_DIM), BF16) for size in sizes],
         compiler_params=params(8),
         cost_estimate=busy(12),
         name="pack_fresh",
-    )(meta, *([prompt] * devices))
+    )(meta, *([prompt] * n), to_hbm(history), *queries)
+    return outs[0], dict(zip(slots, outs[1:]))
 
 
 def split(value):
@@ -137,8 +167,8 @@
     return terms
 
 
-def decode_partials(queries, cache, prompt_queries, decode_queries, entries, meta, local_heads, group):
-    devices = len(queries)
+def decode_partials(queries, bundle, cache, prompt_queries, decode_queries, entries, meta, local_heads, group):
+    devices = 2 * len(queries)
     rows, span, width = cache.shape[1], cache.shape[2], cache.shape[3]
     kv_heads = width // HEAD_DIM
     heads = devices * local_heads
@@ -148,9 +178,9 @@
     prompt_rows = prompt_queries.shape[0]
 
     def body(m, *refs):
-        q_refs, refs = refs[:devices], refs[devices:]
-        cache_ref, pq_hbm, dq_hbm, e_hbm = refs[:4]
-        o_refs, refs = refs[4 : 4 + devices], refs[4 + devices :]
+        q_refs, refs = refs[: devices // 2], refs[devices // 2 :]
+        bundle_ref, cache_ref, pq_hbm, dq_hbm, e_hbm = refs[:5]
+        o_refs, refs = refs[5 : 5 + devices], refs[5 + devices :]
         q_ref, e_ref, q_all, sums, sem = refs
         me = m[0]
         lane = pl.multiple_of(me * local_heads // group * HEAD_DIM, HEAD_DIM)
@@ -162,8 +192,11 @@
         for copy in copies:
             copy.start()
         for k in range(devices):
+            base = bundle.shape[0] - (devices // 2 - k // 2) * part_rows if k % 2 else 0
+            q_ref_k = bundle_ref if k % 2 else q_refs[k // 2]
             for h in range(local_heads):
-                q_all[k, pl.ds(h, rows, stride=local_heads), :] = q_refs[k][h * rows : (h + 1) * rows, :].astype(F32)
+                row = base + h * rows
+                q_all[k, pl.ds(h, rows, stride=local_heads), :] = q_ref_k[row : row + rows, :].astype(F32)
 
         slot = lax.broadcasted_iota(jnp.int32, (heads, 1), 0) // local_heads
         reads = ((slot ^ me) * local_heads) // group
@@ -206,7 +239,7 @@
 
     outs = pl.pallas_call(
         body,
-        in_specs=[smem()] + [in_vmem()] * (devices + 1) + [in_hbm()] * 3,
+        in_specs=[smem()] + [in_vmem()] * (devices // 2 + 2) + [in_hbm()] * 3,
         out_specs=[in_vmem()] * (devices + 2),
         scratch_shapes=[pltpu.VMEM((devices, part_rows, HEAD_DIM), F32)] * 2 + [pltpu.SemaphoreType.DMA((3,))],
         out_shape=[jax.ShapeDtypeStruct((part_rows + 3 * stat_rows, HEAD_DIM), BF16)] * devices
@@ -217,7 +250,7 @@
         compiler_params=params(12),
         cost_estimate=busy(12),
         name="decode",
-    )(meta, *queries, cache, to_hbm(prompt_queries), to_hbm(decode_queries), to_hbm(entries))
+    )(meta, *queries, bundle, cache, to_hbm(prompt_queries), to_hbm(decode_queries), to_hbm(entries))
     return outs[:devices], outs[devices], outs[devices + 1]
 
 
@@ -294,8 +327,9 @@
     )(att, weight)
 
 
-def attend(slots, first, count, block, queries, history, fresh, decoded, weight, meta, h_rows, p_rows, columns):
-    devices = len(history)
+def attend(slots, first, count, block, queries, history, fresh, bundle, decoded, weight, meta, h_rows, p_rows, columns):
+    devices = len(history) + 1
+    held = list(history)
     p_pad = fresh[0].shape[0] // 2
     local_width = queries.shape[1]
     local_heads = local_width // HEAD_DIM
@@ -310,73 +344,101 @@
     decode_rows = decoded.shape[0] if has_decode else 0
 
     def body(m, q, *refs):
-        h_refs, f_refs = refs[:devices], refs[devices : 2 * devices]
-        rest = refs[2 * devices :]
+        bundle_ref, rest = refs[0], refs[1:]
+        n = devices - 1
+        cached = {1: (bundle_ref, 0), **{k: (ref, 0) for k, ref in zip(held, rest[:n])}}
+        own = {1: (bundle_ref, 2 * h_rows), **{k: (ref, 0) for k, ref in zip(held, rest[n : 2 * n])}}
+        rest = rest[2 * n :]
         if has_decode:
             dec_ref, rest = rest[0], rest[1:]
         w, keep_ref, give_ref, att, k_all, v_all = rest
         me, valid_rows = m[0], m[1]
         for k in range(devices):
             for part, dst in ((0, k_all), (1, v_all)):
-                dst[k * h_rows : (k + 1) * h_rows, :] = h_refs[k][part * h_rows : (part + 1) * h_rows, :]
-                dst[h_keys + k * p_pad : h_keys + (k + 1) * p_pad, :] = f_refs[k][
-                    part * p_pad : (part + 1) * p_pad, :
-                ]
+                for copy in range(2 if SPLITQ and part == 0 else 1):
+                    lanes = slice(copy * HEAD_DIM, (copy + 1) * HEAD_DIM)
+                    ref, row = cached[k]
+                    row += part * h_rows
+                    dst[k * h_rows : (k + 1) * h_rows, lanes] = ref[row : row + h_rows, :]
+                    ref, row = own[k]
+                    row += part * p_pad
+                    dst[h_keys + k * p_pad : h_keys + (k + 1) * p_pad, lanes] = ref[row : row + p_pad, :]
+        if ONES:
+            v_all[:, HEAD_DIM:] = jnp.ones((keys, HEAD_DIM), BF16)
         column = lax.broadcasted_iota(jnp.int32, (1, h_keys), 1)
         place = ((column // h_rows) ^ me) * h_rows + column % h_rows
         history_bias = jnp.where(place < valid_rows, 0.0, MASKED)
         column = lax.broadcasted_iota(jnp.int32, (1, p_keys), 1)
         inner = column % p_pad
         seen_from = jnp.where(inner < p_rows, ((column // p_pad) ^ me) * p_rows + inner, 1 << 20)
+        steps = [(i, g) for i in range(len(order)) for g in range(0, local_heads, per)]
+        biases = []
         for i, slot in enumerate(order):
-            target = slot ^ me
-            row0 = pl.multiple_of(target * block + first, 16)
-            rows = row0 + lax.broadcasted_iota(jnp.int32, (count, 1), 0)
+            rows = (slot ^ me) * block + first + lax.broadcasted_iota(jnp.int32, (count, 1), 0)
             bias = jnp.where(seen_from <= rows, 0.0, MASKED)
-            bias = jnp.concatenate([jnp.broadcast_to(history_bias, (count, h_keys)), bias], axis=1)
-            bias = jnp.concatenate([bias] * per, axis=0)
-            for g in range(0, local_heads, per):
-                stacked = jnp.concatenate(
-                    [q[pl.ds(row0, count), h * HEAD_DIM : (h + 1) * HEAD_DIM] for h in range(g, g + per)], axis=0
-                )
-                scores = lax.dot_general(
-                    stacked, k_all[...], (((1,), (1,)), ((), ())), preferred_element_type=F32
-                )
-                scores = scores + bias
-                top = jnp.max(scores, axis=-1, keepdims=True)
-                weights = jnp.exp2((scores - top) * factor)
+            biases.append(jnp.concatenate([jnp.broadcast_to(history_bias, (count, h_keys)), bias], axis=1))
+
+        def scores_of(i, g):
+            row0 = pl.multiple_of((order[i] ^ me) * block + first, 16)
+            stacked = jnp.concatenate(
+                [q[pl.ds(row0, count), h * HEAD_DIM : (h + 1) * HEAD_DIM] for h in range(g, g + per)], axis=0
+            )
+            if SPLITQ:
+                scaled = stacked.astype(F32) * factor
+                high = scaled.astype(BF16)
+                low = (scaled - high.astype(F32)).astype(BF16)
+                stacked = jnp.concatenate([high, low], axis=1)
+            scores = lax.dot_general(
+                stacked, k_all[...], (((1,), (1,)), ((), ())), preferred_element_type=F32
+            )
+            return (scores.reshape(per, count, keys) + biases[i][None]).reshape(per * count, keys)
+
+        ahead = scores_of(*steps[0])
+        for t, (i, g) in enumerate(steps):
+            scores = ahead
+            if PIPE and t + 1 < len(steps):
+                ahead = scores_of(*steps[t + 1])
+            top = jnp.max(scores, axis=-1, keepdims=True)
+            weights = jnp.exp2(scores - top) if SPLITQ else jnp.exp2((scores - top) * factor)
+            if not ONES:
                 total = jnp.sum(weights, axis=-1, keepdims=True)
-                summed = jnp.dot(weights.astype(BF16), v_all[...], preferred_element_type=F32)
-                summed = (summed / total).astype(BF16)
-                for h in range(per):
-                    att[i * count : (i + 1) * count, (g + h) * HEAD_DIM : (g + h + 1) * HEAD_DIM] = summed[
-                        h * count : (h + 1) * count
-                    ]
-            if has_decode:
-
-                @pl.when(target == devices - 1)
+            summed = jnp.dot(weights.astype(BF16), v_all[...], preferred_element_type=F32)
+            if ONES:
+                total = summed[:, HEAD_DIM:]
+                summed = summed[:, :HEAD_DIM]
+            summed = (summed / total).astype(BF16)
+            for h in range(per):
+                att[i * count : (i + 1) * count, (g + h) * HEAD_DIM : (g + h + 1) * HEAD_DIM] = summed[
+                    h * count : (h + 1) * count
+                ]
+            if not PIPE and t + 1 < len(steps):
+                ahead = scores_of(*steps[t + 1])
+        if has_decode:
+            for i, slot in enumerate(order):
+
+                @pl.when(slot ^ me == devices - 1)
                 def _():
                     att[(i + 1) * count - decode_rows : (i + 1) * count, :] = dec_ref[...]
 
         product(att, w, 0, columns, half, keep_ref, give_ref)
 
     flops = 2 * len(order) * count * (2 * local_width * keys + local_width * model)
-    n_vmem = 2 + 2 * devices + has_decode
+    n_vmem = 1 + 2 * devices + has_decode
     return pl.pallas_call(
         body,
         in_specs=[smem()] + [in_vmem()] * n_vmem,
         out_specs=[in_vmem()] * 3,
         out_shape=[jax.ShapeDtypeStruct((half, columns), BF16)] * 2 + [pltpu.VMEM((2 * half, local_width), BF16)],
         scratch_shapes=[
-            pltpu.VMEM((keys, HEAD_DIM), BF16),
-            pltpu.VMEM((keys, HEAD_DIM), BF16),
+            pltpu.VMEM((keys, HEAD_DIM * (2 if SPLITQ else 1)), BF16),
+            pltpu.VMEM((keys, HEAD_DIM * (2 if ONES else 1)), BF16),
         ],
         compiler_params=params(24),
         cost_estimate=pl.CostEstimate(flops=flops, transcendentals=0, bytes_accessed=weight.size * 2),
-    )(meta, queries, *history, *fresh, *([decoded] if has_decode else []), weight)
-
-
-def finish(first, residual, own, given, crossed, gain, previous):
+    )(meta, queries, bundle, *history.values(), *fresh.values(), *([decoded] if has_decode else []), weight)
+
+
+def finish(first, begin, residual, own, given, crossed, gain, previous):
     block, model = residual.shape
     count = crossed[0].shape[0]
     tile = 16
@@ -391,7 +453,8 @@
         copies = []
         for i in range(0, count, tile):
             here, local = slice(first + i, first + i + tile), slice(i, i + tile)
-            hidden = res_ref[here, :].astype(F32) + own_ref[here, :].astype(F32) + given_ref[here, :].astype(F32)
+            mine = slice(begin + i, begin + i + tile)
+            hidden = res_ref[here, :].astype(F32) + own_ref[mine, :].astype(F32) + given_ref[mine, :].astype(F32)
             for c in range(0, n_cross, n_columns):
                 pieces = [piece[local, :].astype(F32) for piece in cross[c : c + n_columns]]
                 hidden = hidden + (jnp.concatenate(pieces, axis=1) if n_columns > 1 else pieces[0])
@@ -445,25 +508,23 @@
     def swapped(values):
         return [values[0]] + [swap(values[k], k) for k in range(1, devices)]
 
-    packed, own_query = pack_history(history_cache, decode_queries, devices, local_heads, group)
-    decode_rows = {0: own_query}
-    for k in range(2, devices, 2):
-        decode_rows[k] = swap(own_query, k)
-    for k in range(1, devices, 2):
-        decode_rows[k] = swap(decode_rows[k ^ 1], 1)
-    history = swapped(packed)
+    slots = [0] + list(range(2, devices))
+    packed, own_query = pack_history(history_cache, decode_queries, slots, local_heads, group)
+    even_queries = [own_query] + [swap(own_query, k) for k in range(2, devices, 2)]
+    history = {k: swap(packed[k], k) if k else packed[k] for k in slots}
     meta = jnp.concatenate([lax.axis_index("tp").astype(jnp.int32)[None], prompt_start, decode_lengths])
-    fresh = swapped(pack_fresh(prompt_entries, meta, devices, local_heads, group))
-    ordered = [decode_rows[k] for k in range(devices)]
+    bundle, packed = pack_fresh(prompt_entries, history_cache, even_queries, meta, slots, local_heads, group)
+    bundle = swap(bundle, 1)
+    fresh = {k: swap(packed[k], k) if k else packed[k] for k in slots}
     parts, queries, entries = decode_partials(
-        ordered, decode_cache, prompt_queries, decode_queries, decode_entries, meta, local_heads, group
+        even_queries, bundle, decode_cache, prompt_queries, decode_queries, decode_entries, meta, local_heads, group
     )
     parts = swapped(parts)
     decoded = decode_join(parts, own_query, entries, local_heads)
 
     def attended(slots, first, count, decoded, columns):
         return attend(
-            slots, first, count, block, queries, history, fresh, decoded, out_weight, meta, h_rows, p_rows, columns
+            slots, first, count, block, queries, history, fresh, bundle, decoded, out_weight, meta, h_rows, p_rows, columns
         )
 
     def chip_sum(keep, give):
@@ -497,12 +558,17 @@
             pieces.append(cross(pair, count, 0, count))
             crossed.append((first, [piece for both in zip(*pieces) for piece in both]))
         first += count
-    own, give, _ = attended([0, 1], 0, block, decoded, model)
-    given = swap(give, 1)
+    owned, first = [], 0
+    for count in chunks:
+        here = decoded if first + count == block else None
+        own, give, _ = attended([0, 1], first, count, here, model)
+        owned.append((first, own, swap(give, 1)))
+        first += count
     gain = norm_gain[None, :]
     outs = []
     for first, pieces in crossed:
-        outs = finish(first, residual, own, given, pieces, gain, outs)
+        begin, own, given = [o for o in owned if o[0] <= first][-1]
+        outs = finish(first, first - begin, residual, own, given, pieces, gain, outs)
     return tuple(outs)
 
 

time: 75 us -> 68.6 us (0.915)
  waiting for transfers between devices: 28.8 us -> 21.5 us
  starting transfers between devices: 14.7 us -> 16.3 us
    ppermute x20 -> x18, waiting for transfers between devices: 28.8 us -> 21.5 us  [swap(): return lax.ppermute(value, 'tp', [(i, i ^ k) for i in range(devices)])]
    pallas_call x3 -> x4, Pallas kernels: 18.5 us -> 16.8 us  [attend(): pl.pallas_call(body, in_specs=[smem()] + [in_vmem()] * n_vmem, out_specs=...]
    ppermute x20 -> x18, starting transfers between devices: 14.7 us -> 16.3 us  [swap(): return lax.ppermute(value, 'tp', [(i, i ^ k) for i in range(devices)])]
    pallas_call x1, Pallas kernels: 0.64 us -> 1.6 us  [pack_fresh(): pl.pallas_call(body, grid_spec=pltpu.PrefetchScalarGridSpec(num_scalar_pr...]
  transfers between devices with their start and end apart: 20 -> 18, of which waited for: 8 -> 6; matrix products, arithmetic and copies ran while one was open for 1% -> 1% of each run, Pallas kernels for 30% -> 36%
where the time goes in v4:
time: 68.6 us; the launch traced here: 68.3 us
  Pallas kernels  28.4 us (41%)
  waiting for transfers between devices  21.5 us (31%)
  starting transfers between devices  16.3 us (24%)
  between operations  1.67 us (2%)
    ppermute x18, waiting for transfers between devices, swap(): return lax.ppermute(value, 'tp', [(i, i ^ k) for i in range(devices)])  21.5 us
    pallas_call x4, Pallas kernels, attend(): pl.pallas_call(body, in_specs=[smem()] + [in_vmem()] * n_vmem, out_specs=...  16.8 us
    ppermute x18, starting transfers between devices, swap(): return lax.ppermute(value, 'tp', [(i, i ^ k) for i in range(devices)])  16.3 us
    pallas_call x1, Pallas kernels, decode_partials(): pl.pallas_call(body, in_specs=[smem()] + [in_vmem()] * (devices // 2 + 2)...  3.5 us
    pallas_call x3, Pallas kernels, finish(): pl.pallas_call(body, in_specs=[in_vmem()] * n_in + [hbm()] * len(previous...  3.39 us
    pallas_call x1, Pallas kernels, pack_fresh(): pl.pallas_call(body, grid_spec=pltpu.PrefetchScalarGridSpec(num_scalar_pr...  1.6 us
  transfers between devices with their start and end apart: 18, of which 6 were waited for; matrix products, arithmetic and copies ran while one was open for 1% of the time, Pallas kernels for 36%

profile of v4, /device:TPU:0, one launch (start us, length us, event | category | flops | bytes accessed | tf_op | source)
XLA Modules:
  0.0 68.3 jit_solution(8808770097211310569)
XLA Ops:
  0.6 1.2 %pack_history.1 = (bf16[512,128]{1,0:T(8,128)(2,1)S(1)}, bf16[512,128]{1,0:T(8,128)(2,1)S(1)}, bf16[512,128]{1,0:T(8,128)(2,1)S(1)}, bf16[128,128]{1,0:T(8,128)(2,1)S(1)}) custom-call(bf16[2,256,512]{2,1,0:T(8,128)(2,1)} %refs_4_.2, bf16[16,1024]{1,0:T(8,128)(2,1)} %refs_5_.1), custom_call_target="tpu_custom_call" | custom-call | flops 3000000000 | bytes 6000000 | tf_op jit(solution)/shard_map/pack_history/pallas_call | solution.py:86
  1.9 3.1 %collective-permute-start = (bf16[128,128]{1,0:T(8,128)(2,1)S(1)}, bf16[128,128]{1,0:T(8,128)(2,1)S(1)}, u32[]{:S(2)}, u32[]{:S(2)}) collective-permute-start(bf16[128,128]{1,0:T(8,128)(2,1)S(1)} %get-tuple-element.31.refs_5_.refs_0_.refs_4_), channel_id=1, source_target_pairs={{0,2},{1,3},{2,0},{3,1},{4,6},{5,7},{6,4},{7,5},{8,10},{9,11},{10,... | collective-permute-start | bytes 98312 | tf_op jit(solution)/shard_map/ppermute | solution.py:506
  5.7 1.1 %collective-permute-done.refs_6_.refs_1_ = bf16[128,128]{1,0:T(8,128)(2,1)S(1)} collective-permute-done((bf16[128,128]{1,0:T(8,128)(2,1)S(1)}, bf16[128,128]{1,0:T(8,128)(2,1)S(1)}, u32[]{:S(2)}, u32[]{:S(2)}) %collective-permute-start) | collective-permute-done | bytes 32800 | tf_op jit(solution)/shard_map/ppermute | solution.py:506
  6.8 1.6 %pack_fresh.1 = (bf16[1024,128]{1,0:T(8,128)(2,1)S(1)}, bf16[256,128]{1,0:T(8,128)(2,1)S(1)}, bf16[256,128]{1,0:T(8,128)(2,1)S(1)}, bf16[256,128]{1,0:T(8,128)(2,1)S(1)}) custom-call(s32[18]{0:T(128)S(1)} %pad_add_fusion.m, bf16[2,124,512]{2,1,0:T(8,128)(2,1)S(1)} %copy.17.refs_0_.refs_1_.refs_2_.refs_3_, ...), custom_call_target="tpu_custom_call" | custom-call | flops 6000000000 | bytes 12000000 | tf_op jit(solution)/shard_map/pack_fresh/pallas_call | solution.py:143
  8.5 2.0 %collective-permute-start.2 = (bf16[512,128]{1,0:T(8,128)(2,1)S(1)}, bf16[512,128]{1,0:T(8,128)(2,1)S(1)}, u32[]{:S(2)}, u32[]{:S(2)}) collective-permute-start(bf16[512,128]{1,0:T(8,128)(2,1)S(1)} %get-tuple-element.35), channel_id=1, source_target_pairs={{0,2},{1,3},{2,0},{3,1},{4,6},{5,7},{6,4},{7,5},{8,10},{9,11},{10,... | collective-permute-start | bytes 393224 | tf_op jit(solution)/shard_map/ppermute | solution.py:506
  10.5 1.7 %collective-permute-start.4 = (bf16[256,128]{1,0:T(8,128)(2,1)S(1)}, bf16[256,128]{1,0:T(8,128)(2,1)S(1)}, u32[]{:S(2)}, u32[]{:S(2)}) collective-permute-start(bf16[256,128]{1,0:T(8,128)(2,1)S(1)} %get-tuple-element.38), channel_id=1, source_target_pairs={{0,2},{1,3},{2,0},{3,1},{4,6},{5,7},{6,4},{7,5},{8,10},{9,11},{10,... | collective-permute-start | bytes 196616 | tf_op jit(solution)/shard_map/ppermute | solution.py:506
  12.3 3.5 %decode.1 = (bf16[152,128]{1,0:T(8,128)(2,1)S(1)}, bf16[152,128]{1,0:T(8,128)(2,1)S(1)}, bf16[152,128]{1,0:T(8,128)(2,1)S(1)}, bf16[152,128]{1,0:T(8,128)(2,1)S(...) custom-call(s32[18]{0:T(128)S(1)} %pad_add_fusion.m, ...), custom_call_target="tpu_custom_call" | custom-call | flops 6000000000 | bytes 12000000 | tf_op jit(solution)/shard_map/decode/pallas_call | solution.py:240
  15.8 0.2 collective-permute-start.6
  16.0 3.2 %collective-permute-done.4.refs_5_ = bf16[256,128]{1,0:T(8,128)(2,1)S(1)} collective-permute-done((bf16[256,128]{1,0:T(8,128)(2,1)S(1)}, bf16[256,128]{1,0:T(8,128)(2,1)S(1)}, u32[]{:S(2)}, u32[]{:S(2)}) %collective-permute-start.4) | collective-permute-done | bytes 65568 | tf_op jit(solution)/shard_map/ppermute | solution.py:506
  19.2 1.9 %collective-permute-start.7 = (bf16[152,128]{1,0:T(8,128)(2,1)S(1)}, bf16[152,128]{1,0:T(8,128)(2,1)S(1)}, u32[]{:S(2)}, u32[]{:S(2)}) collective-permute-start(bf16[152,128]{1,0:T(8,128)(2,1)S(1)} %get-tuple-element.42), channel_id=1, source_target_pairs={{0,2},{1,3},{2,0},{3,1},{4,6},{5,7},{6,4},{7,5},{8,10},{9,11},{10,... | collective-permute-start | bytes 116744 | tf_op jit(solution)/shard_map/ppermute | solution.py:506
  21.1 0.3 collective-permute-start.8
  21.4 3.5 %shard_map.125 = (bf16[64,2048]{1,0:T(8,128)(2,1)S(1)}, bf16[64,2048]{1,0:T(8,128)(2,1)S(1)}, bf16[128,1024]{1,0:T(8,128)(2,1)S(1)}) custom-call(s32[18]{0:T(128)S(1)} %pad_add_fusion.m, bf16[512,1024]{1,0:T(8,128)(2,1)S(1)} %get-tuple-element.33.q, bf16[1024,128]{1,0:T(8,128)(2,1)S(1)} %collective-permute-done.1.refs_2_.refs_0_, ...), custom_call_target="tpu_custom_call" | custom-call | flops 1879048192 | bytes 8388608 | tf_op jit(solution)/shard_map/pallas_call | solution.py:427
  24.9 0.2 collective-permute-start.14
  25.1 0.7 %project.1 = (bf16[64,2048]{1,0:T(8,128)(2,1)S(1)}, bf16[64,2048]{1,0:T(8,128)(2,1)S(1)}) custom-call(bf16[128,1024]{1,0:T(8,128)(2,1)S(1)} %get-tuple-element.53.att_ref, bf16[1024,4096]{1,0:T(8,128)(2,1)S(1)} %bitcast.3), custom_call_target="tpu_custom_call" | custom-call | flops 1000000000 | bytes 2000000 | tf_op jit(solution)/shard_map/project/pallas_call | solution.py:319
  25.9 0.4 collective-permute-start.16
  26.3 4.6 %shard_map.124 = (bf16[64,4096]{1,0:T(8,128)(2,1)S(1)}, bf16[64,4096]{1,0:T(8,128)(2,1)S(1)}, bf16[128,1024]{1,0:T(8,128)(2,1)}) custom-call(s32[18]{0:T(128)S(1)} %pad_add_fusion.m, bf16[512,1024]{1,0:T(8,128)(2,1)S(1)} %get-tuple-element.33.q, bf16[1024,128]{1,0:T(8,128)(2,1)S(1)} %collective-permute-done.1.refs_2_.refs_0_, ...), custom_call_target="tpu_custom_call" | custom-call | flops 1879048192 | bytes 8388608 | tf_op jit(solution)/shard_map/pallas_call | solution.py:427
  31.1 1.2 %join.1.refs_7_ = bf16[16,1024]{1,0:T(8,128)(2,1)S(1)} custom-call(bf16[152,128]{1,0:T(8,128)(2,1)S(1)} %get-tuple-element.40.refs_0_, bf16[152,128]{1,0:T(8,128)(2,1)S(1)} %collective-permute-done.6.refs_1_, bf16[152,128]{1,0:T(8,128)(2,1)S(1)} %collective-permute-done.7.refs_2_, bf16[152,128]{1,0:T(8,128)(2,1)S(1)} %collective-permute-done.8.refs_3_, ...), custom_call_target="tpu_custom_call" | custom-call | flops 500000000 | bytes 1000000 | tf_op jit(solution)/shard_map/join/pallas_call | solution.py:294
  32.3 4.4 %shard_map.123 = (bf16[64,4096]{1,0:T(8,128)(2,1)S(1)}, bf16[64,4096]{1,0:T(8,128)(2,1)S(1)}, bf16[128,1024]{1,0:T(8,128)(2,1)}) custom-call(s32[18]{0:T(128)S(1)} %pad_add_fusion.m, bf16[512,1024]{1,0:T(8,128)(2,1)S(1)} %get-tuple-element.33.q, bf16[1024,128]{1,0:T(8,128)(2,1)S(1)} %collective-permute-done.1.refs_2_.refs_0_, ...), custom_call_target="tpu_custom_call" | custom-call | flops 1879048192 | bytes 8388608 | tf_op jit(solution)/shard_map/pallas_call | solution.py:427
  36.7 0.4 collective-permute-start.10
  37.1 4.2 %shard_map.122 = (bf16[64,4096]{1,0:T(8,128)(2,1)S(1)}, bf16[64,4096]{1,0:T(8,128)(2,1)S(1)}, bf16[128,1024]{1,0:T(8,128)(2,1)}) custom-call(s32[18]{0:T(128)S(1)} %pad_add_fusion.m, bf16[512,1024]{1,0:T(8,128)(2,1)S(1)} %get-tuple-element.33.q, bf16[1024,128]{1,0:T(8,128)(2,1)S(1)} %collective-permute-done.1.refs_2_.refs_0_, ...), custom_call_target="tpu_custom_call" | custom-call | flops 1879048192 | bytes 8388608 | tf_op jit(solution)/shard_map/pallas_call | solution.py:427
  41.4 0.2 collective-permute-start.9
  41.7 1.8 %collective-permute-start.15 = (bf16[64,2048]{1,0:T(8,128)(2,1)S(1)}, bf16[64,2048]{1,0:T(8,128)(2,1)S(1)}, u32[]{:S(2)}, u32[]{:S(2)}) collective-permute-start(bf16[64,2048]{1,0:T(8,128)(2,1)S(1)} %add_convert_fusion.2), channel_id=1, source_target_pairs={{0,2},{1,3},{2,0},{3,1},{4,6},{5,7},{6,4},{7,5},{8,10},{9,11},{10,... | collective-permute-start | bytes 786440 | tf_op jit(solution)/shard_map/ppermute | solution.py:506
  43.5 0.4 collective-permute-start.17
  44.1 1.8 %collective-permute-start.12 = (bf16[32,4096]{1,0:T(8,128)(2,1)S(1)}, bf16[32,4096]{1,0:T(8,128)(2,1)S(1)}, u32[]{:S(2)}, u32[]{:S(2)}) collective-permute-start(bf16[32,4096]{1,0:T(8,128)(2,1)S(1)} %get-tuple-element.60), channel_id=1, source_target_pairs={{0,2},{1,3},{2,0},{3,1},{4,6},{5,7},{6,4},{7,5},{8,10},{9,11},{10,... | collective-permute-start | bytes 786440 | tf_op jit(solution)/shard_map/ppermute | solution.py:506
  45.9 5.1 %collective-permute-done.15.refs_0_ = bf16[64,2048]{1,0:T(8,128)(2,1)S(1)} collective-permute-done((bf16[64,2048]{1,0:T(8,128)(2,1)S(1)}, bf16[64,2048]{1,0:T(8,128)(2,1)S(1)}, u32[]{:S(2)}, u32[]{:S(2)}) %collective-permute-start.15) | collective-permute-done | bytes 262176 | tf_op jit(solution)/shard_map/ppermute | solution.py:506
  50.9 1.7 %collective-permute-start.11 = (bf16[32,4096]{1,0:T(8,128)(2,1)S(1)}, bf16[32,4096]{1,0:T(8,128)(2,1)S(1)}, u32[]{:S(2)}, u32[]{:S(2)}) collective-permute-start(bf16[32,4096]{1,0:T(8,128)(2,1)S(1)} %get-tuple-element.61), channel_id=1, source_target_pairs={{0,2},{1,3},{2,0},{3,1},{4,6},{5,7},{6,4},{7,5},{8,10},{9,11},{10,... | collective-permute-start | bytes 786440 | tf_op jit(solution)/shard_map/ppermute | solution.py:506
  52.6 3.9 %collective-permute-done.17.refs_1_ = bf16[64,2048]{1,0:T(8,128)(2,1)S(1)} collective-permute-done((bf16[64,2048]{1,0:T(8,128)(2,1)S(1)}, bf16[64,2048]{1,0:T(8,128)(2,1)S(1)}, u32[]{:S(2)}, u32[]{:S(2)}) %collective-permute-start.17) | collective-permute-done | bytes 262176 | tf_op jit(solution)/shard_map/ppermute | solution.py:506
  56.6 1.4 %shard_map.126 = (bf16[128,4096]{1,0:T(8,128)(2,1)}, bf16[128,4096]{1,0:T(8,128)(2,1)}) custom-call(bf16[128,4096]{1,0:T(8,128)(2,1)S(1)} %copy-done, bf16[64,4096]{1,0:T(8,128)(2,1)S(1)} %get-tuple-element.49.own_ref, bf16[64,4096]{1,0:T(8,128)(2,1)S(1)} %collective-permute-done.13.given_ref, bf16[64,2048]{1,0:T(8,128)(2,1)S(1)} %collective-permute-done.15.refs_0_, ...), custom_call_target="tpu_custom_call" | custom-call | flops 1000000000 | bytes 2000000 | tf_op jit(solution)/shard_map/pallas_call | solution.py:471
  57.9 4.2 %collective-permute-done.12.refs_0_ = bf16[32,4096]{1,0:T(8,128)(2,1)S(1)} collective-permute-done((bf16[32,4096]{1,0:T(8,128)(2,1)S(1)}, bf16[32,4096]{1,0:T(8,128)(2,1)S(1)}, u32[]{:S(2)}, u32[]{:S(2)}) %collective-permute-start.12) | collective-permute-done | bytes 262176 | tf_op jit(solution)/shard_map/ppermute | solution.py:506
  62.2 1.0 %shard_map.127 = (bf16[128,4096]{1,0:T(8,128)(2,1)}, bf16[128,4096]{1,0:T(8,128)(2,1)}) custom-call(bf16[128,4096]{1,0:T(8,128)(2,1)S(1)} %copy-done, bf16[64,4096]{1,0:T(8,128)(2,1)S(1)} %get-tuple-element.45.own_ref, bf16[64,4096]{1,0:T(8,128)(2,1)S(1)} %collective-permute-done.9.given_ref, ...), custom_call_target="tpu_custom_call", output_to_operand_aliasing={{0}: (5, {}), {1}: (6, {})} | custom-call | flops 1000000000 | bytes 2000000 | tf_op jit(solution)/shard_map/pallas_call | solution.py:471
  63.2 4.0 %collective-permute-done.11.refs_0_ = bf16[32,4096]{1,0:T(8,128)(2,1)S(1)} collective-permute-done((bf16[32,4096]{1,0:T(8,128)(2,1)S(1)}, bf16[32,4096]{1,0:T(8,128)(2,1)S(1)}, u32[]{:S(2)}, u32[]{:S(2)}) %collective-permute-start.11) | collective-permute-done | bytes 262176 | tf_op jit(solution)/shard_map/ppermute | solution.py:506
  67.2 1.0 %shard_map.128 = (bf16[128,4096]{1,0:T(8,128)(2,1)}, bf16[128,4096]{1,0:T(8,128)(2,1)}) custom-call(bf16[128,4096]{1,0:T(8,128)(2,1)S(1)} %copy-done, bf16[64,4096]{1,0:T(8,128)(2,1)S(1)} %get-tuple-element.45.own_ref, bf16[64,4096]{1,0:T(8,128)(2,1)S(1)} %collective-permute-done.9.given_ref, ...), custom_call_target="tpu_custom_call", output_to_operand_aliasing={{0}: (5, {}), {1}: (6, {})} | custom-call | flops 1000000000 | bytes 2000000 | tf_op jit(solution)/shard_map/pallas_call | solution.py:471
  (40 shorter events, 0.7 us)
Async XLA Ops:
  0.6 5.0 %copy-start.3 = (s32[16]{0:T(128)S(1)}, s32[16]{0:T(128)}, u32[]{:S(2)}) copy-start(s32[16]{0:T(128)} %param.17) | copy-start | bytes 196
  0.6 5.0 %copy-start.2 = (bf16[2,124,512]{2,0,1:T(2,128)(2,1)S(1)}, bf16[2,124,512]{2,0,1:T(2,128)(2,1)}, u32[]{:S(2)}) copy-start(bf16[2,124,512]{2,0,1:T(2,128)(2,1)} %param.12) | copy-start | bytes 761860
  1.9 5.0 %collective-permute-start = (bf16[128,128]{1,0:T(8,128)(2,1)S(1)}, bf16[128,128]{1,0:T(8,128)(2,1)S(1)}, u32[]{:S(2)}, u32[]{:S(2)}) collective-permute-start(bf16[128,128]{1,0:T(8,128)(2,1)S(1)} %get-tuple-element.31.refs_5_.refs_0_.refs_4_), channel_id=1, source_target_pairs={{0,2},{1,3},{2,0},{3,1},{4,6},{5,7},{6,4},{7,5},{8,10},{9,11},{10,... | collective-permute-start | bytes 98312 | tf_op jit(solution)/shard_map/ppermute | solution.py:506
  5.7 6.6 %slice-start.2 = ((s8[6291456]{0:T(1024)(128)(4,1)}), s8[4194304]{0:T(1024)(128)(4,1)S(1)}, s32[]{:S(2)}) async-start(s8[6291456]{0:T(1024)(128)(4,1)} %bitcast.7), calls=%async_computation.2 | async-start | bytes 8388608
  5.7 6.6 %slice-start.3 = ((s8[6291456]{0:T(1024)(128)(4,1)}), s8[2097152]{0:T(1024)(128)(4,1)S(1)}, s32[]{:S(2)}) async-start(s8[6291456]{0:T(1024)(128)(4,1)} %bitcast.7), calls=%async_computation.3 | async-start | bytes 4194304
  8.4 3.9 %collective-permute-start.1 = (bf16[1024,128]{1,0:T(8,128)(2,1)S(1)}, bf16[1024,128]{1,0:T(8,128)(2,1)S(1)}, u32[]{:S(2)}, u32[]{:S(2)}) collective-permute-start(bf16[1024,128]{1,0:T(8,128)(2,1)S(1)} %get-tuple-element.32), channel_id=1, source_target_pairs={{0,1},{1,0},{2,3},{3,2},{4,5},{5,4},{6,7},{7,6},{8,9},{9,8},{10,11... | collective-permute-start | bytes 786440 | tf_op jit(solution)/shard_map/ppermute | solution.py:506
  8.5 12.9 %collective-permute-start.2 = (bf16[512,128]{1,0:T(8,128)(2,1)S(1)}, bf16[512,128]{1,0:T(8,128)(2,1)S(1)}, u32[]{:S(2)}, u32[]{:S(2)}) collective-permute-start(bf16[512,128]{1,0:T(8,128)(2,1)S(1)} %get-tuple-element.35), channel_id=1, source_target_pairs={{0,2},{1,3},{2,0},{3,1},{4,6},{5,7},{6,4},{7,5},{8,10},{9,11},{10,... | collective-permute-start | bytes 393224 | tf_op jit(solution)/shard_map/ppermute | solution.py:506
  10.5 10.9 %collective-permute-start.3 = (bf16[512,128]{1,0:T(8,128)(2,1)S(1)}, bf16[512,128]{1,0:T(8,128)(2,1)S(1)}, u32[]{:S(2)}, u32[]{:S(2)}) collective-permute-start(bf16[512,128]{1,0:T(8,128)(2,1)S(1)} %get-tuple-element.36), channel_id=1, source_target_pairs={{0,3},{1,2},{2,1},{3,0},{4,7},{5,6},{6,5},{7,4},{8,11},{9,10},{10,... | collective-permute-start | bytes 393224 | tf_op jit(solution)/shard_map/ppermute | solution.py:506
  10.5 8.6 %collective-permute-start.4 = (bf16[256,128]{1,0:T(8,128)(2,1)S(1)}, bf16[256,128]{1,0:T(8,128)(2,1)S(1)}, u32[]{:S(2)}, u32[]{:S(2)}) collective-permute-start(bf16[256,128]{1,0:T(8,128)(2,1)S(1)} %get-tuple-element.38), channel_id=1, source_target_pairs={{0,2},{1,3},{2,0},{3,1},{4,6},{5,7},{6,4},{7,5},{8,10},{9,11},{10,... | collective-permute-start | bytes 196616 | tf_op jit(solution)/shard_map/ppermute | solution.py:506
  12.3 9.1 %slice-start = ((s8[8388608]{0:T(1024)(128)(4,1)}), s8[4194304]{0:T(1024)(128)(4,1)S(1)}, s32[]{:S(2)}) async-start(s8[8388608]{0:T(1024)(128)(4,1)} %bitcast.2), calls=%async_computation | async-start | bytes 8388608
  12.3 9.1 %slice-start.1 = ((s8[8388608]{0:T(1024)(128)(4,1)}), s8[4194304]{0:T(1024)(128)(4,1)S(1)}, s32[]{:S(2)}) async-start(s8[8388608]{0:T(1024)(128)(4,1)} %bitcast.2), calls=%async_computation.1 | async-start | bytes 8388608
  12.3 8.8 %collective-permute-start.5 = (bf16[256,128]{1,0:T(8,128)(2,1)S(1)}, bf16[256,128]{1,0:T(8,128)(2,1)S(1)}, u32[]{:S(2)}, u32[]{:S(2)}) collective-permute-start(bf16[256,128]{1,0:T(8,128)(2,1)S(1)} %get-tuple-element.39), channel_id=1, source_target_pairs={{0,3},{1,2},{2,1},{3,0},{4,7},{5,6},{6,5},{7,4},{8,11},{9,10},{10,... | collective-permute-start | bytes 196616 | tf_op jit(solution)/shard_map/ppermute | solution.py:506
  15.8 15.1 %collective-permute-start.6 = (bf16[152,128]{1,0:T(8,128)(2,1)S(1)}, bf16[152,128]{1,0:T(8,128)(2,1)S(1)}, u32[]{:S(2)}, u32[]{:S(2)}) collective-permute-start(bf16[152,128]{1,0:T(8,128)(2,1)S(1)} %get-tuple-element.41), channel_id=1, source_target_pairs={{0,1},{1,0},{2,3},{3,2},{4,5},{5,4},{6,7},{7,6},{8,9},{9,8},{10,11... | collective-permute-start | bytes 116744 | tf_op jit(solution)/shard_map/ppermute | solution.py:506
  19.2 11.9 %collective-permute-start.7 = (bf16[152,128]{1,0:T(8,128)(2,1)S(1)}, bf16[152,128]{1,0:T(8,128)(2,1)S(1)}, u32[]{:S(2)}, u32[]{:S(2)}) collective-permute-start(bf16[152,128]{1,0:T(8,128)(2,1)S(1)} %get-tuple-element.42), channel_id=1, source_target_pairs={{0,2},{1,3},{2,0},{3,1},{4,6},{5,7},{6,4},{7,5},{8,10},{9,11},{10,... | collective-permute-start | bytes 116744 | tf_op jit(solution)/shard_map/ppermute | solution.py:506
  21.1 10.0 %collective-permute-start.8 = (bf16[152,128]{1,0:T(8,128)(2,1)S(1)}, bf16[152,128]{1,0:T(8,128)(2,1)S(1)}, u32[]{:S(2)}, u32[]{:S(2)}) collective-permute-start(bf16[152,128]{1,0:T(8,128)(2,1)S(1)} %get-tuple-element.43), channel_id=1, source_target_pairs={{0,3},{1,2},{2,1},{3,0},{4,7},{5,6},{6,5},{7,4},{8,11},{9,10},{10,... | collective-permute-start | bytes 116744 | tf_op jit(solution)/shard_map/ppermute | solution.py:506
  24.9 16.7 %collective-permute-start.14 = (bf16[64,2048]{1,0:T(8,128)(2,1)S(1)}, bf16[64,2048]{1,0:T(8,128)(2,1)S(1)}, u32[]{:S(2)}, u32[]{:S(2)}) collective-permute-start(bf16[64,2048]{1,0:T(8,128)(2,1)S(1)} %get-tuple-element.52), channel_id=1, source_target_pairs={{0,1},{1,0},{2,3},{3,2},{4,5},{5,4},{6,7},{7,6},{8,9},{9,8},{10,11... | collective-permute-start | bytes 786440 | tf_op jit(solution)/shard_map/ppermute | solution.py:506
  25.9 17.6 %collective-permute-start.16 = (bf16[64,2048]{1,0:T(8,128)(2,1)S(1)}, bf16[64,2048]{1,0:T(8,128)(2,1)S(1)}, u32[]{:S(2)}, u32[]{:S(2)}) collective-permute-start(bf16[64,2048]{1,0:T(8,128)(2,1)S(1)} %get-tuple-element.55), channel_id=1, source_target_pairs={{0,1},{1,0},{2,3},{3,2},{4,5},{5,4},{6,7},{7,6},{8,9},{9,8},{10,11... | collective-permute-start | bytes 786440 | tf_op jit(solution)/shard_map/ppermute | solution.py:506
  30.9 25.6 %collective-permute-start.13 = (bf16[64,4096]{1,0:T(8,128)(2,1)S(1)}, bf16[64,4096]{1,0:T(8,128)(2,1)S(1)}, u32[]{:S(2)}, u32[]{:S(2)}) collective-permute-start(bf16[64,4096]{1,0:T(8,128)(2,1)S(1)} %get-tuple-element.50), channel_id=1, source_target_pairs={{0,1},{1,0},{2,3},{3,2},{4,5},{5,4},{6,7},{7,6},{8,9},{9,8},{10,11... | collective-permute-start | bytes 1572872 | tf_op jit(solution)/shard_map/ppermute | solution.py:506
  36.7 19.9 %copy-start = (bf16[128,4096]{1,0:T(8,128)(2,1)S(1)}, bf16[128,4096]{1,0:T(8,128)(2,1)}, u32[]{:S(2)}) copy-start(bf16[128,4096]{1,0:T(8,128)(2,1)} %res_ref.5) | copy-start | bytes 3145732
  36.7 19.8 %copy-start.1 = (f32[4096]{0:T(1024)S(1)}, f32[4096]{0:T(1024)}, u32[]{:S(2)}) copy-start(f32[4096]{0:T(1024)} %param.21) | copy-start | bytes 49156
  36.7 7.2 %collective-permute-start.10 = (bf16[64,4096]{1,0:T(8,128)(2,1)S(1)}, bf16[64,4096]{1,0:T(8,128)(2,1)S(1)}, u32[]{:S(2)}, u32[]{:S(2)}) collective-permute-start(bf16[64,4096]{1,0:T(8,128)(2,1)S(1)} %get-tuple-element.48), channel_id=1, source_target_pairs={{0,1},{1,0},{2,3},{3,2},{4,5},{5,4},{6,7},{7,6},{8,9},{9,8},{10,11... | collective-permute-start | bytes 1572872 | tf_op jit(solution)/shard_map/ppermute | solution.py:506
  41.4 16.5 %collective-permute-start.9 = (bf16[64,4096]{1,0:T(8,128)(2,1)S(1)}, bf16[64,4096]{1,0:T(8,128)(2,1)S(1)}, u32[]{:S(2)}, u32[]{:S(2)}) collective-permute-start(bf16[64,4096]{1,0:T(8,128)(2,1)S(1)} %get-tuple-element.46), channel_id=1, source_target_pairs={{0,1},{1,0},{2,3},{3,2},{4,5},{5,4},{6,7},{7,6},{8,9},{9,8},{10,11... | collective-permute-start | bytes 1572872 | tf_op jit(solution)/shard_map/ppermute | solution.py:506
  41.7 9.2 %collective-permute-start.15 = (bf16[64,2048]{1,0:T(8,128)(2,1)S(1)}, bf16[64,2048]{1,0:T(8,128)(2,1)S(1)}, u32[]{:S(2)}, u32[]{:S(2)}) collective-permute-start(bf16[64,2048]{1,0:T(8,128)(2,1)S(1)} %add_convert_fusion.2), channel_id=1, source_target_pairs={{0,2},{1,3},{2,0},{3,1},{4,6},{5,7},{6,4},{7,5},{8,10},{9,11},{10,... | collective-permute-start | bytes 786440 | tf_op jit(solution)/shard_map/ppermute | solution.py:506
  43.5 13.0 %collective-permute-start.17 = (bf16[64,2048]{1,0:T(8,128)(2,1)S(1)}, bf16[64,2048]{1,0:T(8,128)(2,1)S(1)}, u32[]{:S(2)}, u32[]{:S(2)}) collective-permute-start(bf16[64,2048]{1,0:T(8,128)(2,1)S(1)} %add_convert_fusion.1), channel_id=1, source_target_pairs={{0,2},{1,3},{2,0},{3,1},{4,6},{5,7},{6,4},{7,5},{8,10},{9,11},{10,... | collective-permute-start | bytes 786440 | tf_op jit(solution)/shard_map/ppermute | solution.py:506
  44.1 18.1 %collective-permute-start.12 = (bf16[32,4096]{1,0:T(8,128)(2,1)S(1)}, bf16[32,4096]{1,0:T(8,128)(2,1)S(1)}, u32[]{:S(2)}, u32[]{:S(2)}) collective-permute-start(bf16[32,4096]{1,0:T(8,128)(2,1)S(1)} %get-tuple-element.60), channel_id=1, source_target_pairs={{0,2},{1,3},{2,0},{3,1},{4,6},{5,7},{6,4},{7,5},{8,10},{9,11},{10,... | collective-permute-start | bytes 786440 | tf_op jit(solution)/shard_map/ppermute | solution.py:506
  50.9 16.2 %collective-permute-start.11 = (bf16[32,4096]{1,0:T(8,128)(2,1)S(1)}, bf16[32,4096]{1,0:T(8,128)(2,1)S(1)}, u32[]{:S(2)}, u32[]{:S(2)}) collective-permute-start(bf16[32,4096]{1,0:T(8,128)(2,1)S(1)} %get-tuple-element.61), channel_id=1, source_target_pairs={{0,2},{1,3},{2,0},{3,1},{4,6},{5,7},{6,4},{7,5},{8,10},{9,11},{10,... | collective-permute-start | bytes 786440 | tf_op jit(solution)/shard_map/ppermute | solution.py:506

commit v5 on v4

--- a/solution.py
+++ b/solution.py
@@ -12,8 +12,8 @@
 EPS = 1e-05
 CHUNKS = (64, 64)
 COLUMNS = 512
+FIRST_PART = 4
 GROUP_ROWS = 256
-PIPE, ONES, SPLITQ = True, True, True
 
 F32 = jnp.float32
 BF16 = jnp.bfloat16
@@ -98,7 +98,7 @@
 
 
 def pack_fresh(prompt, history, queries, meta, slots, local_heads, group):
-    h_rows, p_rows = history.shape[1], prompt.shape[1]
+    h_rows, p_rows = history.shape[0] // 2, prompt.shape[1]
     p_pad = round_up(p_rows, 16)
     q_rows = queries[0].shape[0]
     every = [1] + slots
@@ -109,20 +109,9 @@
 
     def body(m, *refs):
         p_refs, refs = refs[:n], refs[n:]
-        h_hbm, refs = refs[0], refs[1:]
-        q_refs, refs = refs[: len(queries)], refs[len(queries) :]
-        o_refs, sem = refs[:n], refs[n]
-        lane = pl.multiple_of((m[0] ^ 1) * local_heads // group * HEAD_DIM, HEAD_DIM)
-        copies = [
-            pltpu.make_async_copy(
-                h_hbm.at[part, :, pl.ds(lane, HEAD_DIM)],
-                o_refs[0].at[part * h_rows : (part + 1) * h_rows, :],
-                sem.at[part],
-            )
-            for part in range(2)
-        ]
-        for copy in copies:
-            copy.start()
+        h_ref, refs = refs[0], refs[1:]
+        q_refs, o_refs = refs[: len(queries)], refs[len(queries) :]
+        o_refs[0][0 : 2 * h_rows, :] = h_ref[...]
         for i in range(n):
             row = 2 * h_rows if i == 0 else 0
             for part in range(2):
@@ -136,8 +125,6 @@
         row = 2 * (h_rows + p_pad)
         for i, q_ref in enumerate(q_refs):
             o_refs[0][row + i * q_rows : row + (i + 1) * q_rows, :] = q_ref[...]
-        for copy in copies:
-            copy.wait()
 
     sizes = [2 * (h_rows + p_pad) + len(queries) * q_rows] + [2 * p_pad] * len(slots)
     outs = pl.pallas_call(
@@ -146,16 +133,14 @@
             num_scalar_prefetch=1,
             grid=(1,),
             in_specs=[pl.BlockSpec((2, p_rows, HEAD_DIM), head_of(k)) for k in every]
-            + [in_hbm()]
-            + [in_vmem()] * len(queries),
+            + [in_vmem()] * (1 + len(queries)),
             out_specs=[in_vmem()] * n,
-            scratch_shapes=[pltpu.SemaphoreType.DMA((2,))],
         ),
         out_shape=[jax.ShapeDtypeStruct((size, HEAD_DIM), BF16) for size in sizes],
         compiler_params=params(8),
         cost_estimate=busy(12),
         name="pack_fresh",
-    )(meta, *([prompt] * n), to_hbm(history), *queries)
+    )(meta, *([prompt] * n), history, *queries)
     return outs[0], dict(zip(slots, outs[1:]))
 
 
@@ -355,7 +340,7 @@
         me, valid_rows = m[0], m[1]
         for k in range(devices):
             for part, dst in ((0, k_all), (1, v_all)):
-                for copy in range(2 if SPLITQ and part == 0 else 1):
+                for copy in range(2 - part):
                     lanes = slice(copy * HEAD_DIM, (copy + 1) * HEAD_DIM)
                     ref, row = cached[k]
                     row += part * h_rows
@@ -363,8 +348,7 @@
                     ref, row = own[k]
                     row += part * p_pad
                     dst[h_keys + k * p_pad : h_keys + (k + 1) * p_pad, lanes] = ref[row : row + p_pad, :]
-        if ONES:
-            v_all[:, HEAD_DIM:] = jnp.ones((keys, HEAD_DIM), BF16)
+        v_all[:, HEAD_DIM:] = jnp.ones((keys, HEAD_DIM), BF16)
         column = lax.broadcasted_iota(jnp.int32, (1, h_keys), 1)
         place = ((column // h_rows) ^ me) * h_rows + column % h_rows
         history_bias = jnp.where(place < valid_rows, 0.0, MASKED)
@@ -383,11 +367,10 @@
             stacked = jnp.concatenate(
                 [q[pl.ds(row0, count), h * HEAD_DIM : (h + 1) * HEAD_DIM] for h in range(g, g + per)], axis=0
             )
-            if SPLITQ:
-                scaled = stacked.astype(F32) * factor
-                high = scaled.astype(BF16)
-                low = (scaled - high.astype(F32)).astype(BF16)
-                stacked = jnp.concatenate([high, low], axis=1)
+            scaled = stacked.astype(F32) * factor
+            high = scaled.astype(BF16)
+            low = (scaled - high.astype(F32)).astype(BF16)
+            stacked = jnp.concatenate([high, low], axis=1)
             scores = lax.dot_general(
                 stacked, k_all[...], (((1,), (1,)), ((), ())), preferred_element_type=F32
             )
@@ -396,23 +379,16 @@
         ahead = scores_of(*steps[0])
         for t, (i, g) in enumerate(steps):
             scores = ahead
-            if PIPE and t + 1 < len(steps):
+            if t + 1 < len(steps):
                 ahead = scores_of(*steps[t + 1])
             top = jnp.max(scores, axis=-1, keepdims=True)
-            weights = jnp.exp2(scores - top) if SPLITQ else jnp.exp2((scores - top) * factor)
-            if not ONES:
-                total = jnp.sum(weights, axis=-1, keepdims=True)
+            weights = jnp.exp2(scores - top)
             summed = jnp.dot(weights.astype(BF16), v_all[...], preferred_element_type=F32)
-            if ONES:
-                total = summed[:, HEAD_DIM:]
-                summed = summed[:, :HEAD_DIM]
-            summed = (summed / total).astype(BF16)
+            summed = (summed[:, :HEAD_DIM] / summed[:, HEAD_DIM:]).astype(BF16)
             for h in range(per):
                 att[i * count : (i + 1) * count, (g + h) * HEAD_DIM : (g + h + 1) * HEAD_DIM] = summed[
                     h * count : (h + 1) * count
                 ]
-            if not PIPE and t + 1 < len(steps):
-                ahead = scores_of(*steps[t + 1])
         if has_decode:
             for i, slot in enumerate(order):
 
@@ -430,8 +406,8 @@
         out_specs=[in_vmem()] * 3,
         out_shape=[jax.ShapeDtypeStruct((half, columns), BF16)] * 2 + [pltpu.VMEM((2 * half, local_width), BF16)],
         scratch_shapes=[
-            pltpu.VMEM((keys, HEAD_DIM * (2 if SPLITQ else 1)), BF16),
-            pltpu.VMEM((keys, HEAD_DIM * (2 if ONES else 1)), BF16),
+            pltpu.VMEM((keys, 2 * HEAD_DIM), BF16),
+            pltpu.VMEM((keys, 2 * HEAD_DIM), BF16),
         ],
         compiler_params=params(24),
         cost_estimate=pl.CostEstimate(flops=flops, transcendentals=0, bytes_accessed=weight.size * 2),
@@ -443,7 +419,7 @@
     count = crossed[0].shape[0]
     tile = 16
     n_cross = len(crossed)
-    n_columns = model // crossed[0].shape[1]
+    n_columns = 1 if crossed[0].shape[1] == model else 2
 
     def body(res_ref, own_ref, given_ref, *refs):
         cross = refs[:n_cross]
@@ -509,11 +485,11 @@
         return [values[0]] + [swap(values[k], k) for k in range(1, devices)]
 
     slots = [0] + list(range(2, devices))
-    packed, own_query = pack_history(history_cache, decode_queries, slots, local_heads, group)
+    packed, own_query = pack_history(history_cache, decode_queries, [1] + slots, local_heads, group)
     even_queries = [own_query] + [swap(own_query, k) for k in range(2, devices, 2)]
     history = {k: swap(packed[k], k) if k else packed[k] for k in slots}
     meta = jnp.concatenate([lax.axis_index("tp").astype(jnp.int32)[None], prompt_start, decode_lengths])
-    bundle, packed = pack_fresh(prompt_entries, history_cache, even_queries, meta, slots, local_heads, group)
+    bundle, packed = pack_fresh(prompt_entries, packed[1], even_queries, meta, slots, local_heads, group)
     bundle = swap(bundle, 1)
     fresh = {k: swap(packed[k], k) if k else packed[k] for k in slots}
     parts, queries, entries = decode_partials(
@@ -544,13 +520,13 @@
     crossed, first = [], 0
     for count in chunks:
         last = first + count == block
-        columns = model if last else model // 2
+        columns = model if last else model // FIRST_PART
         keep, give, att = attended(others, first, count, decoded if last else None, columns)
         pair = chip_sum(keep, give)
         if last:
-            half = count // 2 if count % 32 == 0 else count
-            for start in range(0, count, half):
-                crossed.append((first + start, cross(pair, count, start, start + half)))
+            cut = count - 16 if count > 16 else 0
+            for start, stop in [(0, cut), (cut, count)] if cut else [(0, count)]:
+                crossed.append((first + start, cross(pair, count, start, stop)))
         else:
             pieces = [cross(pair, count, 0, count)]
             keep, give = project(att, out_weight, columns)

time: 68.6 us -> 69.8 us (1.017)
  waiting for transfers between devices: 21.5 us -> 23.7 us
  Pallas kernels: 28.4 us -> 27.6 us
    ppermute x18, waiting for transfers between devices: 21.5 us -> 23.7 us  [swap(): return lax.ppermute(value, 'tp', [(i, i ^ k) for i in range(devices)])]
    pallas_call x1, Pallas kernels: 1.6 us -> 0.64 us  [pack_fresh(): pl.pallas_call(body, grid_spec=pltpu.PrefetchScalarGridSpec(num_scalar_pr...]
  transfers between devices with their start and end apart: 18 -> 18, of which waited for: 6 -> 4; matrix products, arithmetic and copies ran while one was open for 1% -> 1% of each run, Pallas kernels for 36% -> 36%
where the time goes in v5:
time: 69.8 us; the launch traced here: 69.6 us
  Pallas kernels  27.6 us (40%)
  waiting for transfers between devices  23.7 us (34%)
  starting transfers between devices  16.2 us (23%)
  between operations  1.69 us (2%)
    ppermute x18, waiting for transfers between devices, swap(): return lax.ppermute(value, 'tp', [(i, i ^ k) for i in range(devices)])  23.7 us
    pallas_call x4, Pallas kernels, attend(): pl.pallas_call(body, in_specs=[smem()] + [in_vmem()] * n_vmem, out_specs=...  16.5 us
    ppermute x18, starting transfers between devices, swap(): return lax.ppermute(value, 'tp', [(i, i ^ k) for i in range(devices)])  16.2 us
    pallas_call x1, Pallas kernels, decode_partials(): pl.pallas_call(body, in_specs=[smem()] + [in_vmem()] * (devices // 2 + 2)...  3.5 us
    pallas_call x3, Pallas kernels, finish(): pl.pallas_call(body, in_specs=[in_vmem()] * n_in + [hbm()] * len(previous...  3.44 us
  transfers between devices with their start and end apart: 18, of which 4 were waited for; matrix products, arithmetic and copies ran while one was open for 1% of the time, Pallas kernels for 36%

profile of v5, /device:TPU:0, one launch (start us, length us, event | category | flops | bytes accessed | tf_op | source)
XLA Modules:
  0.0 69.6 jit_solution(1196861088853673400)
XLA Ops:
  0.7 1.3 %pack_history.1 = (bf16[512,128]{1,0:T(8,128)(2,1)S(1)}, bf16[512,128]{1,0:T(8,128)(2,1)S(1)}, bf16[512,128]{1,0:T(8,128)(2,1)S(1)}, bf16[512,128]{1,0:T(8,128)(2,1)S(1)}, bf16[128,128]{1,0:T(8,128)(2,1)S(1)}) custom-call(bf16[2,256,512]{2,1,0:T(8,128)(2,1)} %h_hbm.1, bf16[16,1024]{1,0:T(8,128)(2,1)} %refs_5_.1), custom_call_target="tpu_custom_call" | custom-call | flops 3000000000 | bytes 6000000 | tf_op jit(solution)/shard_map/pack_history/pallas_call | solution.py:86
  2.0 3.1 %collective-permute-start = (bf16[128,128]{1,0:T(8,128)(2,1)S(1)}, bf16[128,128]{1,0:T(8,128)(2,1)S(1)}, u32[]{:S(2)}, u32[]{:S(2)}) collective-permute-start(bf16[128,128]{1,0:T(8,128)(2,1)S(1)} %get-tuple-element.32.refs_5_.refs_0_.refs_4_), channel_id=1, source_target_pairs={{0,2},{1,3},{2,0},{3,1},{4,6},{5,7},{6,4},{7,5},{8,10},{9,11},{10,... | collective-permute-start | bytes 98312 | tf_op jit(solution)/shard_map/ppermute | solution.py:482
  5.8 1.1 %collective-permute-done.refs_6_.refs_1_ = bf16[128,128]{1,0:T(8,128)(2,1)S(1)} collective-permute-done((bf16[128,128]{1,0:T(8,128)(2,1)S(1)}, bf16[128,128]{1,0:T(8,128)(2,1)S(1)}, u32[]{:S(2)}, u32[]{:S(2)}) %collective-permute-start) | collective-permute-done | bytes 32800 | tf_op jit(solution)/shard_map/ppermute | solution.py:482
  6.9 0.6 pack_fresh.1
  7.6 2.1 %collective-permute-start.2 = (bf16[512,128]{1,0:T(8,128)(2,1)S(1)}, bf16[512,128]{1,0:T(8,128)(2,1)S(1)}, u32[]{:S(2)}, u32[]{:S(2)}) collective-permute-start(bf16[512,128]{1,0:T(8,128)(2,1)S(1)} %get-tuple-element.37), channel_id=1, source_target_pairs={{0,2},{1,3},{2,0},{3,1},{4,6},{5,7},{6,4},{7,5},{8,10},{9,11},{10,... | collective-permute-start | bytes 393224 | tf_op jit(solution)/shard_map/ppermute | solution.py:482
  9.8 1.7 %collective-permute-start.4 = (bf16[256,128]{1,0:T(8,128)(2,1)S(1)}, bf16[256,128]{1,0:T(8,128)(2,1)S(1)}, u32[]{:S(2)}, u32[]{:S(2)}) collective-permute-start(bf16[256,128]{1,0:T(8,128)(2,1)S(1)} %get-tuple-element.40), channel_id=1, source_target_pairs={{0,2},{1,3},{2,0},{3,1},{4,6},{5,7},{6,4},{7,5},{8,10},{9,11},{10,... | collective-permute-start | bytes 196616 | tf_op jit(solution)/shard_map/ppermute | solution.py:482
  11.6 3.5 %decode.1 = (bf16[152,128]{1,0:T(8,128)(2,1)S(1)}, bf16[152,128]{1,0:T(8,128)(2,1)S(1)}, bf16[152,128]{1,0:T(8,128)(2,1)S(1)}, bf16[152,128]{1,0:T(8,128)(2,1)S(...) custom-call(s32[18]{0:T(128)S(1)} %pad_add_fusion.m, ...), custom_call_target="tpu_custom_call" | custom-call | flops 6000000000 | bytes 12000000 | tf_op jit(solution)/shard_map/decode/pallas_call | solution.py:225
  15.1 0.2 collective-permute-start.6
  15.2 3.1 %collective-permute-done.4.refs_5_ = bf16[256,128]{1,0:T(8,128)(2,1)S(1)} collective-permute-done((bf16[256,128]{1,0:T(8,128)(2,1)S(1)}, bf16[256,128]{1,0:T(8,128)(2,1)S(1)}, u32[]{:S(2)}, u32[]{:S(2)}) %collective-permute-start.4) | collective-permute-done | bytes 65568 | tf_op jit(solution)/shard_map/ppermute | solution.py:482
  18.3 2.0 %collective-permute-start.7 = (bf16[152,128]{1,0:T(8,128)(2,1)S(1)}, bf16[152,128]{1,0:T(8,128)(2,1)S(1)}, u32[]{:S(2)}, u32[]{:S(2)}) collective-permute-start(bf16[152,128]{1,0:T(8,128)(2,1)S(1)} %get-tuple-element.44), channel_id=1, source_target_pairs={{0,2},{1,3},{2,0},{3,1},{4,6},{5,7},{6,4},{7,5},{8,10},{9,11},{10,... | collective-permute-start | bytes 116744 | tf_op jit(solution)/shard_map/ppermute | solution.py:482
  20.3 0.3 collective-permute-start.8
  20.6 3.2 %shard_map.125 = (bf16[64,1024]{1,0:T(8,128)(2,1)S(1)}, bf16[64,1024]{1,0:T(8,128)(2,1)S(1)}, bf16[128,1024]{1,0:T(8,128)(2,1)S(1)}) custom-call(s32[18]{0:T(128)S(1)} %pad_add_fusion.m, bf16[512,1024]{1,0:T(8,128)(2,1)S(1)} %get-tuple-element.35.q, bf16[1024,128]{1,0:T(8,128)(2,1)S(1)} %collective-permute-done.1.refs_2_.refs_0_, ...), custom_call_target="tpu_custom_call" | custom-call | flops 1879048192 | bytes 8388608 | tf_op jit(solution)/shard_map/pallas_call | solution.py:403
  23.9 0.2 collective-permute-start.14
  24.1 1.0 %project.1 = (bf16[64,3072]{1,0:T(8,128)(2,1)S(1)}, bf16[64,3072]{1,0:T(8,128)(2,1)S(1)}) custom-call(bf16[128,1024]{1,0:T(8,128)(2,1)S(1)} %get-tuple-element.55.att_ref, bf16[1024,4096]{1,0:T(8,128)(2,1)S(1)} %bitcast.3), custom_call_target="tpu_custom_call" | custom-call | flops 1000000000 | bytes 2000000 | tf_op jit(solution)/shard_map/project/pallas_call | solution.py:304
  25.1 0.4 collective-permute-start.16
  25.5 4.6 %shard_map.124 = (bf16[64,4096]{1,0:T(8,128)(2,1)S(1)}, bf16[64,4096]{1,0:T(8,128)(2,1)S(1)}, bf16[128,1024]{1,0:T(8,128)(2,1)}) custom-call(s32[18]{0:T(128)S(1)} %pad_add_fusion.m, bf16[512,1024]{1,0:T(8,128)(2,1)S(1)} %get-tuple-element.35.q, bf16[1024,128]{1,0:T(8,128)(2,1)S(1)} %collective-permute-done.1.refs_2_.refs_0_, ...), custom_call_target="tpu_custom_call" | custom-call | flops 1879048192 | bytes 8388608 | tf_op jit(solution)/shard_map/pallas_call | solution.py:403
  30.1 0.2 collective-permute-start.13
  30.3 1.2 %join.1.refs_7_ = bf16[16,1024]{1,0:T(8,128)(2,1)S(1)} custom-call(bf16[152,128]{1,0:T(8,128)(2,1)S(1)} %get-tuple-element.42.refs_0_, bf16[152,128]{1,0:T(8,128)(2,1)S(1)} %collective-permute-done.6.refs_1_, bf16[152,128]{1,0:T(8,128)(2,1)S(1)} %collective-permute-done.7.refs_2_, bf16[152,128]{1,0:T(8,128)(2,1)S(1)} %collective-permute-done.8.refs_3_, ...), custom_call_target="tpu_custom_call" | custom-call | flops 500000000 | bytes 1000000 | tf_op jit(solution)/shard_map/join/pallas_call | solution.py:279
  31.5 4.4 %shard_map.123 = (bf16[64,4096]{1,0:T(8,128)(2,1)S(1)}, bf16[64,4096]{1,0:T(8,128)(2,1)S(1)}, bf16[128,1024]{1,0:T(8,128)(2,1)}) custom-call(s32[18]{0:T(128)S(1)} %pad_add_fusion.m, bf16[512,1024]{1,0:T(8,128)(2,1)S(1)} %get-tuple-element.35.q, bf16[1024,128]{1,0:T(8,128)(2,1)S(1)} %collective-permute-done.1.refs_2_.refs_0_, ...), custom_call_target="tpu_custom_call" | custom-call | flops 1879048192 | bytes 8388608 | tf_op jit(solution)/shard_map/pallas_call | solution.py:403
  36.0 0.4 collective-permute-start.10
  36.4 4.2 %shard_map.122 = (bf16[64,4096]{1,0:T(8,128)(2,1)S(1)}, bf16[64,4096]{1,0:T(8,128)(2,1)S(1)}, bf16[128,1024]{1,0:T(8,128)(2,1)}) custom-call(s32[18]{0:T(128)S(1)} %pad_add_fusion.m, bf16[512,1024]{1,0:T(8,128)(2,1)S(1)} %get-tuple-element.35.q, bf16[1024,128]{1,0:T(8,128)(2,1)S(1)} %collective-permute-done.1.refs_2_.refs_0_, ...), custom_call_target="tpu_custom_call" | custom-call | flops 1879048192 | bytes 8388608 | tf_op jit(solution)/shard_map/pallas_call | solution.py:403
  40.6 0.2 collective-permute-start.9
  41.0 1.8 %collective-permute-start.17 = (bf16[64,3072]{1,0:T(8,128)(2,1)S(1)}, bf16[64,3072]{1,0:T(8,128)(2,1)S(1)}, u32[]{:S(2)}, u32[]{:S(2)}) collective-permute-start(bf16[64,3072]{1,0:T(8,128)(2,1)S(1)} %add_convert_fusion.1), channel_id=1, source_target_pairs={{0,2},{1,3},{2,0},{3,1},{4,6},{5,7},{6,4},{7,5},{8,10},{9,11},{10,... | collective-permute-start | bytes 1179656 | tf_op jit(solution)/shard_map/ppermute | solution.py:482
  42.7 0.1 add_convert_fusion
  42.9 0.4 collective-permute-start.12
  43.3 1.8 %collective-permute-start.15 = (bf16[64,1024]{1,0:T(8,128)(2,1)S(1)}, bf16[64,1024]{1,0:T(8,128)(2,1)S(1)}, u32[]{:S(2)}, u32[]{:S(2)}) collective-permute-start(bf16[64,1024]{1,0:T(8,128)(2,1)S(1)} %add_convert_fusion.2), channel_id=1, source_target_pairs={{0,2},{1,3},{2,0},{3,1},{4,6},{5,7},{6,4},{7,5},{8,10},{9,11},{10,... | collective-permute-start | bytes 393224 | tf_op jit(solution)/shard_map/ppermute | solution.py:482
  45.1 18.5 %collective-permute-done.15.refs_0_ = bf16[64,1024]{1,0:T(8,128)(2,1)S(1)} collective-permute-done((bf16[64,1024]{1,0:T(8,128)(2,1)S(1)}, bf16[64,1024]{1,0:T(8,128)(2,1)S(1)}, u32[]{:S(2)}, u32[]{:S(2)}) %collective-permute-start.15) | collective-permute-done | bytes 131104 | tf_op jit(solution)/shard_map/ppermute | solution.py:482
  63.6 1.4 %collective-permute-start.11 = (bf16[16,4096]{1,0:T(8,128)(2,1)S(1)}, bf16[16,4096]{1,0:T(8,128)(2,1)S(1)}, u32[]{:S(2)}, u32[]{:S(2)}) collective-permute-start(bf16[16,4096]{1,0:T(8,128)(2,1)S(1)} %slice.10), channel_id=1, source_target_pairs={{0,2},{1,3},{2,0},{3,1},{4,6},{5,7},{6,4},{7,5},{8,10},{9,11},{10,... | collective-permute-start | bytes 393224 | tf_op jit(solution)/shard_map/ppermute | solution.py:482
  65.0 1.4 %shard_map.126 = (bf16[128,4096]{1,0:T(8,128)(2,1)}, bf16[128,4096]{1,0:T(8,128)(2,1)}) custom-call(bf16[128,4096]{1,0:T(8,128)(2,1)S(1)} %copy-done, bf16[64,4096]{1,0:T(8,128)(2,1)S(1)} %get-tuple-element.51.own_ref, bf16[64,4096]{1,0:T(8,128)(2,1)S(1)} %collective-permute-done.13.given_ref, bf16[64,1024]{1,0:T(8,128)(2,1)S(1)} %collective-permute-done.15.refs_0_, ...), custom_call_target="tpu_custom_call" | custom-call | flops 1000000000 | bytes 2000000 | tf_op jit(solution)/shard_map/pallas_call | solution.py:447
  66.4 1.2 %shard_map.127 = (bf16[128,4096]{1,0:T(8,128)(2,1)}, bf16[128,4096]{1,0:T(8,128)(2,1)}) custom-call(bf16[128,4096]{1,0:T(8,128)(2,1)S(1)} %copy-done, bf16[64,4096]{1,0:T(8,128)(2,1)S(1)} %get-tuple-element.47.own_ref, bf16[64,4096]{1,0:T(8,128)(2,1)S(1)} %collective-permute-done.9.given_ref, ...), custom_call_target="tpu_custom_call", output_to_operand_aliasing={{0}: (5, {}), {1}: (6, {})} | custom-call | flops 1000000000 | bytes 2000000 | tf_op jit(solution)/shard_map/pallas_call | solution.py:447
  67.6 1.0 %collective-permute-done.11.refs_0_ = bf16[16,4096]{1,0:T(8,128)(2,1)S(1)} collective-permute-done((bf16[16,4096]{1,0:T(8,128)(2,1)S(1)}, bf16[16,4096]{1,0:T(8,128)(2,1)S(1)}, u32[]{:S(2)}, u32[]{:S(2)}) %collective-permute-start.11) | collective-permute-done | bytes 131104 | tf_op jit(solution)/shard_map/ppermute | solution.py:482
  68.6 0.9 %shard_map.128 = (bf16[128,4096]{1,0:T(8,128)(2,1)}, bf16[128,4096]{1,0:T(8,128)(2,1)}) custom-call(bf16[128,4096]{1,0:T(8,128)(2,1)S(1)} %copy-done, bf16[64,4096]{1,0:T(8,128)(2,1)S(1)} %get-tuple-element.47.own_ref, bf16[64,4096]{1,0:T(8,128)(2,1)S(1)} %collective-permute-done.9.given_ref, ...), custom_call_target="tpu_custom_call", output_to_operand_aliasing={{0}: (5, {}), {1}: (6, {})} | custom-call | flops 1000000000 | bytes 2000000 | tf_op jit(solution)/shard_map/pallas_call | solution.py:447
  (41 shorter events, 0.5 us)
Async XLA Ops:
  0.6 5.0 %copy-start.3 = (s32[16]{0:T(128)S(1)}, s32[16]{0:T(128)}, u32[]{:S(2)}) copy-start(s32[16]{0:T(128)} %param.17) | copy-start | bytes 196
  0.6 5.1 %copy-start.2 = (bf16[2,124,512]{2,0,1:T(2,128)(2,1)S(1)}, bf16[2,124,512]{2,0,1:T(2,128)(2,1)}, u32[]{:S(2)}) copy-start(bf16[2,124,512]{2,0,1:T(2,128)(2,1)} %param.12) | copy-start | bytes 761860
  2.0 5.0 %collective-permute-start = (bf16[128,128]{1,0:T(8,128)(2,1)S(1)}, bf16[128,128]{1,0:T(8,128)(2,1)S(1)}, u32[]{:S(2)}, u32[]{:S(2)}) collective-permute-start(bf16[128,128]{1,0:T(8,128)(2,1)S(1)} %get-tuple-element.32.refs_5_.refs_0_.refs_4_), channel_id=1, source_target_pairs={{0,2},{1,3},{2,0},{3,1},{4,6},{5,7},{6,4},{7,5},{8,10},{9,11},{10,... | collective-permute-start | bytes 98312 | tf_op jit(solution)/shard_map/ppermute | solution.py:482
  5.8 5.8 %slice-start.2 = ((s8[6291456]{0:T(1024)(128)(4,1)}), s8[4194304]{0:T(1024)(128)(4,1)S(1)}, s32[]{:S(2)}) async-start(s8[6291456]{0:T(1024)(128)(4,1)} %bitcast.7), calls=%async_computation.2 | async-start | bytes 8388608
  6.9 4.6 %slice-start.3 = ((s8[6291456]{0:T(1024)(128)(4,1)}), s8[2097152]{0:T(1024)(128)(4,1)S(1)}, s32[]{:S(2)}) async-start(s8[6291456]{0:T(1024)(128)(4,1)} %bitcast.7), calls=%async_computation.3 | async-start | bytes 4194304
  7.6 4.0 %collective-permute-start.1 = (bf16[1024,128]{1,0:T(8,128)(2,1)S(1)}, bf16[1024,128]{1,0:T(8,128)(2,1)S(1)}, u32[]{:S(2)}, u32[]{:S(2)}) collective-permute-start(bf16[1024,128]{1,0:T(8,128)(2,1)S(1)} %get-tuple-element.34), channel_id=1, source_target_pairs={{0,1},{1,0},{2,3},{3,2},{4,5},{5,4},{6,7},{7,6},{8,9},{9,8},{10,11... | collective-permute-start | bytes 786440 | tf_op jit(solution)/shard_map/ppermute | solution.py:482
  7.6 13.0 %collective-permute-start.2 = (bf16[512,128]{1,0:T(8,128)(2,1)S(1)}, bf16[512,128]{1,0:T(8,128)(2,1)S(1)}, u32[]{:S(2)}, u32[]{:S(2)}) collective-permute-start(bf16[512,128]{1,0:T(8,128)(2,1)S(1)} %get-tuple-element.37), channel_id=1, source_target_pairs={{0,2},{1,3},{2,0},{3,1},{4,6},{5,7},{6,4},{7,5},{8,10},{9,11},{10,... | collective-permute-start | bytes 393224 | tf_op jit(solution)/shard_map/ppermute | solution.py:482
  9.7 10.9 %collective-permute-start.3 = (bf16[512,128]{1,0:T(8,128)(2,1)S(1)}, bf16[512,128]{1,0:T(8,128)(2,1)S(1)}, u32[]{:S(2)}, u32[]{:S(2)}) collective-permute-start(bf16[512,128]{1,0:T(8,128)(2,1)S(1)} %get-tuple-element.38), channel_id=1, source_target_pairs={{0,3},{1,2},{2,1},{3,0},{4,7},{5,6},{6,5},{7,4},{8,11},{9,10},{10,... | collective-permute-start | bytes 393224 | tf_op jit(solution)/shard_map/ppermute | solution.py:482
  9.8 8.5 %collective-permute-start.4 = (bf16[256,128]{1,0:T(8,128)(2,1)S(1)}, bf16[256,128]{1,0:T(8,128)(2,1)S(1)}, u32[]{:S(2)}, u32[]{:S(2)}) collective-permute-start(bf16[256,128]{1,0:T(8,128)(2,1)S(1)} %get-tuple-element.40), channel_id=1, source_target_pairs={{0,2},{1,3},{2,0},{3,1},{4,6},{5,7},{6,4},{7,5},{8,10},{9,11},{10,... | collective-permute-start | bytes 196616 | tf_op jit(solution)/shard_map/ppermute | solution.py:482
  11.5 9.1 %slice-start = ((s8[8388608]{0:T(1024)(128)(4,1)}), s8[4194304]{0:T(1024)(128)(4,1)S(1)}, s32[]{:S(2)}) async-start(s8[8388608]{0:T(1024)(128)(4,1)} %bitcast.2), calls=%async_computation | async-start | bytes 8388608
  11.5 9.1 %slice-start.1 = ((s8[8388608]{0:T(1024)(128)(4,1)}), s8[4194304]{0:T(1024)(128)(4,1)S(1)}, s32[]{:S(2)}) async-start(s8[8388608]{0:T(1024)(128)(4,1)} %bitcast.2), calls=%async_computation.1 | async-start | bytes 8388608
  11.5 8.8 %collective-permute-start.5 = (bf16[256,128]{1,0:T(8,128)(2,1)S(1)}, bf16[256,128]{1,0:T(8,128)(2,1)S(1)}, u32[]{:S(2)}, u32[]{:S(2)}) collective-permute-start(bf16[256,128]{1,0:T(8,128)(2,1)S(1)} %get-tuple-element.41), channel_id=1, source_target_pairs={{0,3},{1,2},{2,1},{3,0},{4,7},{5,6},{6,5},{7,4},{8,11},{9,10},{10,... | collective-permute-start | bytes 196616 | tf_op jit(solution)/shard_map/ppermute | solution.py:482
  15.1 15.1 %collective-permute-start.6 = (bf16[152,128]{1,0:T(8,128)(2,1)S(1)}, bf16[152,128]{1,0:T(8,128)(2,1)S(1)}, u32[]{:S(2)}, u32[]{:S(2)}) collective-permute-start(bf16[152,128]{1,0:T(8,128)(2,1)S(1)} %get-tuple-element.43), channel_id=1, source_target_pairs={{0,1},{1,0},{2,3},{3,2},{4,5},{5,4},{6,7},{7,6},{8,9},{9,8},{10,11... | collective-permute-start | bytes 116744 | tf_op jit(solution)/shard_map/ppermute | solution.py:482
  18.3 12.0 %collective-permute-start.7 = (bf16[152,128]{1,0:T(8,128)(2,1)S(1)}, bf16[152,128]{1,0:T(8,128)(2,1)S(1)}, u32[]{:S(2)}, u32[]{:S(2)}) collective-permute-start(bf16[152,128]{1,0:T(8,128)(2,1)S(1)} %get-tuple-element.44), channel_id=1, source_target_pairs={{0,2},{1,3},{2,0},{3,1},{4,6},{5,7},{6,4},{7,5},{8,10},{9,11},{10,... | collective-permute-start | bytes 116744 | tf_op jit(solution)/shard_map/ppermute | solution.py:482
  20.3 10.0 %collective-permute-start.8 = (bf16[152,128]{1,0:T(8,128)(2,1)S(1)}, bf16[152,128]{1,0:T(8,128)(2,1)S(1)}, u32[]{:S(2)}, u32[]{:S(2)}) collective-permute-start(bf16[152,128]{1,0:T(8,128)(2,1)S(1)} %get-tuple-element.45), channel_id=1, source_target_pairs={{0,3},{1,2},{2,1},{3,0},{4,7},{5,6},{6,5},{7,4},{8,11},{9,10},{10,... | collective-permute-start | bytes 116744 | tf_op jit(solution)/shard_map/ppermute | solution.py:482
  23.9 19.4 %collective-permute-start.14 = (bf16[64,1024]{1,0:T(8,128)(2,1)S(1)}, bf16[64,1024]{1,0:T(8,128)(2,1)S(1)}, u32[]{:S(2)}, u32[]{:S(2)}) collective-permute-start(bf16[64,1024]{1,0:T(8,128)(2,1)S(1)} %get-tuple-element.54), channel_id=1, source_target_pairs={{0,1},{1,0},{2,3},{3,2},{4,5},{5,4},{6,7},{7,6},{8,9},{9,8},{10,11... | collective-permute-start | bytes 393224 | tf_op jit(solution)/shard_map/ppermute | solution.py:482
  25.1 15.8 %collective-permute-start.16 = (bf16[64,3072]{1,0:T(8,128)(2,1)S(1)}, bf16[64,3072]{1,0:T(8,128)(2,1)S(1)}, u32[]{:S(2)}, u32[]{:S(2)}) collective-permute-start(bf16[64,3072]{1,0:T(8,128)(2,1)S(1)} %get-tuple-element.57), channel_id=1, source_target_pairs={{0,1},{1,0},{2,3},{3,2},{4,5},{5,4},{6,7},{7,6},{8,9},{9,8},{10,11... | collective-permute-start | bytes 1179656 | tf_op jit(solution)/shard_map/ppermute | solution.py:482
  30.1 34.9 %collective-permute-start.13 = (bf16[64,4096]{1,0:T(8,128)(2,1)S(1)}, bf16[64,4096]{1,0:T(8,128)(2,1)S(1)}, u32[]{:S(2)}, u32[]{:S(2)}) collective-permute-start(bf16[64,4096]{1,0:T(8,128)(2,1)S(1)} %get-tuple-element.52), channel_id=1, source_target_pairs={{0,1},{1,0},{2,3},{3,2},{4,5},{5,4},{6,7},{7,6},{8,9},{9,8},{10,11... | collective-permute-start | bytes 1572872 | tf_op jit(solution)/shard_map/ppermute | solution.py:482
  35.9 29.1 %copy-start = (bf16[128,4096]{1,0:T(8,128)(2,1)S(1)}, bf16[128,4096]{1,0:T(8,128)(2,1)}, u32[]{:S(2)}) copy-start(bf16[128,4096]{1,0:T(8,128)(2,1)} %res_ref.5) | copy-start | bytes 3145732
  35.9 29.1 %copy-start.1 = (f32[4096]{0:T(1024)S(1)}, f32[4096]{0:T(1024)}, u32[]{:S(2)}) copy-start(f32[4096]{0:T(1024)} %param.21) | copy-start | bytes 49156
  36.0 6.8 %collective-permute-start.10 = (bf16[64,4096]{1,0:T(8,128)(2,1)S(1)}, bf16[64,4096]{1,0:T(8,128)(2,1)S(1)}, u32[]{:S(2)}, u32[]{:S(2)}) collective-permute-start(bf16[64,4096]{1,0:T(8,128)(2,1)S(1)} %get-tuple-element.50), channel_id=1, source_target_pairs={{0,1},{1,0},{2,3},{3,2},{4,5},{5,4},{6,7},{7,6},{8,9},{9,8},{10,11... | collective-permute-start | bytes 1572872 | tf_op jit(solution)/shard_map/ppermute | solution.py:482
  40.6 25.8 %collective-permute-start.9 = (bf16[64,4096]{1,0:T(8,128)(2,1)S(1)}, bf16[64,4096]{1,0:T(8,128)(2,1)S(1)}, u32[]{:S(2)}, u32[]{:S(2)}) collective-permute-start(bf16[64,4096]{1,0:T(8,128)(2,1)S(1)} %get-tuple-element.48), channel_id=1, source_target_pairs={{0,1},{1,0},{2,3},{3,2},{4,5},{5,4},{6,7},{7,6},{8,9},{9,8},{10,11... | collective-permute-start | bytes 1572872 | tf_op jit(solution)/shard_map/ppermute | solution.py:482
  41.0 24.1 %collective-permute-start.17 = (bf16[64,3072]{1,0:T(8,128)(2,1)S(1)}, bf16[64,3072]{1,0:T(8,128)(2,1)S(1)}, u32[]{:S(2)}, u32[]{:S(2)}) collective-permute-start(bf16[64,3072]{1,0:T(8,128)(2,1)S(1)} %add_convert_fusion.1), channel_id=1, source_target_pairs={{0,2},{1,3},{2,0},{3,1},{4,6},{5,7},{6,4},{7,5},{8,10},{9,11},{10,... | collective-permute-start | bytes 1179656 | tf_op jit(solution)/shard_map/ppermute | solution.py:482
  42.9 23.5 %collective-permute-start.12 = (bf16[48,4096]{1,0:T(8,128)(2,1)S(1)}, bf16[48,4096]{1,0:T(8,128)(2,1)S(1)}, u32[]{:S(2)}, u32[]{:S(2)}) collective-permute-start(bf16[48,4096]{1,0:T(8,128)(2,1)S(1)} %slice.11), channel_id=1, source_target_pairs={{0,2},{1,3},{2,0},{3,1},{4,6},{5,7},{6,4},{7,5},{8,10},{9,11},{10,... | collective-permute-start | bytes 1179656 | tf_op jit(solution)/shard_map/ppermute | solution.py:482
  43.3 20.3 %collective-permute-start.15 = (bf16[64,1024]{1,0:T(8,128)(2,1)S(1)}, bf16[64,1024]{1,0:T(8,128)(2,1)S(1)}, u32[]{:S(2)}, u32[]{:S(2)}) collective-permute-start(bf16[64,1024]{1,0:T(8,128)(2,1)S(1)} %add_convert_fusion.2), channel_id=1, source_target_pairs={{0,2},{1,3},{2,0},{3,1},{4,6},{5,7},{6,4},{7,5},{8,10},{9,11},{10,... | collective-permute-start | bytes 393224 | tf_op jit(solution)/shard_map/ppermute | solution.py:482
  63.6 5.0 %collective-permute-start.11 = (bf16[16,4096]{1,0:T(8,128)(2,1)S(1)}, bf16[16,4096]{1,0:T(8,128)(2,1)S(1)}, u32[]{:S(2)}, u32[]{:S(2)}) collective-permute-start(bf16[16,4096]{1,0:T(8,128)(2,1)S(1)} %slice.10), channel_id=1, source_target_pairs={{0,2},{1,3},{2,0},{3,1},{4,6},{5,7},{6,4},{7,5},{8,10},{9,11},{10,... | collective-permute-start | bytes 393224 | tf_op jit(solution)/shard_map/ppermute | solution.py:482

commit v6 on v5

--- a/solution.py
+++ b/solution.py
@@ -12,7 +12,7 @@
 EPS = 1e-05
 CHUNKS = (64, 64)
 COLUMNS = 512
-FIRST_PART = 4
+FIRST_EIGHTHS = 3
 GROUP_ROWS = 256
 
 F32 = jnp.float32
@@ -164,18 +164,18 @@
 
     def body(m, *refs):
         q_refs, refs = refs[: devices // 2], refs[devices // 2 :]
-        bundle_ref, cache_ref, pq_hbm, dq_hbm, e_hbm = refs[:5]
+        bundle_ref, cache_ref, pq_ref, dq_hbm, e_hbm = refs[:5]
         o_refs, refs = refs[5 : 5 + devices], refs[5 + devices :]
         q_ref, e_ref, q_all, sums, sem = refs
         me = m[0]
         lane = pl.multiple_of(me * local_heads // group * HEAD_DIM, HEAD_DIM)
         copies = [
-            pltpu.make_async_copy(pq_hbm, q_ref.at[0:prompt_rows, :], sem.at[0]),
-            pltpu.make_async_copy(dq_hbm, q_ref.at[prompt_rows : prompt_rows + rows, :], sem.at[1]),
-            pltpu.make_async_copy(e_hbm.at[:, :, pl.ds(lane, HEAD_DIM)], e_ref, sem.at[2]),
+            pltpu.make_async_copy(dq_hbm, q_ref.at[prompt_rows : prompt_rows + rows, :], sem.at[0]),
+            pltpu.make_async_copy(e_hbm.at[:, :, pl.ds(lane, HEAD_DIM)], e_ref, sem.at[1]),
         ]
         for copy in copies:
             copy.start()
+        q_ref[0:prompt_rows, :] = pq_ref[...]
         for k in range(devices):
             base = bundle.shape[0] - (devices // 2 - k // 2) * part_rows if k % 2 else 0
             q_ref_k = bundle_ref if k % 2 else q_refs[k // 2]
@@ -224,9 +224,9 @@
 
     outs = pl.pallas_call(
         body,
-        in_specs=[smem()] + [in_vmem()] * (devices // 2 + 2) + [in_hbm()] * 3,
+        in_specs=[smem()] + [in_vmem()] * (devices // 2 + 3) + [in_hbm()] * 2,
         out_specs=[in_vmem()] * (devices + 2),
-        scratch_shapes=[pltpu.VMEM((devices, part_rows, HEAD_DIM), F32)] * 2 + [pltpu.SemaphoreType.DMA((3,))],
+        scratch_shapes=[pltpu.VMEM((devices, part_rows, HEAD_DIM), F32)] * 2 + [pltpu.SemaphoreType.DMA((2,))],
         out_shape=[jax.ShapeDtypeStruct((part_rows + 3 * stat_rows, HEAD_DIM), BF16)] * devices
         + [
             pltpu.VMEM((prompt_rows + rows, prompt_queries.shape[1]), BF16),
@@ -235,7 +235,7 @@
         compiler_params=params(12),
         cost_estimate=busy(12),
         name="decode",
-    )(meta, *queries, bundle, cache, to_hbm(prompt_queries), to_hbm(decode_queries), to_hbm(entries))
+    )(meta, *queries, bundle, cache, prompt_queries, to_hbm(decode_queries), to_hbm(entries))
     return outs[:devices], outs[devices], outs[devices + 1]
 
 
@@ -288,31 +288,37 @@
     )(*parts, queries, entries)
 
 
-def product(att, w, start, stop, half, keep_ref, give_ref):
+def product(att, w, start, stop, targets):
     for c in range(start, stop, COLUMNS):
-        out = jnp.dot(att[...], w[:, c : c + COLUMNS], preferred_element_type=F32).astype(BF16)
-        keep_ref[:, c - start : c - start + COLUMNS] = out[:half]
-        give_ref[:, c - start : c - start + COLUMNS] = out[half:]
-
-
-def project(att, weight, start):
-    rows, model = att.shape[0], weight.shape[1]
-
-    def body(att_ref, w, keep_ref, give_ref):
-        product(att_ref, w, start, model, rows // 2, keep_ref, give_ref)
+        width = min(COLUMNS, stop - c)
+        out = jnp.dot(att, w[:, c : c + width], preferred_element_type=F32).astype(BF16)
+        row = 0
+        for target in targets:
+            target[:, c - start : c - start + width] = out[row : row + target.shape[0]]
+            row += target.shape[0]
+
+
+def project(atts, weight, start):
+    model = weight.shape[1]
+    n = len(atts)
+
+    def body(*refs):
+        att = jnp.concatenate([ref[...] for ref in refs[:n]], axis=0)
+        product(att, refs[n], start, model, refs[n + 1 :])
 
     return pl.pallas_call(
         body,
-        in_specs=[in_vmem()] * 2,
-        out_specs=[in_vmem()] * 2,
-        out_shape=[jax.ShapeDtypeStruct((rows // 2, model - start), BF16)] * 2,
+        in_specs=[in_vmem()] * (n + 1),
+        out_specs=[in_vmem()] * n,
+        out_shape=[jax.ShapeDtypeStruct((att.shape[0], model - start), BF16) for att in atts],
         compiler_params=params(8),
         cost_estimate=busy(2),
         name="project",
-    )(att, weight)
-
-
-def attend(slots, first, count, block, queries, history, fresh, bundle, decoded, weight, meta, h_rows, p_rows, columns):
+    )(*atts, weight)
+
+
+def attend(order, first, count, block, queries, pieces, joined, decoded, weight, meta, h_rows, p_rows, columns):
+    history, fresh, bundle = pieces
     devices = len(history) + 1
     held = list(history)
     p_pad = fresh[0].shape[0] // 2
@@ -321,23 +327,17 @@
     model = weight.shape[1]
     h_keys, p_keys = devices * h_rows, devices * p_pad
     keys = h_keys + p_keys
-    order = [s for s in slots if s % 2 == 0] + [s for s in slots if s % 2 == 1]
-    half = len(order) // 2 * count
+    shares = [sum(count for s in order if s % 2 == parity) for parity in (0, 1)]
+    shares = [share for share in shares if share]
     factor = HEAD_DIM ** (-0.5) * float(np.log2(np.e))
     per = max(1, min(local_heads, GROUP_ROWS // count))
     has_decode = decoded is not None
     decode_rows = decoded.shape[0] if has_decode else 0
 
-    def body(m, q, *refs):
-        bundle_ref, rest = refs[0], refs[1:]
+    def join_pieces(refs, k_all, v_all):
         n = devices - 1
-        cached = {1: (bundle_ref, 0), **{k: (ref, 0) for k, ref in zip(held, rest[:n])}}
-        own = {1: (bundle_ref, 2 * h_rows), **{k: (ref, 0) for k, ref in zip(held, rest[n : 2 * n])}}
-        rest = rest[2 * n :]
-        if has_decode:
-            dec_ref, rest = rest[0], rest[1:]
-        w, keep_ref, give_ref, att, k_all, v_all = rest
-        me, valid_rows = m[0], m[1]
+        cached = {1: (refs[0], 0), **{k: (ref, 0) for k, ref in zip(held, refs[1:])}}
+        own = {1: (refs[0], 2 * h_rows), **{k: (ref, 0) for k, ref in zip(held, refs[1 + n :])}}
         for k in range(devices):
             for part, dst in ((0, k_all), (1, v_all)):
                 for copy in range(2 - part):
@@ -349,6 +349,19 @@
                     row += part * p_pad
                     dst[h_keys + k * p_pad : h_keys + (k + 1) * p_pad, lanes] = ref[row : row + p_pad, :]
         v_all[:, HEAD_DIM:] = jnp.ones((keys, HEAD_DIM), BF16)
+
+    def body(m, q, w, *refs):
+        if has_decode:
+            dec_ref, refs = refs[0], refs[1:]
+        if joined is None:
+            parts, refs = refs[: 2 * devices - 1], refs[2 * devices - 1 :]
+            k_all, v_all = refs[-2:]
+            join_pieces(parts, k_all, v_all)
+            targets, att = refs[:-3], refs[-3]
+        else:
+            k_all, v_all = refs[:2]
+            targets, att = refs[2:-1], refs[-1]
+        me, valid_rows = m[0], m[1]
         column = lax.broadcasted_iota(jnp.int32, (1, h_keys), 1)
         place = ((column // h_rows) ^ me) * h_rows + column % h_rows
         history_bias = jnp.where(place < valid_rows, 0.0, MASKED)
@@ -396,22 +409,27 @@
                 def _():
                     att[(i + 1) * count - decode_rows : (i + 1) * count, :] = dec_ref[...]
 
-        product(att, w, 0, columns, half, keep_ref, give_ref)
+        product(att[...], w, 0, columns, targets)
 
     flops = 2 * len(order) * count * (2 * local_width * keys + local_width * model)
-    n_vmem = 1 + 2 * devices + has_decode
-    return pl.pallas_call(
+    operands = [queries, weight] + ([decoded] if has_decode else [])
+    out_shape = [jax.ShapeDtypeStruct((share, columns), BF16) for share in shares]
+    out_shape.append(jax.ShapeDtypeStruct((len(order) * count, local_width), BF16))
+    if joined is None:
+        operands += [bundle, *history.values(), *fresh.values()]
+        out_shape += [jax.ShapeDtypeStruct((keys, 2 * HEAD_DIM), BF16)] * 2
+    else:
+        operands += joined
+    outs = pl.pallas_call(
         body,
-        in_specs=[smem()] + [in_vmem()] * n_vmem,
-        out_specs=[in_vmem()] * 3,
-        out_shape=[jax.ShapeDtypeStruct((half, columns), BF16)] * 2 + [pltpu.VMEM((2 * half, local_width), BF16)],
-        scratch_shapes=[
-            pltpu.VMEM((keys, 2 * HEAD_DIM), BF16),
-            pltpu.VMEM((keys, 2 * HEAD_DIM), BF16),
-        ],
+        in_specs=[smem()] + [in_vmem()] * len(operands),
+        out_specs=[in_vmem()] * len(out_shape),
+        out_shape=out_shape,
         compiler_params=params(24),
         cost_estimate=pl.CostEstimate(flops=flops, transcendentals=0, bytes_accessed=weight.size * 2),
-    )(meta, queries, bundle, *history.values(), *fresh.values(), *([decoded] if has_decode else []), weight)
+    )(meta, *operands)
+    n = len(shares)
+    return outs[:n], outs[n], joined or list(outs[n + 1 :])
 
 
 def finish(first, begin, residual, own, given, crossed, gain, previous):
@@ -498,10 +516,26 @@
     parts = swapped(parts)
     decoded = decode_join(parts, own_query, entries, local_heads)
 
-    def attended(slots, first, count, decoded, columns):
-        return attend(
-            slots, first, count, block, queries, history, fresh, bundle, decoded, out_weight, meta, h_rows, p_rows, columns
+    joined = None
+
+    def attended(order, first, count, decoded, columns):
+        nonlocal joined
+        outs, att, joined = attend(
+            order,
+            first,
+            count,
+            block,
+            queries,
+            (history, fresh, bundle),
+            joined,
+            decoded,
+            out_weight,
+            meta,
+            h_rows,
+            p_rows,
+            columns,
         )
+        return outs, att
 
     def chip_sum(keep, give):
         return keep.astype(F32) + swap(give, 1).astype(F32)
@@ -516,28 +550,29 @@
     if any(c % 16 for c in chunks):
         chunks = [block]
     model = out_weight.shape[1]
-    others = list(range(2, devices))
+    stays, leaves = list(range(2, devices, 2)), list(range(3, devices, 2))
     crossed, first = [], 0
     for count in chunks:
         last = first + count == block
-        columns = model if last else model // FIRST_PART
-        keep, give, att = attended(others, first, count, decoded if last else None, columns)
-        pair = chip_sum(keep, give)
         if last:
+            (keep, give), _ = attended(stays + leaves, first, count, decoded, model)
+            pair = chip_sum(keep, give)
             cut = count - 16 if count > 16 else 0
             for start, stop in [(0, cut), (cut, count)] if cut else [(0, count)]:
                 crossed.append((first + start, cross(pair, count, start, stop)))
         else:
-            pieces = [cross(pair, count, 0, count)]
-            keep, give = project(att, out_weight, columns)
-            pair = chip_sum(keep, give)
-            pieces.append(cross(pair, count, 0, count))
+            columns = model // 8 * FIRST_EIGHTHS
+            (give,), gone = attended(leaves, first, count, None, columns)
+            (keep,), kept = attended(stays, first, count, None, columns)
+            pieces = [cross(chip_sum(keep, give), count, 0, count)]
+            keep, give = project([kept, gone], out_weight, columns)
+            pieces.append(cross(chip_sum(keep, give), count, 0, count))
             crossed.append((first, [piece for both in zip(*pieces) for piece in both]))
         first += count
     owned, first = [], 0
     for count in chunks:
         here = decoded if first + count == block else None
-        own, give, _ = attended([0, 1], first, count, here, model)
+        (own, give), _ = attended([0, 1], first, count, here, model)
         owned.append((first, own, swap(give, 1)))
         first += count
     gain = norm_gain[None, :]

time: 69.8 us -> 73.8 us (1.057)
  waiting for transfers between devices: 23.7 us -> 29 us
  starting transfers between devices: 16.2 us -> 13.6 us
  Pallas kernels: 27.6 us -> 28.9 us
    ppermute x18, waiting for transfers between devices: 23.7 us -> 29 us  [swap(): return lax.ppermute(value, 'tp', [(i, i ^ k) for i in range(devices)])]
    ppermute x18, starting transfers between devices: 16.2 us -> 13.6 us  [swap(): return lax.ppermute(value, 'tp', [(i, i ^ k) for i in range(devices)])]
    pallas_call x6 -> x7, Pallas kernels: 21 us -> 22.3 us  [the longest x5 18.3 us: attend(): pl.pallas_call(body, in_specs=[smem()] + [in_vmem()] * len(operands), out...]
  transfers between devices with their start and end apart: 18 -> 18, of which waited for: 4 -> 8; matrix products, arithmetic and copies ran while one was open for 1% -> 1% of each run, Pallas kernels for 36% -> 22%
where the time goes in v6:
time: 73.8 us; the launch traced here: 73.6 us
  waiting for transfers between devices  29 us (39%)
  Pallas kernels  28.9 us (39%)
  starting transfers between devices  13.6 us (18%)
  between operations  1.71 us (2%)
    ppermute x18, waiting for transfers between devices, swap(): return lax.ppermute(value, 'tp', [(i, i ^ k) for i in range(devices)])  29 us
    pallas_call x5, Pallas kernels, attend(): pl.pallas_call(body, in_specs=[smem()] + [in_vmem()] * len(operands), out...  18.3 us
    ppermute x18, starting transfers between devices, swap(): return lax.ppermute(value, 'tp', [(i, i ^ k) for i in range(devices)])  13.6 us
    pallas_call x3, Pallas kernels, finish(): pl.pallas_call(body, in_specs=[in_vmem()] * n_in + [hbm()] * len(previous...  3.44 us
    pallas_call x1, Pallas kernels, decode_partials(): pl.pallas_call(body, in_specs=[smem()] + [in_vmem()] * (devices // 2 + 3)...  3.13 us
  transfers between devices with their start and end apart: 18, of which 8 were waited for; matrix products, arithmetic and copies ran while one was open for 1% of the time, Pallas kernels for 22%

profile of v6, /device:TPU:0, one launch (start us, length us, event | category | flops | bytes accessed | tf_op | source)
XLA Modules:
  0.0 73.6 jit_solution(15771218000961307339)
XLA Ops:
  0.7 1.3 %pack_history.1 = (bf16[512,128]{1,0:T(8,128)(2,1)S(1)}, bf16[512,128]{1,0:T(8,128)(2,1)S(1)}, bf16[512,128]{1,0:T(8,128)(2,1)S(1)}, bf16[512,128]{1,0:T(8,128)(2,1)S(1)}, bf16[128,128]{1,0:T(8,128)(2,1)S(1)}) custom-call(bf16[2,256,512]{2,1,0:T(8,128)(2,1)} %h_hbm.1, bf16[16,1024]{1,0:T(8,128)(2,1)} %refs_5_.1), custom_call_target="tpu_custom_call" | custom-call | flops 3000000000 | bytes 6000000 | tf_op jit(solution)/shard_map/pack_history/pallas_call | solution.py:86
  2.0 3.1 %collective-permute-start = (bf16[128,128]{1,0:T(8,128)(2,1)S(1)}, bf16[128,128]{1,0:T(8,128)(2,1)S(1)}, u32[]{:S(2)}, u32[]{:S(2)}) collective-permute-start(bf16[128,128]{1,0:T(8,128)(2,1)S(1)} %get-tuple-element.35.refs_5_.refs_0_.refs_4_), channel_id=1, source_target_pairs={{0,2},{1,3},{2,0},{3,1},{4,6},{5,7},{6,4},{7,5},{8,10},{9,11},{10,... | collective-permute-start | bytes 98312 | tf_op jit(solution)/shard_map/ppermute | solution.py:500
  5.8 1.1 %collective-permute-done.refs_6_.refs_1_ = bf16[128,128]{1,0:T(8,128)(2,1)S(1)} collective-permute-done((bf16[128,128]{1,0:T(8,128)(2,1)S(1)}, bf16[128,128]{1,0:T(8,128)(2,1)S(1)}, u32[]{:S(2)}, u32[]{:S(2)}) %collective-permute-start) | collective-permute-done | bytes 32800 | tf_op jit(solution)/shard_map/ppermute | solution.py:500
  6.9 0.6 pack_fresh.1
  7.6 2.1 %collective-permute-start.5 = (bf16[512,128]{1,0:T(8,128)(2,1)S(1)}, bf16[512,128]{1,0:T(8,128)(2,1)S(1)}, u32[]{:S(2)}, u32[]{:S(2)}) collective-permute-start(bf16[512,128]{1,0:T(8,128)(2,1)S(1)} %get-tuple-element.45), channel_id=1, source_target_pairs={{0,2},{1,3},{2,0},{3,1},{4,6},{5,7},{6,4},{7,5},{8,10},{9,11},{10,... | collective-permute-start | bytes 393224 | tf_op jit(solution)/shard_map/ppermute | solution.py:500
  9.8 1.7 %collective-permute-start.7 = (bf16[256,128]{1,0:T(8,128)(2,1)S(1)}, bf16[256,128]{1,0:T(8,128)(2,1)S(1)}, u32[]{:S(2)}, u32[]{:S(2)}) collective-permute-start(bf16[256,128]{1,0:T(8,128)(2,1)S(1)} %get-tuple-element.48), channel_id=1, source_target_pairs={{0,2},{1,3},{2,0},{3,1},{4,6},{5,7},{6,4},{7,5},{8,10},{9,11},{10,... | collective-permute-start | bytes 196616 | tf_op jit(solution)/shard_map/ppermute | solution.py:500
  11.6 3.1 %decode.1 = (bf16[152,128]{1,0:T(8,128)(2,1)S(1)}, bf16[152,128]{1,0:T(8,128)(2,1)S(1)}, bf16[152,128]{1,0:T(8,128)(2,1)S(1)}, bf16[152,128]{1,0:T(8,128)(2,1)S(...) custom-call(s32[18]{0:T(128)S(1)} %pad_add_fusion.m, ...), custom_call_target="tpu_custom_call" | custom-call | flops 6000000000 | bytes 12000000 | tf_op jit(solution)/shard_map/decode/pallas_call | solution.py:225
  14.7 3.6 %collective-permute-done.7.refs_5_ = bf16[256,128]{1,0:T(8,128)(2,1)S(1)} collective-permute-done((bf16[256,128]{1,0:T(8,128)(2,1)S(1)}, bf16[256,128]{1,0:T(8,128)(2,1)S(1)}, u32[]{:S(2)}, u32[]{:S(2)}) %collective-permute-start.7) | collective-permute-done | bytes 65568 | tf_op jit(solution)/shard_map/ppermute | solution.py:500
  18.3 0.9 %collective-permute-done.8.refs_6_ = bf16[256,128]{1,0:T(8,128)(2,1)S(1)} collective-permute-done((bf16[256,128]{1,0:T(8,128)(2,1)S(1)}, bf16[256,128]{1,0:T(8,128)(2,1)S(1)}, u32[]{:S(2)}, u32[]{:S(2)}) %collective-permute-start.8) | collective-permute-done | bytes 65568 | tf_op jit(solution)/shard_map/ppermute | solution.py:500
  19.2 2.5 %shard_map.122 = (bf16[64,1536]{1,0:T(8,128)(2,1)S(1)}, bf16[64,1024]{1,0:T(8,128)(2,1)S(1)}, bf16[1536,256]{1,0:T(8,128)(2,1)S(1)}, bf16[1536,256]{1,0:T(8,128)(2,1)S(1)}) custom-call(s32[18]{0:T(128)S(1)} %pad_add_fusion.m, bf16[512,1024]{1,0:T(8,128)(2,1)S(1)} %get-tuple-element.38.q, bf16[1024,4096]{1,0:T(8,128)(2,1)S(1)} %bitcast.3, ...), custom_call_target="tpu_custom_call" | custom-call | flops 939524096 | bytes 8388608 | tf_op jit(solution)/shard_map/pallas_call | solution.py:423
  21.8 4.7 %shard_map.125 = (bf16[64,4096]{1,0:T(8,128)(2,1)S(1)}, bf16[64,4096]{1,0:T(8,128)(2,1)S(1)}, bf16[128,1024]{1,0:T(8,128)(2,1)}) custom-call(s32[18]{0:T(128)S(1)} %pad_add_fusion.m, bf16[512,1024]{1,0:T(8,128)(2,1)S(1)} %get-tuple-element.38.q, bf16[1024,4096]{1,0:T(8,128)(2,1)S(1)} %bitcast.3, bf16[1536,256]{1,0:T(8,128)(2,1)S(1)} %get-tuple-element.50.refs_1_.refs_0_, ...), custom_call_target="tpu_custom_call" | custom-call | flops 1879048192 | bytes 8388608 | tf_op jit(solution)/shard_map/pallas_call | solution.py:423
  26.4 2.4 %shard_map.126 = (bf16[64,1536]{1,0:T(8,128)(2,1)S(1)}, bf16[64,1024]{1,0:T(8,128)(2,1)S(1)}) custom-call(s32[18]{0:T(128)S(1)} %pad_add_fusion.m, bf16[512,1024]{1,0:T(8,128)(2,1)S(1)} %get-tuple-element.38.q, bf16[1024,4096]{1,0:T(8,128)(2,1)S(1)} %bitcast.3, bf16[1536,256]{1,0:T(8,128)(2,1)S(1)} %get-tuple-element.50.refs_1_.refs_0_, ...), custom_call_target="tpu_custom_call" | custom-call | flops 939524096 | bytes 8388608 | tf_op jit(solution)/shard_map/pallas_call | solution.py:423
  29.0 1.7 %collective-permute-start.3 = (bf16[152,128]{1,0:T(8,128)(2,1)S(1)}, bf16[152,128]{1,0:T(8,128)(2,1)S(1)}, u32[]{:S(2)}, u32[]{:S(2)}) collective-permute-start(bf16[152,128]{1,0:T(8,128)(2,1)S(1)} %get-tuple-element.41), channel_id=1, source_target_pairs={{0,2},{1,3},{2,0},{3,1},{4,6},{5,7},{6,4},{7,5},{8,10},{9,11},{10,... | collective-permute-start | bytes 116744 | tf_op jit(solution)/shard_map/ppermute | solution.py:500
  30.8 0.4 collective-permute-start.13
  31.3 0.9 %project.1 = (bf16[64,2560]{1,0:T(8,128)(2,1)S(1)}, bf16[64,2560]{1,0:T(8,128)(2,1)S(1)}) custom-call(bf16[64,1024]{1,0:T(8,128)(2,1)S(1)} %get-tuple-element.60.refs_0_, bf16[64,1024]{1,0:T(8,128)(2,1)S(1)} %get-tuple-element.61.refs_1_, bf16[1024,4096]{1,0:T(8,128)(2,1)S(1)} %bitcast.3), custom_call_target="tpu_custom_call" | custom-call | flops 1000000000 | bytes 2000000 | tf_op jit(solution)/shard_map/project/pallas_call | solution.py:309
  32.2 0.5 collective-permute-start.16
  32.6 0.4 collective-permute-done.3.refs_2_
  33.0 1.5 %collective-permute-done.4.refs_3_ = bf16[152,128]{1,0:T(8,128)(2,1)S(1)} collective-permute-done((bf16[152,128]{1,0:T(8,128)(2,1)S(1)}, bf16[152,128]{1,0:T(8,128)(2,1)S(1)}, u32[]{:S(2)}, u32[]{:S(2)}) %collective-permute-start.4) | collective-permute-done | bytes 38944 | tf_op jit(solution)/shard_map/ppermute | solution.py:500
  34.5 1.2 %join.1.refs_0_ = bf16[16,1024]{1,0:T(8,128)(2,1)S(1)} custom-call(bf16[152,128]{1,0:T(8,128)(2,1)S(1)} %get-tuple-element.39.refs_0_, bf16[152,128]{1,0:T(8,128)(2,1)S(1)} %collective-permute-done.2.refs_1_, bf16[152,128]{1,0:T(8,128)(2,1)S(1)} %collective-permute-done.3.refs_2_, bf16[152,128]{1,0:T(8,128)(2,1)S(1)} %collective-permute-done.4.refs_3_, ...), custom_call_target="tpu_custom_call" | custom-call | flops 500000000 | bytes 1000000 | tf_op jit(solution)/shard_map/join/pallas_call | solution.py:279
  35.7 4.4 %shard_map.123 = (bf16[64,4096]{1,0:T(8,128)(2,1)S(1)}, bf16[64,4096]{1,0:T(8,128)(2,1)S(1)}, bf16[128,1024]{1,0:T(8,128)(2,1)}) custom-call(s32[18]{0:T(128)S(1)} %pad_add_fusion.m, bf16[512,1024]{1,0:T(8,128)(2,1)S(1)} %get-tuple-element.38.q, bf16[1024,4096]{1,0:T(8,128)(2,1)S(1)} %bitcast.3, bf16[16,1024]{1,0:T(8,128)(2,1)S(1)} %join.1.refs_0_, ...), custom_call_target="tpu_custom_call" | custom-call | flops 1879048192 | bytes 8388608 | tf_op jit(solution)/shard_map/pallas_call | solution.py:423
  40.3 4.2 %shard_map.124 = (bf16[64,4096]{1,0:T(8,128)(2,1)S(1)}, bf16[64,4096]{1,0:T(8,128)(2,1)S(1)}, bf16[128,1024]{1,0:T(8,128)(2,1)}) custom-call(s32[18]{0:T(128)S(1)} %pad_add_fusion.m, bf16[512,1024]{1,0:T(8,128)(2,1)S(1)} %get-tuple-element.38.q, bf16[1024,4096]{1,0:T(8,128)(2,1)S(1)} %bitcast.3, bf16[16,1024]{1,0:T(8,128)(2,1)S(1)} %join.1.refs_0_, ...), custom_call_target="tpu_custom_call" | custom-call | flops 1879048192 | bytes 8388608 | tf_op jit(solution)/shard_map/pallas_call | solution.py:423
  44.6 0.5 collective-permute-start.10
  45.1 0.4 collective-permute-start.17
  45.6 1.0 %collective-permute-done.10 = bf16[64,4096]{1,0:T(8,128)(2,1)S(1)} collective-permute-done((bf16[64,4096]{1,0:T(8,128)(2,1)S(1)}, bf16[64,4096]{1,0:T(8,128)(2,1)S(1)}, u32[]{:S(2)}, u32[]{:S(2)}) %collective-permute-start.10) | collective-permute-done | bytes 524320 | tf_op jit(solution)/shard_map/ppermute | solution.py:500
  46.8 0.7 collective-permute-start.12
  47.5 1.4 %collective-permute-start.15 = (bf16[64,1536]{1,0:T(8,128)(2,1)S(1)}, bf16[64,1536]{1,0:T(8,128)(2,1)S(1)}, u32[]{:S(2)}, u32[]{:S(2)}) collective-permute-start(bf16[64,1536]{1,0:T(8,128)(2,1)S(1)} %add_convert_fusion.2), channel_id=1, source_target_pairs={{0,2},{1,3},{2,0},{3,1},{4,6},{5,7},{6,4},{7,5},{8,10},{9,11},{10,... | collective-permute-start | bytes 589832 | tf_op jit(solution)/shard_map/ppermute | solution.py:500
  49.0 18.6 %collective-permute-done.15.refs_0_ = bf16[64,1536]{1,0:T(8,128)(2,1)S(1)} collective-permute-done((bf16[64,1536]{1,0:T(8,128)(2,1)S(1)}, bf16[64,1536]{1,0:T(8,128)(2,1)S(1)}, u32[]{:S(2)}, u32[]{:S(2)}) %collective-permute-start.15) | collective-permute-done | bytes 196640 | tf_op jit(solution)/shard_map/ppermute | solution.py:500
  67.6 0.5 collective-permute-start.11
  68.1 1.4 %shard_map.127 = (bf16[128,4096]{1,0:T(8,128)(2,1)}, bf16[128,4096]{1,0:T(8,128)(2,1)}) custom-call(bf16[128,4096]{1,0:T(8,128)(2,1)S(1)} %copy-done, bf16[64,4096]{1,0:T(8,128)(2,1)S(1)} %get-tuple-element.56.own_ref, bf16[64,4096]{1,0:T(8,128)(2,1)S(1)} %collective-permute-done.13.given_ref, bf16[64,1536]{1,0:T(8,128)(2,1)S(1)} %collective-permute-done.15.refs_0_, ...), custom_call_target="tpu_custom_call" | custom-call | flops 1000000000 | bytes 2000000 | tf_op jit(solution)/shard_map/pallas_call | solution.py:465
  69.5 1.2 %shard_map.128 = (bf16[128,4096]{1,0:T(8,128)(2,1)}, bf16[128,4096]{1,0:T(8,128)(2,1)}) custom-call(bf16[128,4096]{1,0:T(8,128)(2,1)S(1)} %copy-done, bf16[64,4096]{1,0:T(8,128)(2,1)S(1)} %get-tuple-element.52.own_ref, bf16[64,4096]{1,0:T(8,128)(2,1)S(1)} %collective-permute-done.9.given_ref, ...), custom_call_target="tpu_custom_call", output_to_operand_aliasing={{0}: (5, {}), {1}: (6, {})} | custom-call | flops 1000000000 | bytes 2000000 | tf_op jit(solution)/shard_map/pallas_call | solution.py:465
  70.7 1.9 %collective-permute-done.11.refs_0_ = bf16[16,4096]{1,0:T(8,128)(2,1)S(1)} collective-permute-done((bf16[16,4096]{1,0:T(8,128)(2,1)S(1)}, bf16[16,4096]{1,0:T(8,128)(2,1)S(1)}, u32[]{:S(2)}, u32[]{:S(2)}) %collective-permute-start.11) | collective-permute-done | bytes 131104 | tf_op jit(solution)/shard_map/ppermute | solution.py:500
  72.5 0.9 %shard_map.129 = (bf16[128,4096]{1,0:T(8,128)(2,1)}, bf16[128,4096]{1,0:T(8,128)(2,1)}) custom-call(bf16[128,4096]{1,0:T(8,128)(2,1)S(1)} %copy-done, bf16[64,4096]{1,0:T(8,128)(2,1)S(1)} %get-tuple-element.52.own_ref, bf16[64,4096]{1,0:T(8,128)(2,1)S(1)} %collective-permute-done.9.given_ref, ...), custom_call_target="tpu_custom_call", output_to_operand_aliasing={{0}: (5, {}), {1}: (6, {})} | custom-call | flops 1000000000 | bytes 2000000 | tf_op jit(solution)/shard_map/pallas_call | solution.py:465
  (44 shorter events, 1.1 us)
Async XLA Ops:
  0.6 5.0 %copy-start.4 = (s32[16]{0:T(128)S(1)}, s32[16]{0:T(128)}, u32[]{:S(2)}) copy-start(s32[16]{0:T(128)} %param.17) | copy-start | bytes 196
  0.6 5.1 %copy-start.3 = (bf16[2,124,512]{2,0,1:T(2,128)(2,1)S(1)}, bf16[2,124,512]{2,0,1:T(2,128)(2,1)}, u32[]{:S(2)}) copy-start(bf16[2,124,512]{2,0,1:T(2,128)(2,1)} %param.12) | copy-start | bytes 761860
  2.0 5.0 %collective-permute-start = (bf16[128,128]{1,0:T(8,128)(2,1)S(1)}, bf16[128,128]{1,0:T(8,128)(2,1)S(1)}, u32[]{:S(2)}, u32[]{:S(2)}) collective-permute-start(bf16[128,128]{1,0:T(8,128)(2,1)S(1)} %get-tuple-element.35.refs_5_.refs_0_.refs_4_), channel_id=1, source_target_pairs={{0,2},{1,3},{2,0},{3,1},{4,6},{5,7},{6,4},{7,5},{8,10},{9,11},{10,... | collective-permute-start | bytes 98312 | tf_op jit(solution)/shard_map/ppermute | solution.py:500
  5.8 5.8 %slice-start.2 = ((s8[6291456]{0:T(1024)(128)(4,1)}), s8[4194304]{0:T(1024)(128)(4,1)S(1)}, s32[]{:S(2)}) async-start(s8[6291456]{0:T(1024)(128)(4,1)} %bitcast.7), calls=%async_computation.2 | async-start | bytes 8388608
  6.9 4.6 %slice-start.3 = ((s8[6291456]{0:T(1024)(128)(4,1)}), s8[2097152]{0:T(1024)(128)(4,1)S(1)}, s32[]{:S(2)}) async-start(s8[6291456]{0:T(1024)(128)(4,1)} %bitcast.7), calls=%async_computation.3 | async-start | bytes 4194304
  6.9 4.6 %copy-start.2 = (bf16[496,1024]{1,0:T(8,128)(2,1)S(1)}, bf16[496,1024]{1,0:T(8,128)(2,1)}, u32[]{:S(2)}) copy-start(bf16[496,1024]{1,0:T(8,128)(2,1)} %refs_4_.1) | copy-start | bytes 3047428
  7.6 4.0 %collective-permute-start.1 = (bf16[1024,128]{1,0:T(8,128)(2,1)S(1)}, bf16[1024,128]{1,0:T(8,128)(2,1)S(1)}, u32[]{:S(2)}, u32[]{:S(2)}) collective-permute-start(bf16[1024,128]{1,0:T(8,128)(2,1)S(1)} %get-tuple-element.37), channel_id=1, source_target_pairs={{0,1},{1,0},{2,3},{3,2},{4,5},{5,4},{6,7},{7,6},{8,9},{9,8},{10,11... | collective-permute-start | bytes 786440 | tf_op jit(solution)/shard_map/ppermute | solution.py:500
  7.6 11.5 %collective-permute-start.5 = (bf16[512,128]{1,0:T(8,128)(2,1)S(1)}, bf16[512,128]{1,0:T(8,128)(2,1)S(1)}, u32[]{:S(2)}, u32[]{:S(2)}) collective-permute-start(bf16[512,128]{1,0:T(8,128)(2,1)S(1)} %get-tuple-element.45), channel_id=1, source_target_pairs={{0,2},{1,3},{2,0},{3,1},{4,6},{5,7},{6,4},{7,5},{8,10},{9,11},{10,... | collective-permute-start | bytes 393224 | tf_op jit(solution)/shard_map/ppermute | solution.py:500
  9.7 9.5 %collective-permute-start.6 = (bf16[512,128]{1,0:T(8,128)(2,1)S(1)}, bf16[512,128]{1,0:T(8,128)(2,1)S(1)}, u32[]{:S(2)}, u32[]{:S(2)}) collective-permute-start(bf16[512,128]{1,0:T(8,128)(2,1)S(1)} %get-tuple-element.46), channel_id=1, source_target_pairs={{0,3},{1,2},{2,1},{3,0},{4,7},{5,6},{6,5},{7,4},{8,11},{9,10},{10,... | collective-permute-start | bytes 393224 | tf_op jit(solution)/shard_map/ppermute | solution.py:500
  9.8 8.5 %collective-permute-start.7 = (bf16[256,128]{1,0:T(8,128)(2,1)S(1)}, bf16[256,128]{1,0:T(8,128)(2,1)S(1)}, u32[]{:S(2)}, u32[]{:S(2)}) collective-permute-start(bf16[256,128]{1,0:T(8,128)(2,1)S(1)} %get-tuple-element.48), channel_id=1, source_target_pairs={{0,2},{1,3},{2,0},{3,1},{4,6},{5,7},{6,4},{7,5},{8,10},{9,11},{10,... | collective-permute-start | bytes 196616 | tf_op jit(solution)/shard_map/ppermute | solution.py:500
  11.5 7.7 %slice-start = ((s8[8388608]{0:T(1024)(128)(4,1)}), s8[4194304]{0:T(1024)(128)(4,1)S(1)}, s32[]{:S(2)}) async-start(s8[8388608]{0:T(1024)(128)(4,1)} %bitcast.2), calls=%async_computation | async-start | bytes 8388608
  11.5 7.7 %slice-start.1 = ((s8[8388608]{0:T(1024)(128)(4,1)}), s8[4194304]{0:T(1024)(128)(4,1)S(1)}, s32[]{:S(2)}) async-start(s8[8388608]{0:T(1024)(128)(4,1)} %bitcast.2), calls=%async_computation.1 | async-start | bytes 8388608
  11.5 7.7 %collective-permute-start.8 = (bf16[256,128]{1,0:T(8,128)(2,1)S(1)}, bf16[256,128]{1,0:T(8,128)(2,1)S(1)}, u32[]{:S(2)}, u32[]{:S(2)}) collective-permute-start(bf16[256,128]{1,0:T(8,128)(2,1)S(1)} %get-tuple-element.49), channel_id=1, source_target_pairs={{0,3},{1,2},{2,1},{3,0},{4,7},{5,6},{6,5},{7,4},{8,11},{9,10},{10,... | collective-permute-start | bytes 196616 | tf_op jit(solution)/shard_map/ppermute | solution.py:500
  28.9 3.3 %collective-permute-start.2 = (bf16[152,128]{1,0:T(8,128)(2,1)S(1)}, bf16[152,128]{1,0:T(8,128)(2,1)S(1)}, u32[]{:S(2)}, u32[]{:S(2)}) collective-permute-start(bf16[152,128]{1,0:T(8,128)(2,1)S(1)} %get-tuple-element.40), channel_id=1, source_target_pairs={{0,1},{1,0},{2,3},{3,2},{4,5},{5,4},{6,7},{7,6},{8,9},{9,8},{10,11... | collective-permute-start | bytes 116744 | tf_op jit(solution)/shard_map/ppermute | solution.py:500
  29.0 4.0 %collective-permute-start.3 = (bf16[152,128]{1,0:T(8,128)(2,1)S(1)}, bf16[152,128]{1,0:T(8,128)(2,1)S(1)}, u32[]{:S(2)}, u32[]{:S(2)}) collective-permute-start(bf16[152,128]{1,0:T(8,128)(2,1)S(1)} %get-tuple-element.41), channel_id=1, source_target_pairs={{0,2},{1,3},{2,0},{3,1},{4,6},{5,7},{6,4},{7,5},{8,10},{9,11},{10,... | collective-permute-start | bytes 116744 | tf_op jit(solution)/shard_map/ppermute | solution.py:500
  30.8 3.8 %collective-permute-start.4 = (bf16[152,128]{1,0:T(8,128)(2,1)S(1)}, bf16[152,128]{1,0:T(8,128)(2,1)S(1)}, u32[]{:S(2)}, u32[]{:S(2)}) collective-permute-start(bf16[152,128]{1,0:T(8,128)(2,1)S(1)} %get-tuple-element.42), channel_id=1, source_target_pairs={{0,3},{1,2},{2,1},{3,0},{4,7},{5,6},{6,5},{7,4},{8,11},{9,10},{10,... | collective-permute-start | bytes 116744 | tf_op jit(solution)/shard_map/ppermute | solution.py:500
  30.8 37.3 %collective-permute-start.13 = (bf16[64,4096]{1,0:T(8,128)(2,1)S(1)}, bf16[64,4096]{1,0:T(8,128)(2,1)S(1)}, u32[]{:S(2)}, u32[]{:S(2)}) collective-permute-start(bf16[64,4096]{1,0:T(8,128)(2,1)S(1)} %get-tuple-element.57), channel_id=1, source_target_pairs={{0,1},{1,0},{2,3},{3,2},{4,5},{5,4},{6,7},{7,6},{8,9},{9,8},{10,11... | collective-permute-start | bytes 1572872 | tf_op jit(solution)/shard_map/ppermute | solution.py:500
  31.2 16.3 %collective-permute-start.14 = (bf16[64,1536]{1,0:T(8,128)(2,1)S(1)}, bf16[64,1536]{1,0:T(8,128)(2,1)S(1)}, u32[]{:S(2)}, u32[]{:S(2)}) collective-permute-start(bf16[64,1536]{1,0:T(8,128)(2,1)S(1)} %get-tuple-element.59), channel_id=1, source_target_pairs={{0,1},{1,0},{2,3},{3,2},{4,5},{5,4},{6,7},{7,6},{8,9},{9,8},{10,11... | collective-permute-start | bytes 589832 | tf_op jit(solution)/shard_map/ppermute | solution.py:500
  32.2 12.9 %collective-permute-start.16 = (bf16[64,2560]{1,0:T(8,128)(2,1)S(1)}, bf16[64,2560]{1,0:T(8,128)(2,1)S(1)}, u32[]{:S(2)}, u32[]{:S(2)}) collective-permute-start(bf16[64,2560]{1,0:T(8,128)(2,1)S(1)} %get-tuple-element.63), channel_id=1, source_target_pairs={{0,1},{1,0},{2,3},{3,2},{4,5},{5,4},{6,7},{7,6},{8,9},{9,8},{10,11... | collective-permute-start | bytes 983048 | tf_op jit(solution)/shard_map/ppermute | solution.py:500
  40.1 27.9 %copy-start = (bf16[128,4096]{1,0:T(8,128)(2,1)S(1)}, bf16[128,4096]{1,0:T(8,128)(2,1)}, u32[]{:S(2)}) copy-start(bf16[128,4096]{1,0:T(8,128)(2,1)} %res_ref.5) | copy-start | bytes 3145732
  40.2 27.9 %copy-start.1 = (f32[4096]{0:T(1024)S(1)}, f32[4096]{0:T(1024)}, u32[]{:S(2)}) copy-start(f32[4096]{0:T(1024)} %param.21) | copy-start | bytes 49156
  40.2 29.3 %collective-permute-start.9 = (bf16[64,4096]{1,0:T(8,128)(2,1)S(1)}, bf16[64,4096]{1,0:T(8,128)(2,1)S(1)}, u32[]{:S(2)}, u32[]{:S(2)}) collective-permute-start(bf16[64,4096]{1,0:T(8,128)(2,1)S(1)} %get-tuple-element.53), channel_id=1, source_target_pairs={{0,1},{1,0},{2,3},{3,2},{4,5},{5,4},{6,7},{7,6},{8,9},{9,8},{10,11... | collective-permute-start | bytes 1572872 | tf_op jit(solution)/shard_map/ppermute | solution.py:500
  44.6 2.0 %collective-permute-start.10 = (bf16[64,4096]{1,0:T(8,128)(2,1)S(1)}, bf16[64,4096]{1,0:T(8,128)(2,1)S(1)}, u32[]{:S(2)}, u32[]{:S(2)}) collective-permute-start(bf16[64,4096]{1,0:T(8,128)(2,1)S(1)} %get-tuple-element.55), channel_id=1, source_target_pairs={{0,1},{1,0},{2,3},{3,2},{4,5},{5,4},{6,7},{7,6},{8,9},{9,8},{10,11... | collective-permute-start | bytes 1572872 | tf_op jit(solution)/shard_map/ppermute | solution.py:500
  45.1 22.9 %collective-permute-start.17 = (bf16[64,2560]{1,0:T(8,128)(2,1)S(1)}, bf16[64,2560]{1,0:T(8,128)(2,1)S(1)}, u32[]{:S(2)}, u32[]{:S(2)}) collective-permute-start(bf16[64,2560]{1,0:T(8,128)(2,1)S(1)} %add_convert_fusion.1), channel_id=1, source_target_pairs={{0,2},{1,3},{2,0},{3,1},{4,6},{5,7},{6,4},{7,5},{8,10},{9,11},{10,... | collective-permute-start | bytes 983048 | tf_op jit(solution)/shard_map/ppermute | solution.py:500
  46.8 22.7 %collective-permute-start.12 = (bf16[48,4096]{1,0:T(8,128)(2,1)S(1)}, bf16[48,4096]{1,0:T(8,128)(2,1)S(1)}, u32[]{:S(2)}, u32[]{:S(2)}) collective-permute-start(bf16[48,4096]{1,0:T(8,128)(2,1)S(1)} %slice.11), channel_id=1, source_target_pairs={{0,2},{1,3},{2,0},{3,1},{4,6},{5,7},{6,4},{7,5},{8,10},{9,11},{10,... | collective-permute-start | bytes 1179656 | tf_op jit(solution)/shard_map/ppermute | solution.py:500
  47.5 20.1 %collective-permute-start.15 = (bf16[64,1536]{1,0:T(8,128)(2,1)S(1)}, bf16[64,1536]{1,0:T(8,128)(2,1)S(1)}, u32[]{:S(2)}, u32[]{:S(2)}) collective-permute-start(bf16[64,1536]{1,0:T(8,128)(2,1)S(1)} %add_convert_fusion.2), channel_id=1, source_target_pairs={{0,2},{1,3},{2,0},{3,1},{4,6},{5,7},{6,4},{7,5},{8,10},{9,11},{10,... | collective-permute-start | bytes 589832 | tf_op jit(solution)/shard_map/ppermute | solution.py:500
  67.6 5.0 %collective-permute-start.11 = (bf16[16,4096]{1,0:T(8,128)(2,1)S(1)}, bf16[16,4096]{1,0:T(8,128)(2,1)S(1)}, u32[]{:S(2)}, u32[]{:S(2)}) collective-permute-start(bf16[16,4096]{1,0:T(8,128)(2,1)S(1)} %slice.10), channel_id=1, source_target_pairs={{0,2},{1,3},{2,0},{3,1},{4,6},{5,7},{6,4},{7,5},{8,10},{9,11},{10,... | collective-permute-start | bytes 393224 | tf_op jit(solution)/shard_map/ppermute | solution.py:500
